TPU v7x, 32 devices: a whole 2x2x4 slice. The times are simulated.
32 devices in a mesh: dp: 4 (over x, core), expert: 8 (over z, y).
Axes of the slice: x: 2, y: 2, z: 4, core: 2. Of those that a mesh axis runs over, the one named last changes fastest.
Arguments:
- tokens: bfloat16 [4096, 1024], P(('dp', 'expert')), may hold values from -6 to 6
- task_ids: int32 [32], P('dp'), may hold values from 0 to 5
- routing: int32 [32, 2], P('dp'), may hold values from 0 to 7, all different within a row; in each aligned block of 8 rows (0 to 7, 8 to 15, ...) at most 3 rows name the same one
- gate_weight: bfloat16 [1024, 48], replicated, may hold values from -0.1875 to 0.1875
- w_in: bfloat16 [8, 1024, 4096], P('expert', None, 'dp'), may hold values from -0.1875 to 0.1875
- w_out: bfloat16 [8, 4096, 1024], P('expert', 'dp'), may hold values from -0.09375 to 0.09375
Outputs:
- mixed: bfloat16 [4096, 1024], P(('dp', 'expert'))
Inputs may be any that keep to these rules, and one draw needn't show every extreme that they name: `routing`: each row names two different experts. Within the 8 blocks of one index of dp no expert is named more than 3 times, a bound that some block reaches.
All inputs are finite; a program needn't handle non-finite values.
Results may differ from a plain program's by a relative error of at most 0.015.
Values may be sent and summed in bfloat16 or wider, within the bound.
No kernel may reach another device: no remote copies, remote signals or barrier semaphores. Data moves between devices by JAX's collectives and lax.ppermute only.
A program may use at most 64 MiB of HBM per device.

v0:
```python
import functools
import math

import jax
import jax.numpy as jnp
from jax import lax
from jax.experimental import pallas as pl
from jax.experimental.pallas import tpu as pltpu
from jax.sharding import PartitionSpec as P


BLK = 128
STREAMS = 2
MAJOR = 4
CORES = 2
DIRECT = (0,1)
LANES = 128


VMEM = pl.BlockSpec(memory_space=pltpu.VMEM)
ANY = pl.BlockSpec(memory_space=pl.ANY)


def xor_pairs(size, mask):
    return [(i, i ^ mask) for i in range(size)]


def size_of(x):
    return math.prod(x.shape) * jnp.dtype(x.dtype).itemsize


def call(body, out_shapes, *operands, flops, in_specs=None, scratch=(), spare=4 * 2**20):
    moved = sum(size_of(x) for x in list(operands) + jax.tree.leaves(out_shapes))
    return pl.pallas_call(
        body,
        out_shape=out_shapes,
        in_specs=in_specs or [VMEM] * len(operands),
        out_specs=jax.tree.map(lambda _: VMEM, out_shapes),
        scratch_shapes=list(scratch),
        compiler_params=pltpu.CompilerParams(vmem_limit_bytes=moved + spare),
        cost_estimate=pl.CostEstimate(
            flops=int(flops), transcendentals=0, bytes_accessed=moved
        ),
    )(*operands)


def hold_body(n, *refs):
    copies = [pltpu.make_async_copy(refs[i], refs[n + i], refs[-1].at[i]) for i in range(n)]
    for copy in copies:
        copy.start()
    for copy in copies:
        copy.wait()


def add_body(a_ref, b_ref, out_ref):
    out_ref[...] = (a_ref[...].astype(jnp.float32) + b_ref[...].astype(jnp.float32)).astype(
        out_ref.dtype
    )


def combine_body(capacity, start, n, *refs):
    gate_ref, near, far, out_ref = refs[0], refs[1:3], refs[3 : 3 + n], refs[3 + n]
    rows = out_ref.shape[0] // capacity
    whole = near[0].shape[0] // capacity
    for s in range(capacity):
        cut, part = pl.ds(s * whole + start, rows), pl.ds(s * rows, rows)
        value = near[0][cut, :].astype(jnp.float32) + near[1][cut, :].astype(jnp.float32)
        for ref in far:
            value = value + ref[part, :].astype(jnp.float32)
        out_ref[part, :] = (value * gate_ref[cut, :][:, :1]).astype(out_ref.dtype)


def select_body(capacity, n, mask_ref, *refs):
    blocks, full_ref, outs, held, sems = refs[:n], refs[n], refs[n + 1 : -2], refs[-2], refs[-1]
    copies = [pltpu.make_async_copy(blocks[k], held.at[k], sems.at[k]) for k in range(1, n)]
    for copy in copies:
        copy.start()
    for copy in copies:
        copy.wait()
    rows = held.shape[1]
    part = rows // len(outs)
    for s in range(capacity):
        value = None
        for k in range(n):
            flag = mask_ref[pl.ds(s * n + k, 1), :][:, :1]
            term = (held[k] if k else blocks[0][...]) * flag
            value = term if value is None else value + term
        full_ref[pl.ds(s * rows, rows), :] = value
        for i, out_ref in enumerate(outs):
            out_ref[pl.ds(s * part, part), :] = value[i * part : (i + 1) * part]


def ffn_body(n, *refs):
    xs, w_in_ref, w_out_ref, outs = refs[:n], refs[n], refs[n + 1], refs[n + 2 :]
    for x_ref, out_ref in zip(xs, outs):
        hidden = jax.nn.gelu(
            jnp.dot(x_ref[...], w_in_ref[...], preferred_element_type=jnp.float32)
        ).astype(jnp.bfloat16)
        out_ref[...] = jnp.dot(
            hidden, w_out_ref[...], preferred_element_type=jnp.float32
        ).astype(jnp.bfloat16)


def gate_body(capacity, pick_ref, x_ref, gate_weight_ref, out_ref):
    rows = x_ref.shape[0] // capacity
    logits = jnp.dot(x_ref[...], gate_weight_ref[...], preferred_element_type=jnp.float32)
    for s in range(capacity):
        part = logits[s * rows : (s + 1) * rows] * pick_ref[pl.ds(s, 1), :]
        gate = jax.nn.sigmoid(jnp.sum(part, axis=1, keepdims=True))
        out_ref[pl.ds(s * rows, rows), :] = jnp.broadcast_to(gate, (rows, LANES))


def place_body(capacity, major, n, mask_ref, *refs):
    arrived, outs = refs[:n], refs[n:]
    rows = arrived[0].shape[0] // capacity
    step = min(rows, 16)

    @pl.loop(0, rows, step=step)
    def _(start):
        for ka in range(major):
            value = None
            for k in range(n):
                for s in range(capacity):
                    flag = mask_ref[pl.ds((ka * n + k) * capacity + s, 1), :][:, :1]
                    piece = arrived[k][pl.ds(s * rows + start, step), :]
                    term = piece.astype(jnp.float32) * flag
                    value = term if value is None else value + term
            outs[ka][pl.ds(start, step), :] = value.astype(outs[ka].dtype)


def shards(tokens, task_ids, routing, gate_weight, w_in, w_out):
    n_experts = lax.axis_size("expert")
    n_dp = lax.axis_size("dp")
    me = lax.axis_index("expert")
    major = min(MAJOR, n_experts)
    minor = n_experts // major
    chips = n_dp // CORES
    capacity = 2 * (tokens.shape[0] // BLK) + 1
    width = tokens.shape[1]
    rows = BLK // STREAMS
    move = lambda x, mask: lax.ppermute(x, "expert", xor_pairs(n_experts, mask))
    move_dp = lambda x, mask: lax.ppermute(x, "dp", xor_pairs(n_dp, mask))
    shape = lambda r, dtype=jnp.bfloat16: jax.ShapeDtypeStruct((r, width), dtype)

    blocks = jnp.arange(n_experts, dtype=jnp.int32)
    slots = jnp.arange(capacity, dtype=jnp.int32)

    experts = me ^ blocks[:minor]
    chosen = jnp.any(routing[None] == experts[:, None, None], axis=2)
    before = (blocks[None, :] < blocks[:, None])[None]
    rank = jnp.sum(before & chosen[:, None, :], axis=2)
    table = chosen[:, None, :] & (rank[:, None, :] == slots[None, :, None])
    hit = table[0].astype(jnp.int32)
    other = jnp.where(routing[:, 0] == me, routing[:, 1], routing[:, 0])
    slot_task = jnp.sum(hit * task_ids[None, :], axis=1)
    slot_other = jnp.sum(hit * other[None, :], axis=1)
    spread = lambda x: jnp.broadcast_to(x.reshape(-1, 1), (x.size, LANES))

    relative = (blocks[None, None, :] ^ me) == blocks[None, :, None]
    select_mask = spread(jnp.any(table[0][:, None, :] & relative, axis=2).astype(jnp.bfloat16))
    targets = me ^ (blocks[:major] * minor)
    place_mask = spread(
        jnp.any(
            table[None] & (blocks[None, None, None, :] == targets[:, None, None, None]), axis=3
        ).astype(jnp.float32)
    )
    columns = jnp.arange(gate_weight.shape[1], dtype=jnp.int32)
    pick_self = columns[None, :] == (slot_task * n_experts + me)[:, None]
    pick_other = columns[None, :] == (slot_task * n_experts + slot_other)[:, None]
    pick = pick_self.astype(jnp.float32) - pick_other.astype(jnp.float32)

    weight_in, weight_out = w_in[0], w_out[0]

    weight_in, weight_out, own_held = call(
        functools.partial(hold_body, 3),
        [jax.ShapeDtypeStruct(x.shape, x.dtype) for x in (weight_in, weight_out, tokens)],
        weight_in, weight_out, tokens,
        flops=1e8, in_specs=[ANY] * 3,
        scratch=[pltpu.SemaphoreType.DMA((3,))],
    )

    def ffn(xs):
        return call(
            functools.partial(ffn_body, len(xs)),
            [shape(x.shape[0]) for x in xs],
            *xs, weight_in, weight_out,
            spare=16 * 2**20,
            flops=4 * sum(x.size for x in xs) * weight_in.shape[1],
        )

    own = tokens
    gathered = {0: own}
    for mask in range(1, major):
        low = mask & -mask
        gathered[mask * minor] = move(gathered[(mask ^ low) * minor], low * minor)
    for ka in range(major):
        for kb in range(1, minor):
            gathered[ka * minor + kb] = move(gathered[ka * minor], kb)
    picked, *parts = call(
        functools.partial(select_body, capacity, n_experts),
        [shape(capacity * BLK)] + [shape(capacity * rows)] * STREAMS,
        select_mask, own_held, *[gathered[k] for k in range(1, n_experts)],
        spare=8 * 2**20, flops=2e8,
        in_specs=[VMEM] * 2 + [ANY] * (n_experts - 1),
        scratch=[
            pltpu.VMEM((n_experts, BLK, width), jnp.bfloat16),
            pltpu.SemaphoreType.DMA((n_experts,)),
        ],
    )

    foreign = []
    for part in parts:
        foreign.append({c: move_dp(part, c * CORES) for c in range(1, chips)})
    near = move_dp(picked, 1)
    gate = call(
        functools.partial(gate_body, capacity),
        jax.ShapeDtypeStruct((capacity * BLK, LANES), jnp.float32),
        pick, picked, gate_weight,
        flops=1e8,
    )
    mine, theirs = ffn([picked, near])
    theirs = move_dp(theirs, 1)

    outs = []
    for stream in range(STREAMS):
        backs = []
        for chip in range(1, chips):
            far = foreign[stream][chip]
            far_near = move_dp(far, 1)
            (kept,) = ffn([far])
            (sent,) = ffn([far_near])
            sent = move_dp(sent, 1)
            summed = call(add_body, shape(capacity * rows), kept, sent, flops=1e8)
            backs.append(move_dp(summed, chip * CORES))
        gated = call(
            functools.partial(combine_body, capacity, stream * rows, len(backs)),
            shape(capacity * rows),
            gate, mine, theirs, *backs,
            flops=1e8,
        )

        arrived = [gated] + [move(gated, kb) for kb in range(1, minor)]
        values = call(
            functools.partial(place_body, capacity, major, minor),
            [shape(rows)] * major,
            place_mask, *arrived,
            flops=1e8,
        )
        values = [v.astype(jnp.float32) for v in values]
        for mask in reversed(range(1, major)):
            low = mask if stream in DIRECT else mask & -mask
            back = move(values[mask].astype(jnp.bfloat16), low * minor)
            values[mask ^ low] = values[mask ^ low] + back.astype(jnp.float32)
        outs.append(values[0].astype(jnp.bfloat16))
    return outs[0] if STREAMS == 1 else jnp.concatenate(outs, axis=0)


def solution(mesh):
    placed = (
        P(("dp", "expert"), None),
        P("dp"),
        P("dp", None),
        P(),
        P("expert", None, "dp"),
        P("expert", "dp", None),
    )
    return jax.shard_map(
        shards, mesh=mesh, in_specs=placed, out_specs=P(("dp", "expert"), None), check_vma=False
    )
```

profile of v0, /device:TPU:0, one launch (start us, length us, event | category | flops | bytes accessed | tf_op | source)
XLA Modules:
  0.0 118.0 jit_solution(2810111953099194267)
XLA Ops:
  0.0 4.1 %collective-permute-start.3 = (bf16[128,1024]{1,0:T(8,128)(2,1)}, bf16[128,1024]{1,0:T(8,128)(2,1)S(1)}, u32[]{:S(2)}, u32[]{:S(2)}) collective-permute-start(bf16[128,1024]{1,0:T(8,128)(2,1)} %refs_2_.1), channel_id=1, source_target_pairs={{0,4},{1,5},{2,6},{3,7},{4,0},{5,1},{6,2},{7,3},{8,12},{9,13},{10,... | collective-permute-start | bytes 786440 | tf_op jit(solution)/shard_map/ppermute | solution.py:141
  4.1 1.6 %collective-permute-start.1 = (bf16[128,1024]{1,0:T(8,128)(2,1)}, bf16[128,1024]{1,0:T(8,128)(2,1)S(1)}, u32[]{:S(2)}, u32[]{:S(2)}) collective-permute-start(bf16[128,1024]{1,0:T(8,128)(2,1)} %refs_2_.1), channel_id=1, source_target_pairs={{0,2},{1,3},{2,0},{3,1},{4,6},{5,7},{6,4},{7,5},{8,10},{9,11},{10,... | collective-permute-start | bytes 786440 | tf_op jit(solution)/shard_map/ppermute | solution.py:141
  5.6 1.5 %collective-permute-start = (bf16[128,1024]{1,0:T(8,128)(2,1)}, bf16[128,1024]{1,0:T(8,128)(2,1)S(1)}, u32[]{:S(2)}, u32[]{:S(2)}) collective-permute-start(bf16[128,1024]{1,0:T(8,128)(2,1)} %refs_2_.1), channel_id=1, source_target_pairs={{0,1},{1,0},{2,3},{3,2},{4,5},{5,4},{6,7},{7,6},{8,9},{9,8},{10,11... | collective-permute-start | bytes 786440 | tf_op jit(solution)/shard_map/ppermute | solution.py:141
  7.2 0.8 compare_select_fusion
  7.9 0.8 compare_reduce_fusion
  8.7 7.6 %collective-permute-done.3.refs_4_ = bf16[128,1024]{1,0:T(8,128)(2,1)S(1)} collective-permute-done((bf16[128,1024]{1,0:T(8,128)(2,1)}, bf16[128,1024]{1,0:T(8,128)(2,1)S(1)}, u32[]{:S(2)}, u32[]{:S(2)}) %collective-permute-start.3) | collective-permute-done | bytes 262176 | tf_op jit(solution)/shard_map/ppermute | solution.py:141
  16.3 0.7 collective-permute-start.5
  17.0 0.1 convert_reduce_fusion
  17.2 1.6 %collective-permute-start.4 = (bf16[128,1024]{1,0:T(8,128)(2,1)S(1)}, bf16[128,1024]{1,0:T(8,128)(2,1)S(1)}, u32[]{:S(2)}, u32[]{:S(2)}) collective-permute-start(bf16[128,1024]{1,0:T(8,128)(2,1)S(1)} %collective-permute-done.3.refs_4_), channel_id=1, source_target_pairs={{0,1},{1,0},{2,3},{3,2},{4,5},{5,4},{6,7},{7,6},{8,9},{9,8},{10,11... | collective-permute-start | bytes 786440 | tf_op jit(solution)/shard_map/ppermute | solution.py:141
  18.8 0.5 collective-permute-start.2
  19.3 4.4 %collective-permute-done.5.refs_6_ = bf16[128,1024]{1,0:T(8,128)(2,1)S(1)} collective-permute-done((bf16[128,1024]{1,0:T(8,128)(2,1)S(1)}, bf16[128,1024]{1,0:T(8,128)(2,1)S(1)}, u32[]{:S(2)}, u32[]{:S(2)}) %collective-permute-start.5) | collective-permute-done | bytes 262176 | tf_op jit(solution)/shard_map/ppermute | solution.py:141
  23.7 1.3 %collective-permute-start.6 = (bf16[128,1024]{1,0:T(8,128)(2,1)S(1)}, bf16[128,1024]{1,0:T(8,128)(2,1)}, u32[]{:S(2)}, u32[]{:S(2)}) collective-permute-start(bf16[128,1024]{1,0:T(8,128)(2,1)S(1)} %collective-permute-done.5.refs_6_), channel_id=1, source_target_pairs={{0,1},{1,0},{2,3},{3,2},{4,5},{5,4},{6,7},{7,6},{8,9},{9,8},{10,11... | collective-permute-start | bytes 786440 | tf_op jit(solution)/shard_map/ppermute | solution.py:141
  25.0 0.2 and_reduce_fusion
  25.2 0.1 reshape.111
  25.3 1.6 %copy-done.2 = bf16[1,1024,1024]{2,1,0:T(8,128)(2,1)S(1)} copy-done((bf16[1,1024,1024]{2,1,0:T(8,128)(2,1)S(1)}, bf16[1,1024,1024]{2,1,0:T(8,128)(2,1)}, u32[]{:S(2)}) %copy-start.2) | copy-done | bytes 2097176
  26.9 1.6 %copy-done.3 = bf16[1,1024,1024]{2,1,0:T(8,128)(2,1)S(1)} copy-done((bf16[1,1024,1024]{2,1,0:T(8,128)(2,1)S(1)}, bf16[1,1024,1024]{2,1,0:T(8,128)(2,1)}, u32[]{:S(2)}) %copy-start.3) | copy-done | bytes 2097176
  28.5 0.9 copy-done.6
  29.4 0.3 shard_map.64
  29.8 2.4 %collective-permute-done.2.refs_3_ = bf16[128,1024]{1,0:T(8,128)(2,1)} collective-permute-done((bf16[128,1024]{1,0:T(8,128)(2,1)S(1)}, bf16[128,1024]{1,0:T(8,128)(2,1)}, u32[]{:S(2)}, u32[]{:S(2)}) %collective-permute-start.2) | collective-permute-done | bytes 262176 | tf_op jit(solution)/shard_map/ppermute | solution.py:141
  32.1 4.4 %collective-permute-done.6.refs_7_ = bf16[128,1024]{1,0:T(8,128)(2,1)} collective-permute-done((bf16[128,1024]{1,0:T(8,128)(2,1)S(1)}, bf16[128,1024]{1,0:T(8,128)(2,1)}, u32[]{:S(2)}, u32[]{:S(2)}) %collective-permute-start.6) | collective-permute-done | bytes 262176 | tf_op jit(solution)/shard_map/ppermute | solution.py:141
  36.5 0.1 broadcast_in_dim.5.mask_ref
  36.6 1.9 %shard_map.65 = (bf16[384,1024]{1,0:T(8,128)(2,1)S(1)}, bf16[192,1024]{1,0:T(8,128)(2,1)S(1)}, bf16[192,1024]{1,0:T(8,128)(2,1)S(1)}) custom-call(bf16[24,128]{1,0:T(8,128)(2,1)S(1)} %broadcast_in_dim.5.mask_ref, bf16[128,1024]{1,0:T(8,128)(2,1)S(1)} %get-tuple-element.21.refs_0_, bf16[128,1024]{1,0:T(8,128)(2,1)S(1)} %collective-permute-done.refs_1_, ...), custom_call_target="tpu_custom_call" | custom-call | flops 200000000 | bytes 3676160 | tf_op jit(solution)/shard_map/pallas_call | solution.py:34
  38.5 1.6 %collective-permute-start.9 = (bf16[192,1024]{1,0:T(8,128)(2,1)S(1)}, bf16[192,1024]{1,0:T(8,128)(2,1)S(1)}, u32[]{:S(2)}, u32[]{:S(2)}) collective-permute-start(bf16[192,1024]{1,0:T(8,128)(2,1)S(1)} %get-tuple-element.27), channel_id=1, source_target_pairs={{0,16},{8,24},{16,0},{24,8},{1,17},{9,25},{17,1},{25,9},{2,18},{10... | collective-permute-start | bytes 1179656 | tf_op jit(solution)/shard_map/ppermute | solution.py:142
  40.1 0.5 collective-permute-start.17
  40.6 10.0 %collective-permute-done.9.refs_0_ = bf16[192,1024]{1,0:T(8,128)(2,1)S(1)} collective-permute-done((bf16[192,1024]{1,0:T(8,128)(2,1)S(1)}, bf16[192,1024]{1,0:T(8,128)(2,1)S(1)}, u32[]{:S(2)}, u32[]{:S(2)}) %collective-permute-start.9) | collective-permute-done | bytes 393248 | tf_op jit(solution)/shard_map/ppermute | solution.py:142
  50.6 6.3 %collective-permute-done.17.refs_0_ = bf16[192,1024]{1,0:T(8,128)(2,1)S(1)} collective-permute-done((bf16[192,1024]{1,0:T(8,128)(2,1)S(1)}, bf16[192,1024]{1,0:T(8,128)(2,1)S(1)}, u32[]{:S(2)}, u32[]{:S(2)}) %collective-permute-start.17) | collective-permute-done | bytes 393248 | tf_op jit(solution)/shard_map/ppermute | solution.py:142
  56.9 1.2 shard_map.69
  58.1 0.6 collective-permute-start.11
  58.7 4.4 %shard_map.67 = (bf16[384,1024]{1,0:T(8,128)(2,1)S(1)}, bf16[384,1024]{1,0:T(8,128)(2,1)}) custom-call(bf16[384,1024]{1,0:T(8,128)(2,1)S(1)} %get-tuple-element.22.x_ref.refs_0_, bf16[384,1024]{1,0:T(8,128)(2,1)S(1)} %collective-permute-done.7.refs_1_, bf16[1024,1024]{1,0:T(8,128)(2,1)S(1)} %get-tuple-element.23.refs_2_.refs_1_, ...), custom_call_target="tpu_custom_call" | custom-call | flops 3221225472 | bytes 7340032 | tf_op jit(solution)/shard_map/pallas_call | solution.py:34
  63.1 1.9 %shard_map.74 = bf16[192,1024]{1,0:T(8,128)(2,1)} custom-call(bf16[192,1024]{1,0:T(8,128)(2,1)S(1)} %collective-permute-done.18.refs_0_, bf16[1024,1024]{1,0:T(8,128)(2,1)S(1)} %get-tuple-element.23.refs_2_.refs_1_, bf16[1024,1024]{1,0:T(8,128)(2,1)S(1)} %get-tuple-element.24.refs_3_.refs_2_), custom_call_target="tpu_custom_call" | custom-call | flops 805306368 | bytes 4980736 | tf_op jit(solution)/shard_map/pallas_call | solution.py:34
  65.1 0.5 collective-permute-start.19
  65.5 0.1 select_reduce_fusion.1
  65.7 1.2 shard_map.68.a_ref
  66.9 0.8 shard_map.70
  67.7 1.5 %collective-permute-start.12 = (bf16[192,1024]{1,0:T(8,128)(2,1)}, bf16[192,1024]{1,0:T(8,128)(2,1)}, u32[]{:S(2)}, u32[]{:S(2)}) collective-permute-start(bf16[192,1024]{1,0:T(8,128)(2,1)} %shard_map.70), channel_id=1, source_target_pairs={{0,16},{8,24},{16,0},{24,8},{1,17},{9,25},{17,1},{25,9},{2,18},{10... | collective-permute-start | bytes 1179656 | tf_op jit(solution)/shard_map/ppermute | solution.py:142
  69.2 1.1 copy.12.gate_weight_ref
  70.3 1.6 %copy-done.1 = bf16[1024,1024]{1,0:T(8,128)(2,1)S(1)} copy-done((bf16[1024,1024]{1,0:T(8,128)(2,1)S(1)}, bf16[1024,1024]{1,0:T(8,128)(2,1)}, u32[]{:S(2)}) %copy-start.1) | copy-done | bytes 2097176
  71.9 1.2 shard_map.73.a_ref
  73.1 1.1 shard_map.75
  74.2 0.6 collective-permute-start.20
  74.8 0.5 shard_map.66.refs_0_
  75.3 4.7 %collective-permute-done.12.refs_3_ = bf16[192,1024]{1,0:T(8,128)(2,1)} collective-permute-done((bf16[192,1024]{1,0:T(8,128)(2,1)}, bf16[192,1024]{1,0:T(8,128)(2,1)}, u32[]{:S(2)}, u32[]{:S(2)}) %collective-permute-start.12) | collective-permute-done | bytes 393248 | tf_op jit(solution)/shard_map/ppermute | solution.py:142
  80.0 1.4 %shard_map.71.refs_0_ = bf16[192,1024]{1,0:T(8,128)(2,1)S(1)} custom-call(f32[384,128]{1,0:T(8,128)S(1)} %shard_map.66.refs_0_, bf16[384,1024]{1,0:T(8,128)(2,1)S(1)} %get-tuple-element.25.refs_1_, bf16[384,1024]{1,0:T(8,128)(2,1)} %collective-permute-done.8.refs_2_, bf16[192,1024]{1,0:T(8,128)(2,1)} %collective-permute-done.12.refs_3_), custom_call_target="tpu_custom_call" | custom-call | flops 100000000 | bytes 2555904 | tf_op jit(solution)/shard_map/pallas_call | solution.py:34
  81.4 1.6 %collective-permute-start.13 = (bf16[192,1024]{1,0:T(8,128)(2,1)S(1)}, bf16[192,1024]{1,0:T(8,128)(2,1)S(1)}, u32[]{:S(2)}, u32[]{:S(2)}) collective-permute-start(bf16[192,1024]{1,0:T(8,128)(2,1)S(1)} %shard_map.71.refs_0_), channel_id=1, source_target_pairs={{0,1},{1,0},{2,3},{3,2},{4,5},{5,4},{6,7},{7,6},{8,9},{9,8},{10,11... | collective-permute-start | bytes 1179656 | tf_op jit(solution)/shard_map/ppermute | solution.py:141
  83.0 4.4 %collective-permute-done.20.refs_3_ = bf16[192,1024]{1,0:T(8,128)(2,1)S(1)} collective-permute-done((bf16[192,1024]{1,0:T(8,128)(2,1)S(1)}, bf16[192,1024]{1,0:T(8,128)(2,1)S(1)}, u32[]{:S(2)}, u32[]{:S(2)}) %collective-permute-start.20) | collective-permute-done | bytes 393248 | tf_op jit(solution)/shard_map/ppermute | solution.py:142
  87.4 1.3 %shard_map.76.refs_0_ = bf16[192,1024]{1,0:T(8,128)(2,1)S(1)} custom-call(f32[384,128]{1,0:T(8,128)S(1)} %shard_map.66.refs_0_, bf16[384,1024]{1,0:T(8,128)(2,1)S(1)} %get-tuple-element.25.refs_1_, bf16[384,1024]{1,0:T(8,128)(2,1)} %collective-permute-done.8.refs_2_, bf16[192,1024]{1,0:T(8,128)(2,1)S(1)} %collective-permute-done.20.refs_3_), custom_call_target="tpu_custom_call" | custom-call | flops 100000000 | bytes 2555904 | tf_op jit(solution)/shard_map/pallas_call | solution.py:34
  88.7 1.6 %collective-permute-start.21 = (bf16[192,1024]{1,0:T(8,128)(2,1)S(1)}, bf16[192,1024]{1,0:T(8,128)(2,1)S(1)}, u32[]{:S(2)}, u32[]{:S(2)}) collective-permute-start(bf16[192,1024]{1,0:T(8,128)(2,1)S(1)} %shard_map.76.refs_0_), channel_id=1, source_target_pairs={{0,1},{1,0},{2,3},{3,2},{4,5},{5,4},{6,7},{7,6},{8,9},{9,8},{10,11... | collective-permute-start | bytes 1179656 | tf_op jit(solution)/shard_map/ppermute | solution.py:141
  90.3 0.1 iota_compare_fusion.5
  90.4 0.2 and_reduce_fusion.1
  90.6 0.1 copy.11
  90.7 0.1 reshape.110
  90.8 0.2 collective-permute-done.13.refs_1_
  91.0 0.7 shard_map.72
  91.8 3.3 %collective-permute-start.14 = (bf16[64,1024]{1,0:T(8,128)(2,1)S(1)}, bf16[64,1024]{1,0:T(8,128)(2,1)S(1)}, u32[]{:S(2)}, u32[]{:S(2)}) collective-permute-start(bf16[64,1024]{1,0:T(8,128)(2,1)S(1)} %get-tuple-element.29), channel_id=1, source_target_pairs={{0,6},{1,7},{2,4},{3,5},{4,2},{5,3},{6,0},{7,1},{8,14},{9,15},{10,... | collective-permute-start | bytes 393224 | tf_op jit(solution)/shard_map/ppermute | solution.py:141
  95.1 0.1 collective-permute-start.15
  95.2 1.0 collective-permute-start.16
  96.3 2.9 %collective-permute-done.21.refs_1_ = bf16[192,1024]{1,0:T(8,128)(2,1)S(1)} collective-permute-done((bf16[192,1024]{1,0:T(8,128)(2,1)S(1)}, bf16[192,1024]{1,0:T(8,128)(2,1)S(1)}, u32[]{:S(2)}, u32[]{:S(2)}) %collective-permute-start.21) | collective-permute-done | bytes 393248 | tf_op jit(solution)/shard_map/ppermute | solution.py:141
  99.2 0.7 shard_map.77
  99.9 3.3 %collective-permute-start.22 = (bf16[64,1024]{1,0:T(8,128)(2,1)S(1)}, bf16[64,1024]{1,0:T(8,128)(2,1)S(1)}, u32[]{:S(2)}, u32[]{:S(2)}) collective-permute-start(bf16[64,1024]{1,0:T(8,128)(2,1)S(1)} %get-tuple-element.34), channel_id=1, source_target_pairs={{0,6},{1,7},{2,4},{3,5},{4,2},{5,3},{6,0},{7,1},{8,14},{9,15},{10,... | collective-permute-start | bytes 393224 | tf_op jit(solution)/shard_map/ppermute | solution.py:141
  103.3 0.1 collective-permute-start.23
  103.4 1.7 %collective-permute-start.24 = (bf16[64,1024]{1,0:T(8,128)(2,1)S(1)}, bf16[64,1024]{1,0:T(8,128)(2,1)S(1)}, u32[]{:S(2)}, u32[]{:S(2)}) collective-permute-start(bf16[64,1024]{1,0:T(8,128)(2,1)S(1)} %get-tuple-element.36), channel_id=1, source_target_pairs={{0,2},{1,3},{2,0},{3,1},{4,6},{5,7},{6,4},{7,5},{8,10},{9,11},{10,... | collective-permute-start | bytes 393224 | tf_op jit(solution)/shard_map/ppermute | solution.py:141
  105.0 7.1 %collective-permute-done.15 = bf16[64,1024]{1,0:T(8,128)(2,1)S(1)} collective-permute-done((bf16[64,1024]{1,0:T(8,128)(2,1)S(1)}, bf16[64,1024]{1,0:T(8,128)(2,1)S(1)}, u32[]{:S(2)}, u32[]{:S(2)}) %collective-permute-start.15) | collective-permute-done | bytes 131104 | tf_op jit(solution)/shard_map/ppermute | solution.py:141
  112.2 4.9 %collective-permute-done.23 = bf16[64,1024]{1,0:T(8,128)(2,1)S(1)} collective-permute-done((bf16[64,1024]{1,0:T(8,128)(2,1)S(1)}, bf16[64,1024]{1,0:T(8,128)(2,1)S(1)}, u32[]{:S(2)}, u32[]{:S(2)}) %collective-permute-start.23) | collective-permute-done | bytes 131104 | tf_op jit(solution)/shard_map/ppermute | solution.py:141
  117.2 0.7 pad_maximum_fusion
  (44 shorter events, 0.4 us)
Async XLA Ops:
  0.0 16.3 %collective-permute-start.3 = (bf16[128,1024]{1,0:T(8,128)(2,1)}, bf16[128,1024]{1,0:T(8,128)(2,1)S(1)}, u32[]{:S(2)}, u32[]{:S(2)}) collective-permute-start(bf16[128,1024]{1,0:T(8,128)(2,1)} %refs_2_.1), channel_id=1, source_target_pairs={{0,4},{1,5},{2,6},{3,7},{4,0},{5,1},{6,2},{7,3},{8,12},{9,13},{10,... | collective-permute-start | bytes 786440 | tf_op jit(solution)/shard_map/ppermute | solution.py:141
  4.1 14.7 %collective-permute-start.1 = (bf16[128,1024]{1,0:T(8,128)(2,1)}, bf16[128,1024]{1,0:T(8,128)(2,1)S(1)}, u32[]{:S(2)}, u32[]{:S(2)}) collective-permute-start(bf16[128,1024]{1,0:T(8,128)(2,1)} %refs_2_.1), channel_id=1, source_target_pairs={{0,2},{1,3},{2,0},{3,1},{4,6},{5,7},{6,4},{7,5},{8,10},{9,11},{10,... | collective-permute-start | bytes 786440 | tf_op jit(solution)/shard_map/ppermute | solution.py:141
  5.6 24.1 %collective-permute-start = (bf16[128,1024]{1,0:T(8,128)(2,1)}, bf16[128,1024]{1,0:T(8,128)(2,1)S(1)}, u32[]{:S(2)}, u32[]{:S(2)}) collective-permute-start(bf16[128,1024]{1,0:T(8,128)(2,1)} %refs_2_.1), channel_id=1, source_target_pairs={{0,1},{1,0},{2,3},{3,2},{4,5},{5,4},{6,7},{7,6},{8,9},{9,8},{10,11... | collective-permute-start | bytes 786440 | tf_op jit(solution)/shard_map/ppermute | solution.py:141
  16.3 7.4 %collective-permute-start.5 = (bf16[128,1024]{1,0:T(8,128)(2,1)S(1)}, bf16[128,1024]{1,0:T(8,128)(2,1)S(1)}, u32[]{:S(2)}, u32[]{:S(2)}) collective-permute-start(bf16[128,1024]{1,0:T(8,128)(2,1)S(1)} %collective-permute-done.3.refs_4_), channel_id=1, source_target_pairs={{0,2},{1,3},{2,0},{3,1},{4,6},{5,7},{6,4},{7,5},{8,10},{9,11},{10,... | collective-permute-start | bytes 786440 | tf_op jit(solution)/shard_map/ppermute | solution.py:141
  17.2 12.6 %collective-permute-start.4 = (bf16[128,1024]{1,0:T(8,128)(2,1)S(1)}, bf16[128,1024]{1,0:T(8,128)(2,1)S(1)}, u32[]{:S(2)}, u32[]{:S(2)}) collective-permute-start(bf16[128,1024]{1,0:T(8,128)(2,1)S(1)} %collective-permute-done.3.refs_4_), channel_id=1, source_target_pairs={{0,1},{1,0},{2,3},{3,2},{4,5},{5,4},{6,7},{7,6},{8,9},{9,8},{10,11... | collective-permute-start | bytes 786440 | tf_op jit(solution)/shard_map/ppermute | solution.py:141
  18.8 13.4 %collective-permute-start.2 = (bf16[128,1024]{1,0:T(8,128)(2,1)S(1)}, bf16[128,1024]{1,0:T(8,128)(2,1)}, u32[]{:S(2)}, u32[]{:S(2)}) collective-permute-start(bf16[128,1024]{1,0:T(8,128)(2,1)S(1)} %collective-permute-done.1.refs_2_), channel_id=1, source_target_pairs={{0,1},{1,0},{2,3},{3,2},{4,5},{5,4},{6,7},{7,6},{8,9},{9,8},{10,11... | collective-permute-start | bytes 786440 | tf_op jit(solution)/shard_map/ppermute | solution.py:141
  23.7 12.8 %collective-permute-start.6 = (bf16[128,1024]{1,0:T(8,128)(2,1)S(1)}, bf16[128,1024]{1,0:T(8,128)(2,1)}, u32[]{:S(2)}, u32[]{:S(2)}) collective-permute-start(bf16[128,1024]{1,0:T(8,128)(2,1)S(1)} %collective-permute-done.5.refs_6_), channel_id=1, source_target_pairs={{0,1},{1,0},{2,3},{3,2},{4,5},{5,4},{6,7},{7,6},{8,9},{9,8},{10,11... | collective-permute-start | bytes 786440 | tf_op jit(solution)/shard_map/ppermute | solution.py:141
  25.3 1.6 %copy-start.2 = (bf16[1,1024,1024]{2,1,0:T(8,128)(2,1)S(1)}, bf16[1,1024,1024]{2,1,0:T(8,128)(2,1)}, u32[]{:S(2)}) copy-start(bf16[1,1024,1024]{2,1,0:T(8,128)(2,1)} %param.10) | copy-start | bytes 6291460
  26.9 1.6 %copy-start.3 = (bf16[1,1024,1024]{2,1,0:T(8,128)(2,1)S(1)}, bf16[1,1024,1024]{2,1,0:T(8,128)(2,1)}, u32[]{:S(2)}) copy-start(bf16[1,1024,1024]{2,1,0:T(8,128)(2,1)} %param.11) | copy-start | bytes 6291460
  28.5 0.9 copy-start.6
  29.8 35.9 %copy-start = (bf16[1024,1024]{1,0:T(8,128)(2,1)}, bf16[1024,1024]{1,0:T(8,128)(2,1)S(1)}, u32[]{:S(2)}) copy-start(bf16[1024,1024]{1,0:T(8,128)(2,1)S(1)} %get-tuple-element.24.refs_3_.refs_2_) | copy-start | bytes 6291460
  38.5 20.2 %copy-start.4 = (bf16[384,1024]{1,0:T(8,128)(2,1)}, bf16[384,1024]{1,0:T(8,128)(2,1)S(1)}, u32[]{:S(2)}) copy-start(bf16[384,1024]{1,0:T(8,128)(2,1)S(1)} %get-tuple-element.22.x_ref.refs_0_) | copy-start | bytes 2359300
  38.5 12.1 %collective-permute-start.9 = (bf16[192,1024]{1,0:T(8,128)(2,1)S(1)}, bf16[192,1024]{1,0:T(8,128)(2,1)S(1)}, u32[]{:S(2)}, u32[]{:S(2)}) collective-permute-start(bf16[192,1024]{1,0:T(8,128)(2,1)S(1)} %get-tuple-element.27), channel_id=1, source_target_pairs={{0,16},{8,24},{16,0},{24,8},{1,17},{9,25},{17,1},{25,9},{2,18},{10... | collective-permute-start | bytes 1179656 | tf_op jit(solution)/shard_map/ppermute | solution.py:142
  40.1 18.6 %collective-permute-start.7 = (bf16[384,1024]{1,0:T(8,128)(2,1)S(1)}, bf16[384,1024]{1,0:T(8,128)(2,1)S(1)}, u32[]{:S(2)}, u32[]{:S(2)}) collective-permute-start(bf16[384,1024]{1,0:T(8,128)(2,1)S(1)} %get-tuple-element.22.x_ref.refs_0_), channel_id=1, source_target_pairs={{0,8},{8,0},{16,24},{24,16},{1,9},{9,1},{17,25},{25,17},{2,10},{10... | collective-permute-start | bytes 2359304 | tf_op jit(solution)/shard_map/ppermute | solution.py:142
  40.1 16.8 %collective-permute-start.17 = (bf16[192,1024]{1,0:T(8,128)(2,1)S(1)}, bf16[192,1024]{1,0:T(8,128)(2,1)S(1)}, u32[]{:S(2)}, u32[]{:S(2)}) collective-permute-start(bf16[192,1024]{1,0:T(8,128)(2,1)S(1)} %get-tuple-element.32), channel_id=1, source_target_pairs={{0,16},{8,24},{16,0},{24,8},{1,17},{9,25},{17,1},{25,9},{2,18},{10... | collective-permute-start | bytes 1179656 | tf_op jit(solution)/shard_map/ppermute | solution.py:142
  50.6 6.3 %collective-permute-start.10 = (bf16[192,1024]{1,0:T(8,128)(2,1)S(1)}, bf16[192,1024]{1,0:T(8,128)(2,1)S(1)}, u32[]{:S(2)}, u32[]{:S(2)}) collective-permute-start(bf16[192,1024]{1,0:T(8,128)(2,1)S(1)} %collective-permute-done.9.refs_0_), channel_id=1, source_target_pairs={{0,8},{8,0},{16,24},{24,16},{1,9},{9,1},{17,25},{25,17},{2,10},{10... | collective-permute-start | bytes 1179656 | tf_op jit(solution)/shard_map/ppermute | solution.py:142
  56.9 6.2 %collective-permute-start.18 = (bf16[192,1024]{1,0:T(8,128)(2,1)S(1)}, bf16[192,1024]{1,0:T(8,128)(2,1)S(1)}, u32[]{:S(2)}, u32[]{:S(2)}) collective-permute-start(bf16[192,1024]{1,0:T(8,128)(2,1)S(1)} %collective-permute-done.17.refs_0_), channel_id=1, source_target_pairs={{0,8},{8,0},{16,24},{24,16},{1,9},{9,1},{17,25},{25,17},{2,10},{10... | collective-permute-start | bytes 1179656 | tf_op jit(solution)/shard_map/ppermute | solution.py:142
  58.1 8.8 %collective-permute-start.11 = (bf16[192,1024]{1,0:T(8,128)(2,1)S(1)}, bf16[192,1024]{1,0:T(8,128)(2,1)S(1)}, u32[]{:S(2)}, u32[]{:S(2)}) collective-permute-start(bf16[192,1024]{1,0:T(8,128)(2,1)S(1)} %shard_map.69), channel_id=1, source_target_pairs={{0,8},{8,0},{16,24},{24,16},{1,9},{9,1},{17,25},{25,17},{2,10},{10... | collective-permute-start | bytes 1179656 | tf_op jit(solution)/shard_map/ppermute | solution.py:142
  63.1 2.5 %copy-start.7 = (s32[8]{0:T(128)S(1)}, s32[8]{0:T(128)}, u32[]{:S(2)}) copy-start(s32[8]{0:T(128)} %param.7) | copy-start | bytes 100
  63.1 16.9 %collective-permute-start.8 = (bf16[384,1024]{1,0:T(8,128)(2,1)}, bf16[384,1024]{1,0:T(8,128)(2,1)}, u32[]{:S(2)}, u32[]{:S(2)}) collective-permute-start(bf16[384,1024]{1,0:T(8,128)(2,1)} %get-tuple-element.26), channel_id=1, source_target_pairs={{0,8},{8,0},{16,24},{24,16},{1,9},{9,1},{17,25},{25,17},{2,10},{10... | collective-permute-start | bytes 2359304 | tf_op jit(solution)/shard_map/ppermute | solution.py:142
  65.1 8.0 %collective-permute-start.19 = (bf16[192,1024]{1,0:T(8,128)(2,1)}, bf16[192,1024]{1,0:T(8,128)(2,1)}, u32[]{:S(2)}, u32[]{:S(2)}) collective-permute-start(bf16[192,1024]{1,0:T(8,128)(2,1)} %shard_map.74), channel_id=1, source_target_pairs={{0,8},{8,0},{16,24},{24,16},{1,9},{9,1},{17,25},{25,17},{2,10},{10... | collective-permute-start | bytes 1179656 | tf_op jit(solution)/shard_map/ppermute | solution.py:142
  67.7 12.3 %collective-permute-start.12 = (bf16[192,1024]{1,0:T(8,128)(2,1)}, bf16[192,1024]{1,0:T(8,128)(2,1)}, u32[]{:S(2)}, u32[]{:S(2)}) collective-permute-start(bf16[192,1024]{1,0:T(8,128)(2,1)} %shard_map.70), channel_id=1, source_target_pairs={{0,16},{8,24},{16,0},{24,8},{1,17},{9,25},{17,1},{25,9},{2,18},{10... | collective-permute-start | bytes 1179656 | tf_op jit(solution)/shard_map/ppermute | solution.py:142
  70.3 1.6 %copy-start.1 = (bf16[1024,1024]{1,0:T(8,128)(2,1)S(1)}, bf16[1024,1024]{1,0:T(8,128)(2,1)}, u32[]{:S(2)}) copy-start(bf16[1024,1024]{1,0:T(8,128)(2,1)} %copy-done) | copy-start | bytes 6291460
  71.9 3.0 %copy-start.5 = (bf16[384,1024]{1,0:T(8,128)(2,1)S(1)}, bf16[384,1024]{1,0:T(8,128)(2,1)}, u32[]{:S(2)}) copy-start(bf16[384,1024]{1,0:T(8,128)(2,1)} %copy-done.4) | copy-start | bytes 2359300
  74.2 13.3 %collective-permute-start.20 = (bf16[192,1024]{1,0:T(8,128)(2,1)S(1)}, bf16[192,1024]{1,0:T(8,128)(2,1)S(1)}, u32[]{:S(2)}, u32[]{:S(2)}) collective-permute-start(bf16[192,1024]{1,0:T(8,128)(2,1)S(1)} %shard_map.75), channel_id=1, source_target_pairs={{0,16},{8,24},{16,0},{24,8},{1,17},{9,25},{17,1},{25,9},{2,18},{10... | collective-permute-start | bytes 1179656 | tf_op jit(solution)/shard_map/ppermute | solution.py:142
  81.4 9.5 %collective-permute-start.13 = (bf16[192,1024]{1,0:T(8,128)(2,1)S(1)}, bf16[192,1024]{1,0:T(8,128)(2,1)S(1)}, u32[]{:S(2)}, u32[]{:S(2)}) collective-permute-start(bf16[192,1024]{1,0:T(8,128)(2,1)S(1)} %shard_map.71.refs_0_), channel_id=1, source_target_pairs={{0,1},{1,0},{2,3},{3,2},{4,5},{5,4},{6,7},{7,6},{8,9},{9,8},{10,11... | collective-permute-start | bytes 1179656 | tf_op jit(solution)/shard_map/ppermute | solution.py:141
  88.7 10.5 %collective-permute-start.21 = (bf16[192,1024]{1,0:T(8,128)(2,1)S(1)}, bf16[192,1024]{1,0:T(8,128)(2,1)S(1)}, u32[]{:S(2)}, u32[]{:S(2)}) collective-permute-start(bf16[192,1024]{1,0:T(8,128)(2,1)S(1)} %shard_map.76.refs_0_), channel_id=1, source_target_pairs={{0,1},{1,0},{2,3},{3,2},{4,5},{5,4},{6,7},{7,6},{8,9},{9,8},{10,11... | collective-permute-start | bytes 1179656 | tf_op jit(solution)/shard_map/ppermute | solution.py:141
  91.8 11.6 %collective-permute-start.14 = (bf16[64,1024]{1,0:T(8,128)(2,1)S(1)}, bf16[64,1024]{1,0:T(8,128)(2,1)S(1)}, u32[]{:S(2)}, u32[]{:S(2)}) collective-permute-start(bf16[64,1024]{1,0:T(8,128)(2,1)S(1)} %get-tuple-element.29), channel_id=1, source_target_pairs={{0,6},{1,7},{2,4},{3,5},{4,2},{5,3},{6,0},{7,1},{8,14},{9,15},{10,... | collective-permute-start | bytes 393224 | tf_op jit(solution)/shard_map/ppermute | solution.py:141
  95.1 17.0 %collective-permute-start.15 = (bf16[64,1024]{1,0:T(8,128)(2,1)S(1)}, bf16[64,1024]{1,0:T(8,128)(2,1)S(1)}, u32[]{:S(2)}, u32[]{:S(2)}) collective-permute-start(bf16[64,1024]{1,0:T(8,128)(2,1)S(1)} %get-tuple-element.30), channel_id=1, source_target_pairs={{0,4},{1,5},{2,6},{3,7},{4,0},{5,1},{6,2},{7,3},{8,12},{9,13},{10,... | collective-permute-start | bytes 393224 | tf_op jit(solution)/shard_map/ppermute | solution.py:141
  95.2 16.9 %collective-permute-start.16 = (bf16[64,1024]{1,0:T(8,128)(2,1)S(1)}, bf16[64,1024]{1,0:T(8,128)(2,1)S(1)}, u32[]{:S(2)}, u32[]{:S(2)}) collective-permute-start(bf16[64,1024]{1,0:T(8,128)(2,1)S(1)} %get-tuple-element.31), channel_id=1, source_target_pairs={{0,2},{1,3},{2,0},{3,1},{4,6},{5,7},{6,4},{7,5},{8,10},{9,11},{10,... | collective-permute-start | bytes 393224 | tf_op jit(solution)/shard_map/ppermute | solution.py:141
  99.9 12.3 %collective-permute-start.22 = (bf16[64,1024]{1,0:T(8,128)(2,1)S(1)}, bf16[64,1024]{1,0:T(8,128)(2,1)S(1)}, u32[]{:S(2)}, u32[]{:S(2)}) collective-permute-start(bf16[64,1024]{1,0:T(8,128)(2,1)S(1)} %get-tuple-element.34), channel_id=1, source_target_pairs={{0,6},{1,7},{2,4},{3,5},{4,2},{5,3},{6,0},{7,1},{8,14},{9,15},{10,... | collective-permute-start | bytes 393224 | tf_op jit(solution)/shard_map/ppermute | solution.py:141
  103.3 13.9 %collective-permute-start.23 = (bf16[64,1024]{1,0:T(8,128)(2,1)S(1)}, bf16[64,1024]{1,0:T(8,128)(2,1)S(1)}, u32[]{:S(2)}, u32[]{:S(2)}) collective-permute-start(bf16[64,1024]{1,0:T(8,128)(2,1)S(1)} %get-tuple-element.35), channel_id=1, source_target_pairs={{0,4},{1,5},{2,6},{3,7},{4,0},{5,1},{6,2},{7,3},{8,12},{9,13},{10,... | collective-permute-start | bytes 393224 | tf_op jit(solution)/shard_map/ppermute | solution.py:141
  103.4 13.8 %collective-permute-start.24 = (bf16[64,1024]{1,0:T(8,128)(2,1)S(1)}, bf16[64,1024]{1,0:T(8,128)(2,1)S(1)}, u32[]{:S(2)}, u32[]{:S(2)}) collective-permute-start(bf16[64,1024]{1,0:T(8,128)(2,1)S(1)} %get-tuple-element.36), channel_id=1, source_target_pairs={{0,2},{1,3},{2,0},{3,1},{4,6},{5,7},{6,4},{7,5},{8,10},{9,11},{10,... | collective-permute-start | bytes 393224 | tf_op jit(solution)/shard_map/ppermute | solution.py:141
where the time goes:
time: 118 us
  waiting for transfers between devices  59.4 us (50%)
  starting transfers between devices  29.3 us (25%)
  Pallas kernels  18.7 us (16%)
  local copies, waits for them, and re-layouts  7.22 us (6%)
  other arithmetic  3.22 us (3%)
    ppermute x15, waiting for transfers between devices, shards(): move = lambda x, mask: lax.ppermute(x, 'expert', xor_pairs(n_experts, mask))  34 us
    ppermute x10, waiting for transfers between devices, shards(): move_dp = lambda x, mask: lax.ppermute(x, 'dp', xor_pairs(n_dp, mask))  25.4 us
    ppermute x15, starting transfers between devices, shards(): move = lambda x, mask: lax.ppermute(x, 'expert', xor_pairs(n_experts, mask))  24 us
    pallas_call x14, Pallas kernels, call(): pl.pallas_call(body, out_shape=out_shapes, in_specs=in_specs or [VMEM] *...  18.7 us
    unnamed x17, local copies, waits for them, and re-layouts  6.8 us
    ppermute x10, starting transfers between devices, shards(): move_dp = lambda x, mask: lax.ppermute(x, 'dp', xor_pairs(n_dp, mask))  5.27 us
  transfers between devices with their start and end apart: 25, of which 12 were waited for; matrix products, arithmetic and copies ran while one was open for 3% of the time, Pallas kernels for 14%

commit v1 on v0

--- a/solution.py
+++ b/solution.py
@@ -10,10 +10,11 @@
 
 
 BLK = 128
-STREAMS = 2
+SPLIT = (4, 4)
 MAJOR = 4
 CORES = 2
-DIRECT = (0,1)
+SPLIT_SPARE = 4
+SELECT_SPARE = 8
 LANES = 128
 
 
@@ -44,50 +45,46 @@
     )(*operands)
 
 
-def hold_body(n, *refs):
-    copies = [pltpu.make_async_copy(refs[i], refs[n + i], refs[-1].at[i]) for i in range(n)]
+def add_body(a_ref, b_ref, out_ref):
+    out_ref[...] = (a_ref[...].astype(jnp.float32) + b_ref[...].astype(jnp.float32)).astype(
+        out_ref.dtype
+    )
+
+
+def combine_body(*refs):
+    gate_ref, parts, out_ref = refs[0], refs[1:-1], refs[-1]
+    value = parts[0][...].astype(jnp.float32)
+    for ref in parts[1:]:
+        value = value + ref[...].astype(jnp.float32)
+    out_ref[...] = (value * gate_ref[...][:, :1]).astype(out_ref.dtype)
+
+
+def split_body(n, *refs):
+    start, copies = 0, []
+    for i in range(n):
+        source = refs[0].at[pl.ds(start, refs[1 + i].shape[0]), :]
+        copies.append(pltpu.make_async_copy(source, refs[1 + i], refs[-1].at[i]))
+        start += refs[1 + i].shape[0]
     for copy in copies:
         copy.start()
     for copy in copies:
         copy.wait()
 
 
-def add_body(a_ref, b_ref, out_ref):
-    out_ref[...] = (a_ref[...].astype(jnp.float32) + b_ref[...].astype(jnp.float32)).astype(
-        out_ref.dtype
-    )
-
-
-def combine_body(capacity, start, n, *refs):
-    gate_ref, near, far, out_ref = refs[0], refs[1:3], refs[3 : 3 + n], refs[3 + n]
-    rows = out_ref.shape[0] // capacity
-    whole = near[0].shape[0] // capacity
-    for s in range(capacity):
-        cut, part = pl.ds(s * whole + start, rows), pl.ds(s * rows, rows)
-        value = near[0][cut, :].astype(jnp.float32) + near[1][cut, :].astype(jnp.float32)
-        for ref in far:
-            value = value + ref[part, :].astype(jnp.float32)
-        out_ref[part, :] = (value * gate_ref[cut, :][:, :1]).astype(out_ref.dtype)
-
-
 def select_body(capacity, n, mask_ref, *refs):
-    blocks, full_ref, outs, held, sems = refs[:n], refs[n], refs[n + 1 : -2], refs[-2], refs[-1]
+    blocks, out_ref, held, sems = refs[:n], refs[n], refs[n + 1], refs[n + 2]
     copies = [pltpu.make_async_copy(blocks[k], held.at[k], sems.at[k]) for k in range(1, n)]
     for copy in copies:
         copy.start()
-    for copy in copies:
-        copy.wait()
     rows = held.shape[1]
-    part = rows // len(outs)
-    for s in range(capacity):
-        value = None
-        for k in range(n):
+    for k in range(n):
+        if k:
+            copies[k - 1].wait()
+        for s in range(capacity):
             flag = mask_ref[pl.ds(s * n + k, 1), :][:, :1]
             term = (held[k] if k else blocks[0][...]) * flag
-            value = term if value is None else value + term
-        full_ref[pl.ds(s * rows, rows), :] = value
-        for i, out_ref in enumerate(outs):
-            out_ref[pl.ds(s * part, part), :] = value[i * part : (i + 1) * part]
+            part = pl.ds(s * rows, rows)
+            out_ref[part, :] = out_ref[part, :] + term if k else term
 
 
 def ffn_body(n, *refs):
@@ -103,7 +100,10 @@
 
 def gate_body(capacity, pick_ref, x_ref, gate_weight_ref, out_ref):
     rows = x_ref.shape[0] // capacity
-    logits = jnp.dot(x_ref[...], gate_weight_ref[...], preferred_element_type=jnp.float32)
+    logits = lax.dot_general(
+        x_ref[...], gate_weight_ref[...], (((1,), (1,)), ((), ())),
+        preferred_element_type=jnp.float32,
+    )
     for s in range(capacity):
         part = logits[s * rows : (s + 1) * rows] * pick_ref[pl.ds(s, 1), :]
         gate = jax.nn.sigmoid(jnp.sum(part, axis=1, keepdims=True))
@@ -137,7 +137,7 @@
     chips = n_dp // CORES
     capacity = 2 * (tokens.shape[0] // BLK) + 1
     width = tokens.shape[1]
-    rows = BLK // STREAMS
+    split = [BLK * part // sum(SPLIT) for part in SPLIT]
     move = lambda x, mask: lax.ppermute(x, "expert", xor_pairs(n_experts, mask))
     move_dp = lambda x, mask: lax.ppermute(x, "dp", xor_pairs(n_dp, mask))
     shape = lambda r, dtype=jnp.bfloat16: jax.ShapeDtypeStruct((r, width), dtype)
@@ -171,14 +171,6 @@
 
     weight_in, weight_out = w_in[0], w_out[0]
 
-    weight_in, weight_out, own_held = call(
-        functools.partial(hold_body, 3),
-        [jax.ShapeDtypeStruct(x.shape, x.dtype) for x in (weight_in, weight_out, tokens)],
-        weight_in, weight_out, tokens,
-        flops=1e8, in_specs=[ANY] * 3,
-        scratch=[pltpu.SemaphoreType.DMA((3,))],
-    )
-
     def ffn(xs):
         return call(
             functools.partial(ffn_body, len(xs)),
@@ -188,56 +180,56 @@
             flops=4 * sum(x.size for x in xs) * weight_in.shape[1],
         )
 
-    own = tokens
-    gathered = {0: own}
-    for mask in range(1, major):
-        low = mask & -mask
-        gathered[mask * minor] = move(gathered[(mask ^ low) * minor], low * minor)
-    for ka in range(major):
-        for kb in range(1, minor):
-            gathered[ka * minor + kb] = move(gathered[ka * minor], kb)
-    picked, *parts = call(
-        functools.partial(select_body, capacity, n_experts),
-        [shape(capacity * BLK)] + [shape(capacity * rows)] * STREAMS,
-        select_mask, own_held, *[gathered[k] for k in range(1, n_experts)],
-        spare=8 * 2**20, flops=2e8,
-        in_specs=[VMEM] * 2 + [ANY] * (n_experts - 1),
-        scratch=[
-            pltpu.VMEM((n_experts, BLK, width), jnp.bfloat16),
-            pltpu.SemaphoreType.DMA((n_experts,)),
-        ],
-    )
-
-    foreign = []
-    for part in parts:
-        foreign.append({c: move_dp(part, c * CORES) for c in range(1, chips)})
-    near = move_dp(picked, 1)
-    gate = call(
-        functools.partial(gate_body, capacity),
-        jax.ShapeDtypeStruct((capacity * BLK, LANES), jnp.float32),
-        pick, picked, gate_weight,
-        flops=1e8,
-    )
-    mine, theirs = ffn([picked, near])
-    theirs = move_dp(theirs, 1)
-
+    owns = call(
+        functools.partial(split_body, len(split)),
+        [shape(rows) for rows in split],
+        tokens,
+        flops=1e8, in_specs=[ANY], spare=SPLIT_SPARE * 2**20,
+        scratch=[pltpu.SemaphoreType.DMA((len(split),))],
+    )
     outs = []
-    for stream in range(STREAMS):
+    for own, rows in zip(owns, split):
+        full = shape(capacity * rows)
+
+        gathered = {0: own}
+        for mask in range(1, major):
+            low = mask & -mask
+            gathered[mask * minor] = move(gathered[(mask ^ low) * minor], low * minor)
+        for ka in range(major):
+            for kb in range(1, minor):
+                gathered[ka * minor + kb] = move(gathered[ka * minor], kb)
+        picked = call(
+            functools.partial(select_body, capacity, n_experts),
+            full,
+            select_mask, *[gathered[k] for k in range(n_experts)],
+            flops=2e8, spare=SELECT_SPARE * 2**20,
+            in_specs=[VMEM] * 2 + [ANY] * (n_experts - 1),
+            scratch=[
+                pltpu.VMEM((n_experts, rows, width), jnp.bfloat16),
+                pltpu.SemaphoreType.DMA((n_experts,)),
+            ],
+        )
+
+        foreign = {chip: move_dp(picked, chip * CORES) for chip in range(1, chips)}
+        near = move_dp(picked, 1)
+        gate = call(
+            functools.partial(gate_body, capacity),
+            jax.ShapeDtypeStruct((capacity * rows, LANES), jnp.float32),
+            pick, picked, gate_weight.T,
+            flops=1e8,
+        )
+        mine, theirs = ffn([picked, near])
+        theirs = move_dp(theirs, 1)
         backs = []
         for chip in range(1, chips):
-            far = foreign[stream][chip]
+            far = foreign[chip]
             far_near = move_dp(far, 1)
             (kept,) = ffn([far])
             (sent,) = ffn([far_near])
             sent = move_dp(sent, 1)
-            summed = call(add_body, shape(capacity * rows), kept, sent, flops=1e8)
+            summed = call(add_body, full, kept, sent, flops=1e8)
             backs.append(move_dp(summed, chip * CORES))
-        gated = call(
-            functools.partial(combine_body, capacity, stream * rows, len(backs)),
-            shape(capacity * rows),
-            gate, mine, theirs, *backs,
-            flops=1e8,
-        )
+        gated = call(combine_body, full, gate, mine, theirs, *backs, flops=1e8)
 
         arrived = [gated] + [move(gated, kb) for kb in range(1, minor)]
         values = call(
@@ -246,13 +238,11 @@
             place_mask, *arrived,
             flops=1e8,
         )
-        values = [v.astype(jnp.float32) for v in values]
+        result = values[0].astype(jnp.float32)
         for mask in reversed(range(1, major)):
-            low = mask if stream in DIRECT else mask & -mask
-            back = move(values[mask].astype(jnp.bfloat16), low * minor)
-            values[mask ^ low] = values[mask ^ low] + back.astype(jnp.float32)
-        outs.append(values[0].astype(jnp.bfloat16))
-    return outs[0] if STREAMS == 1 else jnp.concatenate(outs, axis=0)
+            result = result + move(values[mask], mask * minor).astype(jnp.float32)
+        outs.append(result.astype(jnp.bfloat16))
+    return jnp.concatenate(outs, axis=0)
 
 
 def solution(mesh):

time: 118 us -> 111 us (0.941)
  starting transfers between devices: 29.3 us -> 42.3 us
  waiting for transfers between devices: 59.4 us -> 46.6 us
  local copies, waits for them, and re-layouts: 7.22 us -> 3.13 us
  Pallas kernels: 18.7 us -> 15.2 us
    ppermute x15 -> x22, starting transfers between devices: 24 us -> 35.7 us  [shards(): move = lambda x, mask: lax.ppermute(x, 'expert', xor_pairs(n_experts, mask))]
    ppermute x15 -> x22, waiting for transfers between devices: 34 us -> 26.9 us  [shards(): move = lambda x, mask: lax.ppermute(x, 'expert', xor_pairs(n_experts, mask))]
    ppermute x10 -> x12, waiting for transfers between devices: 25.4 us -> 19.6 us  [shards(): move_dp = lambda x, mask: lax.ppermute(x, 'dp', xor_pairs(n_dp, mask))]
    unnamed x17 -> x12, local copies, waits for them, and re-layouts: 6.8 us -> 2.71 us
    pallas_call x14 -> x17, Pallas kernels: 18.7 us -> 15.2 us  [call(): pl.pallas_call(body, out_shape=out_shapes, in_specs=in_specs or [VMEM] *...]
    ppermute x10 -> x12, starting transfers between devices: 5.27 us -> 6.52 us  [shards(): move_dp = lambda x, mask: lax.ppermute(x, 'dp', xor_pairs(n_dp, mask))]
  transfers between devices with their start and end apart: 25 -> 34, of which waited for: 12 -> 13; matrix products, arithmetic and copies ran while one was open for 3% -> 3% of each run, Pallas kernels for 14% -> 13%
where the time goes in v1:
time: 111 us
  waiting for transfers between devices  46.6 us (42%)
  starting transfers between devices  42.3 us (38%)
  Pallas kernels  15.2 us (14%)
  other arithmetic  3.23 us (3%)
  local copies, waits for them, and re-layouts  3.13 us (3%)
    ppermute x22, starting transfers between devices, shards(): move = lambda x, mask: lax.ppermute(x, 'expert', xor_pairs(n_experts, mask))  35.7 us
    ppermute x22, waiting for transfers between devices, shards(): move = lambda x, mask: lax.ppermute(x, 'expert', xor_pairs(n_experts, mask))  26.9 us
    ppermute x12, waiting for transfers between devices, shards(): move_dp = lambda x, mask: lax.ppermute(x, 'dp', xor_pairs(n_dp, mask))  19.6 us
    pallas_call x17, Pallas kernels, call(): pl.pallas_call(body, out_shape=out_shapes, in_specs=in_specs or [VMEM] *...  15.2 us
    ppermute x12, starting transfers between devices, shards(): move_dp = lambda x, mask: lax.ppermute(x, 'dp', xor_pairs(n_dp, mask))  6.52 us
    unnamed x12, local copies, waits for them, and re-layouts  2.71 us
  transfers between devices with their start and end apart: 34, of which 13 were waited for; matrix products, arithmetic and copies ran while one was open for 3% of the time, Pallas kernels for 13%

profile of v1, /device:TPU:0, one launch (start us, length us, event | category | flops | bytes accessed | tf_op | source)
XLA Modules:
  0.0 110.6 jit_solution(5558808645876545013)
XLA Ops:
  0.0 1.1 copy-done.4
  1.1 0.3 shard_map.64
  1.4 4.1 %collective-permute-start.3 = (bf16[64,1024]{1,0:T(8,128)(2,1)S(1)}, bf16[64,1024]{1,0:T(8,128)(2,1)S(1)}, u32[]{:S(2)}, u32[]{:S(2)}) collective-permute-start(bf16[64,1024]{1,0:T(8,128)(2,1)S(1)} %get-tuple-element.19.refs_0_), channel_id=1, source_target_pairs={{0,4},{1,5},{2,6},{3,7},{4,0},{5,1},{6,2},{7,3},{8,12},{9,13},{10,... | collective-permute-start | bytes 393224 | tf_op jit(solution)/shard_map/ppermute | solution.py:141
  5.6 1.6 %collective-permute-start.1 = (bf16[64,1024]{1,0:T(8,128)(2,1)S(1)}, bf16[64,1024]{1,0:T(8,128)(2,1)S(1)}, u32[]{:S(2)}, u32[]{:S(2)}) collective-permute-start(bf16[64,1024]{1,0:T(8,128)(2,1)S(1)} %get-tuple-element.19.refs_0_), channel_id=1, source_target_pairs={{0,2},{1,3},{2,0},{3,1},{4,6},{5,7},{6,4},{7,5},{8,10},{9,11},{10,... | collective-permute-start | bytes 393224 | tf_op jit(solution)/shard_map/ppermute | solution.py:141
  7.2 1.5 %collective-permute-start = (bf16[64,1024]{1,0:T(8,128)(2,1)S(1)}, bf16[64,1024]{1,0:T(8,128)(2,1)S(1)}, u32[]{:S(2)}, u32[]{:S(2)}) collective-permute-start(bf16[64,1024]{1,0:T(8,128)(2,1)S(1)} %get-tuple-element.19.refs_0_), channel_id=1, source_target_pairs={{0,1},{1,0},{2,3},{3,2},{4,5},{5,4},{6,7},{7,6},{8,9},{9,8},{10,11... | collective-permute-start | bytes 393224 | tf_op jit(solution)/shard_map/ppermute | solution.py:141
  8.7 0.3 collective-permute-start.20
  9.0 0.8 compare_reduce_fusion
  9.8 0.1 convert_reduce_fusion
  10.0 0.8 compare_select_fusion
  10.7 2.5 %collective-permute-done.3.refs_4_ = bf16[64,1024]{1,0:T(8,128)(2,1)S(1)} collective-permute-done((bf16[64,1024]{1,0:T(8,128)(2,1)S(1)}, bf16[64,1024]{1,0:T(8,128)(2,1)S(1)}, u32[]{:S(2)}, u32[]{:S(2)}) %collective-permute-start.3) | collective-permute-done | bytes 131104 | tf_op jit(solution)/shard_map/ppermute | solution.py:141
  13.2 0.4 collective-permute-start.5
  13.6 2.1 %collective-permute-start.4 = (bf16[64,1024]{1,0:T(8,128)(2,1)S(1)}, bf16[64,1024]{1,0:T(8,128)(2,1)S(1)}, u32[]{:S(2)}, u32[]{:S(2)}) collective-permute-start(bf16[64,1024]{1,0:T(8,128)(2,1)S(1)} %collective-permute-done.3.refs_4_), channel_id=1, source_target_pairs={{0,1},{1,0},{2,3},{3,2},{4,5},{5,4},{6,7},{7,6},{8,9},{9,8},{10,11... | collective-permute-start | bytes 393224 | tf_op jit(solution)/shard_map/ppermute | solution.py:141
  15.8 3.1 %collective-permute-done.5.refs_6_ = bf16[64,1024]{1,0:T(8,128)(2,1)S(1)} collective-permute-done((bf16[64,1024]{1,0:T(8,128)(2,1)S(1)}, bf16[64,1024]{1,0:T(8,128)(2,1)S(1)}, u32[]{:S(2)}, u32[]{:S(2)}) %collective-permute-start.5) | collective-permute-done | bytes 131104 | tf_op jit(solution)/shard_map/ppermute | solution.py:141
  18.9 1.7 %collective-permute-start.6 = (bf16[64,1024]{1,0:T(8,128)(2,1)S(1)}, bf16[64,1024]{1,0:T(8,128)(2,1)S(1)}, u32[]{:S(2)}, u32[]{:S(2)}) collective-permute-start(bf16[64,1024]{1,0:T(8,128)(2,1)S(1)} %collective-permute-done.5.refs_6_), channel_id=1, source_target_pairs={{0,1},{1,0},{2,3},{3,2},{4,5},{5,4},{6,7},{7,6},{8,9},{9,8},{10,11... | collective-permute-start | bytes 393224 | tf_op jit(solution)/shard_map/ppermute | solution.py:141
  20.6 0.2 and_reduce_fusion
  20.9 0.2 collective-permute-start.18
  21.1 1.8 %collective-permute-start.22 = (bf16[64,1024]{1,0:T(8,128)(2,1)S(1)}, bf16[64,1024]{1,0:T(8,128)(2,1)S(1)}, u32[]{:S(2)}, u32[]{:S(2)}) collective-permute-start(bf16[64,1024]{1,0:T(8,128)(2,1)S(1)} %collective-permute-done.20.refs_4_), channel_id=1, source_target_pairs={{0,2},{1,3},{2,0},{3,1},{4,6},{5,7},{6,4},{7,5},{8,10},{9,11},{10,... | collective-permute-start | bytes 393224 | tf_op jit(solution)/shard_map/ppermute | solution.py:141
  22.9 1.0 collective-permute-done.6.refs_7_
  24.0 1.8 %shard_map.65.x_ref.refs_0_ = bf16[192,1024]{1,0:T(8,128)(2,1)S(1)} custom-call(bf16[24,128]{1,0:T(8,128)(2,1)S(1)} %broadcast_in_dim.5.mask_ref, bf16[64,1024]{1,0:T(8,128)(2,1)S(1)} %get-tuple-element.19.refs_0_, bf16[64,1024]{1,0:T(8,128)(2,1)S(1)} %collective-permute-done.refs_1_, bf16[64,1024]{1,0:T(8,128)(2,1)S(1)} %collective-permute-done.1.refs_2_, ...), custom_call_target="tpu_custom_call" | custom-call | flops 200000000 | bytes 1447936 | tf_op jit(solution)/shard_map/pallas_call | solution.py:35
  25.8 1.6 %collective-permute-start.9 = (bf16[192,1024]{1,0:T(8,128)(2,1)S(1)}, bf16[192,1024]{1,0:T(8,128)(2,1)S(1)}, u32[]{:S(2)}, u32[]{:S(2)}) collective-permute-start(bf16[192,1024]{1,0:T(8,128)(2,1)S(1)} %shard_map.65.x_ref.refs_0_), channel_id=1, source_target_pairs={{0,16},{8,24},{16,0},{24,8},{1,17},{9,25},{17,1},{25,9},{2,18},{10... | collective-permute-start | bytes 1179656 | tf_op jit(solution)/shard_map/ppermute | solution.py:142
  27.4 1.7 %collective-permute-start.17 = (bf16[64,1024]{1,0:T(8,128)(2,1)S(1)}, bf16[64,1024]{1,0:T(8,128)(2,1)S(1)}, u32[]{:S(2)}, u32[]{:S(2)}) collective-permute-start(bf16[64,1024]{1,0:T(8,128)(2,1)S(1)} %get-tuple-element.26.refs_0_), channel_id=1, source_target_pairs={{0,1},{1,0},{2,3},{3,2},{4,5},{5,4},{6,7},{7,6},{8,9},{9,8},{10,11... | collective-permute-start | bytes 393224 | tf_op jit(solution)/shard_map/ppermute | solution.py:141
  29.0 0.4 collective-permute-start.21
  29.4 1.7 %collective-permute-start.19 = (bf16[64,1024]{1,0:T(8,128)(2,1)S(1)}, bf16[64,1024]{1,0:T(8,128)(2,1)S(1)}, u32[]{:S(2)}, u32[]{:S(2)}) collective-permute-start(bf16[64,1024]{1,0:T(8,128)(2,1)S(1)} %collective-permute-done.18.refs_2_), channel_id=1, source_target_pairs={{0,1},{1,0},{2,3},{3,2},{4,5},{5,4},{6,7},{7,6},{8,9},{9,8},{10,11... | collective-permute-start | bytes 393224 | tf_op jit(solution)/shard_map/ppermute | solution.py:141
  31.1 0.4 collective-permute-start.23
  31.4 2.3 %collective-permute-done.17.refs_1_ = bf16[64,1024]{1,0:T(8,128)(2,1)S(1)} collective-permute-done((bf16[64,1024]{1,0:T(8,128)(2,1)S(1)}, bf16[64,1024]{1,0:T(8,128)(2,1)S(1)}, u32[]{:S(2)}, u32[]{:S(2)}) %collective-permute-start.17) | collective-permute-done | bytes 131104 | tf_op jit(solution)/shard_map/ppermute | solution.py:141
  33.7 2.6 %collective-permute-done.21.refs_5_ = bf16[64,1024]{1,0:T(8,128)(2,1)S(1)} collective-permute-done((bf16[64,1024]{1,0:T(8,128)(2,1)S(1)}, bf16[64,1024]{1,0:T(8,128)(2,1)S(1)}, u32[]{:S(2)}, u32[]{:S(2)}) %collective-permute-start.21) | collective-permute-done | bytes 131104 | tf_op jit(solution)/shard_map/ppermute | solution.py:141
  36.4 1.4 %collective-permute-done.19.refs_3_ = bf16[64,1024]{1,0:T(8,128)(2,1)S(1)} collective-permute-done((bf16[64,1024]{1,0:T(8,128)(2,1)S(1)}, bf16[64,1024]{1,0:T(8,128)(2,1)S(1)}, u32[]{:S(2)}, u32[]{:S(2)}) %collective-permute-start.19) | collective-permute-done | bytes 131104 | tf_op jit(solution)/shard_map/ppermute | solution.py:141
  37.8 1.4 %collective-permute-done.23.refs_7_ = bf16[64,1024]{1,0:T(8,128)(2,1)S(1)} collective-permute-done((bf16[64,1024]{1,0:T(8,128)(2,1)S(1)}, bf16[64,1024]{1,0:T(8,128)(2,1)S(1)}, u32[]{:S(2)}, u32[]{:S(2)}) %collective-permute-start.23) | collective-permute-done | bytes 131104 | tf_op jit(solution)/shard_map/ppermute | solution.py:141
  39.2 1.8 %shard_map.73.x_ref.refs_0_ = bf16[192,1024]{1,0:T(8,128)(2,1)S(1)} custom-call(bf16[24,128]{1,0:T(8,128)(2,1)S(1)} %broadcast_in_dim.5.mask_ref, bf16[64,1024]{1,0:T(8,128)(2,1)S(1)} %get-tuple-element.26.refs_0_, bf16[64,1024]{1,0:T(8,128)(2,1)S(1)} %collective-permute-done.17.refs_1_, bf16[64,1024]{1,0:T(8,128)(2,1)S(1)} %collective-permute-done.18.refs_2_, ...), custom_call_target="tpu_custom_call" | custom-call | flops 200000000 | bytes 1447936 | tf_op jit(solution)/shard_map/pallas_call | solution.py:35
  41.0 0.6 collective-permute-start.26
  41.6 0.5 collective-permute-start.7
  42.1 7.1 %collective-permute-done.26.refs_0_ = bf16[192,1024]{1,0:T(8,128)(2,1)S(1)} collective-permute-done((bf16[192,1024]{1,0:T(8,128)(2,1)S(1)}, bf16[192,1024]{1,0:T(8,128)(2,1)S(1)}, u32[]{:S(2)}, u32[]{:S(2)}) %collective-permute-start.26) | collective-permute-done | bytes 393248 | tf_op jit(solution)/shard_map/ppermute | solution.py:142
  49.2 0.1 select_reduce_fusion.1
  49.4 0.6 collective-permute-start.24
  49.9 1.6 %copy-done.1 = bf16[1,1024,1024]{2,1,0:T(8,128)(2,1)S(1)} copy-done((bf16[1,1024,1024]{2,1,0:T(8,128)(2,1)S(1)}, bf16[1,1024,1024]{2,1,0:T(8,128)(2,1)}, u32[]{:S(2)}) %copy-start.1) | copy-done | bytes 2097176
  51.5 1.2 %shard_map.69 = bf16[192,1024]{1,0:T(8,128)(2,1)S(1)} custom-call(bf16[192,1024]{1,0:T(8,128)(2,1)S(1)} %collective-permute-done.10.refs_0_, bf16[1024,1024]{1,0:T(8,128)(2,1)S(1)} %bitcast.13, bf16[1024,1024]{1,0:T(8,128)(2,1)S(1)} %bitcast.19), custom_call_target="tpu_custom_call" | custom-call | flops 805306368 | bytes 4980736 | tf_op jit(solution)/shard_map/pallas_call | solution.py:35
  52.8 1.2 %shard_map.77 = bf16[192,1024]{1,0:T(8,128)(2,1)S(1)} custom-call(bf16[192,1024]{1,0:T(8,128)(2,1)S(1)} %collective-permute-done.27.refs_0_, bf16[1024,1024]{1,0:T(8,128)(2,1)S(1)} %bitcast.14, bf16[1024,1024]{1,0:T(8,128)(2,1)S(1)} %bitcast.20), custom_call_target="tpu_custom_call" | custom-call | flops 805306368 | bytes 4980736 | tf_op jit(solution)/shard_map/pallas_call | solution.py:35
  54.0 0.5 collective-permute-start.28
  54.5 2.0 %shard_map.67 = (bf16[192,1024]{1,0:T(8,128)(2,1)S(1)}, bf16[192,1024]{1,0:T(8,128)(2,1)S(1)}) custom-call(bf16[192,1024]{1,0:T(8,128)(2,1)S(1)} %shard_map.65.x_ref.refs_0_, bf16[192,1024]{1,0:T(8,128)(2,1)S(1)} %collective-permute-done.7.refs_1_, bf16[1024,1024]{1,0:T(8,128)(2,1)S(1)} %bitcast.15, bf16[1024,1024]{1,0:T(8,128)(2,1)S(1)} %bitcast.21), custom_call_target="tpu_custom_call" | custom-call | flops 1610612736 | bytes 5767168 | tf_op jit(solution)/shard_map/pallas_call | solution.py:35
  56.5 0.4 collective-permute-start.8
  56.9 1.2 %shard_map.68.a_ref = bf16[192,1024]{1,0:T(8,128)(2,1)S(1)} custom-call(bf16[192,1024]{1,0:T(8,128)(2,1)S(1)} %collective-permute-done.9.refs_0_, bf16[1024,1024]{1,0:T(8,128)(2,1)S(1)} %bitcast.16, bf16[1024,1024]{1,0:T(8,128)(2,1)S(1)} %bitcast.22), custom_call_target="tpu_custom_call" | custom-call | flops 805306368 | bytes 4980736 | tf_op jit(solution)/shard_map/pallas_call | solution.py:35
  58.2 0.6 collective-permute-start.12
  58.8 2.0 %shard_map.75 = (bf16[192,1024]{1,0:T(8,128)(2,1)S(1)}, bf16[192,1024]{1,0:T(8,128)(2,1)S(1)}) custom-call(bf16[192,1024]{1,0:T(8,128)(2,1)S(1)} %shard_map.73.x_ref.refs_0_, bf16[192,1024]{1,0:T(8,128)(2,1)S(1)} %collective-permute-done.24.refs_1_, bf16[1024,1024]{1,0:T(8,128)(2,1)S(1)} %bitcast.17, bf16[1024,1024]{1,0:T(8,128)(2,1)S(1)} %bitcast.23), custom_call_target="tpu_custom_call" | custom-call | flops 1610612736 | bytes 5767168 | tf_op jit(solution)/shard_map/pallas_call | solution.py:35
  60.9 1.2 %shard_map.76.a_ref = bf16[192,1024]{1,0:T(8,128)(2,1)S(1)} custom-call(bf16[192,1024]{1,0:T(8,128)(2,1)S(1)} %collective-permute-done.26.refs_0_, bf16[1024,1024]{1,0:T(8,128)(2,1)S(1)} %bitcast.18, bf16[1024,1024]{1,0:T(8,128)(2,1)S(1)} %bitcast.24), custom_call_target="tpu_custom_call" | custom-call | flops 805306368 | bytes 4980736 | tf_op jit(solution)/shard_map/pallas_call | solution.py:35
  62.2 1.5 %collective-permute-start.29 = (bf16[192,1024]{1,0:T(8,128)(2,1)S(1)}, bf16[192,1024]{1,0:T(8,128)(2,1)S(1)}, u32[]{:S(2)}, u32[]{:S(2)}) collective-permute-start(bf16[192,1024]{1,0:T(8,128)(2,1)S(1)} %shard_map.78), channel_id=1, source_target_pairs={{0,16},{8,24},{16,0},{24,8},{1,17},{9,25},{17,1},{25,9},{2,18},{10... | collective-permute-start | bytes 1179656 | tf_op jit(solution)/shard_map/ppermute | solution.py:142
  63.8 0.3 shard_map.66.refs_0_
  64.1 6.1 %collective-permute-done.12.refs_3_ = bf16[192,1024]{1,0:T(8,128)(2,1)S(1)} collective-permute-done((bf16[192,1024]{1,0:T(8,128)(2,1)S(1)}, bf16[192,1024]{1,0:T(8,128)(2,1)S(1)}, u32[]{:S(2)}, u32[]{:S(2)}) %collective-permute-start.12) | collective-permute-done | bytes 393248 | tf_op jit(solution)/shard_map/ppermute | solution.py:142
  70.3 0.2 shard_map.71.refs_0_
  70.4 0.7 collective-permute-start.13
  71.2 0.3 shard_map.74.refs_0_
  71.5 6.4 %collective-permute-done.29.refs_3_ = bf16[192,1024]{1,0:T(8,128)(2,1)S(1)} collective-permute-done((bf16[192,1024]{1,0:T(8,128)(2,1)S(1)}, bf16[192,1024]{1,0:T(8,128)(2,1)S(1)}, u32[]{:S(2)}, u32[]{:S(2)}) %collective-permute-start.29) | collective-permute-done | bytes 393248 | tf_op jit(solution)/shard_map/ppermute | solution.py:142
  77.9 0.2 shard_map.79.refs_0_
  78.1 0.7 collective-permute-start.30
  78.8 0.2 and_reduce_fusion.1
  79.2 0.8 collective-permute-done.13.refs_1_
  80.1 0.7 shard_map.72
  80.9 7.2 %collective-permute-start.14 = (bf16[64,1024]{1,0:T(8,128)(2,1)S(1)}, bf16[64,1024]{1,0:T(8,128)(2,1)S(1)}, u32[]{:S(2)}, u32[]{:S(2)}) collective-permute-start(bf16[64,1024]{1,0:T(8,128)(2,1)S(1)} %get-tuple-element.23), channel_id=1, source_target_pairs={{0,6},{1,7},{2,4},{3,5},{4,2},{5,3},{6,0},{7,1},{8,14},{9,15},{10,... | collective-permute-start | bytes 393224 | tf_op jit(solution)/shard_map/ppermute | solution.py:141
  88.1 0.6 collective-permute-start.16
  88.8 0.7 shard_map.80
  89.5 6.9 %collective-permute-start.31 = (bf16[64,1024]{1,0:T(8,128)(2,1)S(1)}, bf16[64,1024]{1,0:T(8,128)(2,1)S(1)}, u32[]{:S(2)}, u32[]{:S(2)}) collective-permute-start(bf16[64,1024]{1,0:T(8,128)(2,1)S(1)} %get-tuple-element.30), channel_id=1, source_target_pairs={{0,6},{1,7},{2,4},{3,5},{4,2},{5,3},{6,0},{7,1},{8,14},{9,15},{10,... | collective-permute-start | bytes 393224 | tf_op jit(solution)/shard_map/ppermute | solution.py:141
  96.4 1.6 %collective-permute-start.33 = (bf16[64,1024]{1,0:T(8,128)(2,1)S(1)}, bf16[64,1024]{1,0:T(8,128)(2,1)S(1)}, u32[]{:S(2)}, u32[]{:S(2)}) collective-permute-start(bf16[64,1024]{1,0:T(8,128)(2,1)S(1)} %get-tuple-element.32), channel_id=1, source_target_pairs={{0,2},{1,3},{2,0},{3,1},{4,6},{5,7},{6,4},{7,5},{8,10},{9,11},{10,... | collective-permute-start | bytes 393224 | tf_op jit(solution)/shard_map/ppermute | solution.py:141
  98.0 7.0 %collective-permute-done.15 = bf16[64,1024]{1,0:T(8,128)(2,1)S(1)} collective-permute-done((bf16[64,1024]{1,0:T(8,128)(2,1)S(1)}, bf16[64,1024]{1,0:T(8,128)(2,1)S(1)}, u32[]{:S(2)}, u32[]{:S(2)}) %collective-permute-start.15) | collective-permute-done | bytes 131104 | tf_op jit(solution)/shard_map/ppermute | solution.py:141
  105.1 4.8 %collective-permute-done.32 = bf16[64,1024]{1,0:T(8,128)(2,1)S(1)} collective-permute-done((bf16[64,1024]{1,0:T(8,128)(2,1)S(1)}, bf16[64,1024]{1,0:T(8,128)(2,1)S(1)}, u32[]{:S(2)}, u32[]{:S(2)}) %collective-permute-start.32) | collective-permute-done | bytes 131104 | tf_op jit(solution)/shard_map/ppermute | solution.py:141
  109.9 0.7 pad_maximum_fusion
  (60 shorter events, 1.3 us)
Async XLA Ops:
  0.0 49.9 %copy-start = (bf16[1,1024,1024]{2,1,0:T(8,128)(2,1)S(1)}, bf16[1,1024,1024]{2,1,0:T(8,128)(2,1)}, u32[]{:S(2)}) copy-start(bf16[1,1024,1024]{2,1,0:T(8,128)(2,1)} %param.10) | copy-start | bytes 6291460
  0.0 1.1 copy-start.4
  1.1 48.1 %copy-start.5 = (s32[8]{0:T(128)S(1)}, s32[8]{0:T(128)}, u32[]{:S(2)}) copy-start(s32[8]{0:T(128)} %param.7) | copy-start | bytes 100
  1.4 11.7 %collective-permute-start.3 = (bf16[64,1024]{1,0:T(8,128)(2,1)S(1)}, bf16[64,1024]{1,0:T(8,128)(2,1)S(1)}, u32[]{:S(2)}, u32[]{:S(2)}) collective-permute-start(bf16[64,1024]{1,0:T(8,128)(2,1)S(1)} %get-tuple-element.19.refs_0_), channel_id=1, source_target_pairs={{0,4},{1,5},{2,6},{3,7},{4,0},{5,1},{6,2},{7,3},{8,12},{9,13},{10,... | collective-permute-start | bytes 393224 | tf_op jit(solution)/shard_map/ppermute | solution.py:141
  5.6 10.2 %collective-permute-start.1 = (bf16[64,1024]{1,0:T(8,128)(2,1)S(1)}, bf16[64,1024]{1,0:T(8,128)(2,1)S(1)}, u32[]{:S(2)}, u32[]{:S(2)}) collective-permute-start(bf16[64,1024]{1,0:T(8,128)(2,1)S(1)} %get-tuple-element.19.refs_0_), channel_id=1, source_target_pairs={{0,2},{1,3},{2,0},{3,1},{4,6},{5,7},{6,4},{7,5},{8,10},{9,11},{10,... | collective-permute-start | bytes 393224 | tf_op jit(solution)/shard_map/ppermute | solution.py:141
  7.2 13.7 %collective-permute-start = (bf16[64,1024]{1,0:T(8,128)(2,1)S(1)}, bf16[64,1024]{1,0:T(8,128)(2,1)S(1)}, u32[]{:S(2)}, u32[]{:S(2)}) collective-permute-start(bf16[64,1024]{1,0:T(8,128)(2,1)S(1)} %get-tuple-element.19.refs_0_), channel_id=1, source_target_pairs={{0,1},{1,0},{2,3},{3,2},{4,5},{5,4},{6,7},{7,6},{8,9},{9,8},{10,11... | collective-permute-start | bytes 393224 | tf_op jit(solution)/shard_map/ppermute | solution.py:141
  8.7 12.4 %collective-permute-start.20 = (bf16[64,1024]{1,0:T(8,128)(2,1)S(1)}, bf16[64,1024]{1,0:T(8,128)(2,1)S(1)}, u32[]{:S(2)}, u32[]{:S(2)}) collective-permute-start(bf16[64,1024]{1,0:T(8,128)(2,1)S(1)} %get-tuple-element.26.refs_0_), channel_id=1, source_target_pairs={{0,4},{1,5},{2,6},{3,7},{4,0},{5,1},{6,2},{7,3},{8,12},{9,13},{10,... | collective-permute-start | bytes 393224 | tf_op jit(solution)/shard_map/ppermute | solution.py:141
  13.2 5.7 %collective-permute-start.5 = (bf16[64,1024]{1,0:T(8,128)(2,1)S(1)}, bf16[64,1024]{1,0:T(8,128)(2,1)S(1)}, u32[]{:S(2)}, u32[]{:S(2)}) collective-permute-start(bf16[64,1024]{1,0:T(8,128)(2,1)S(1)} %collective-permute-done.3.refs_4_), channel_id=1, source_target_pairs={{0,2},{1,3},{2,0},{3,1},{4,6},{5,7},{6,4},{7,5},{8,10},{9,11},{10,... | collective-permute-start | bytes 393224 | tf_op jit(solution)/shard_map/ppermute | solution.py:141
  13.6 9.3 %collective-permute-start.4 = (bf16[64,1024]{1,0:T(8,128)(2,1)S(1)}, bf16[64,1024]{1,0:T(8,128)(2,1)S(1)}, u32[]{:S(2)}, u32[]{:S(2)}) collective-permute-start(bf16[64,1024]{1,0:T(8,128)(2,1)S(1)} %collective-permute-done.3.refs_4_), channel_id=1, source_target_pairs={{0,1},{1,0},{2,3},{3,2},{4,5},{5,4},{6,7},{7,6},{8,9},{9,8},{10,11... | collective-permute-start | bytes 393224 | tf_op jit(solution)/shard_map/ppermute | solution.py:141
  15.7 7.2 %collective-permute-start.2 = (bf16[64,1024]{1,0:T(8,128)(2,1)S(1)}, bf16[64,1024]{1,0:T(8,128)(2,1)S(1)}, u32[]{:S(2)}, u32[]{:S(2)}) collective-permute-start(bf16[64,1024]{1,0:T(8,128)(2,1)S(1)} %collective-permute-done.1.refs_2_), channel_id=1, source_target_pairs={{0,1},{1,0},{2,3},{3,2},{4,5},{5,4},{6,7},{7,6},{8,9},{9,8},{10,11... | collective-permute-start | bytes 393224 | tf_op jit(solution)/shard_map/ppermute | solution.py:141
  18.9 5.0 %collective-permute-start.6 = (bf16[64,1024]{1,0:T(8,128)(2,1)S(1)}, bf16[64,1024]{1,0:T(8,128)(2,1)S(1)}, u32[]{:S(2)}, u32[]{:S(2)}) collective-permute-start(bf16[64,1024]{1,0:T(8,128)(2,1)S(1)} %collective-permute-done.5.refs_6_), channel_id=1, source_target_pairs={{0,1},{1,0},{2,3},{3,2},{4,5},{5,4},{6,7},{7,6},{8,9},{9,8},{10,11... | collective-permute-start | bytes 393224 | tf_op jit(solution)/shard_map/ppermute | solution.py:141
  20.9 8.5 %collective-permute-start.18 = (bf16[64,1024]{1,0:T(8,128)(2,1)S(1)}, bf16[64,1024]{1,0:T(8,128)(2,1)S(1)}, u32[]{:S(2)}, u32[]{:S(2)}) collective-permute-start(bf16[64,1024]{1,0:T(8,128)(2,1)S(1)} %get-tuple-element.26.refs_0_), channel_id=1, source_target_pairs={{0,2},{1,3},{2,0},{3,1},{4,6},{5,7},{6,4},{7,5},{8,10},{9,11},{10,... | collective-permute-start | bytes 393224 | tf_op jit(solution)/shard_map/ppermute | solution.py:141
  21.1 10.0 %collective-permute-start.22 = (bf16[64,1024]{1,0:T(8,128)(2,1)S(1)}, bf16[64,1024]{1,0:T(8,128)(2,1)S(1)}, u32[]{:S(2)}, u32[]{:S(2)}) collective-permute-start(bf16[64,1024]{1,0:T(8,128)(2,1)S(1)} %collective-permute-done.20.refs_4_), channel_id=1, source_target_pairs={{0,2},{1,3},{2,0},{3,1},{4,6},{5,7},{6,4},{7,5},{8,10},{9,11},{10,... | collective-permute-start | bytes 393224 | tf_op jit(solution)/shard_map/ppermute | solution.py:141
  25.8 15.8 %collective-permute-start.9 = (bf16[192,1024]{1,0:T(8,128)(2,1)S(1)}, bf16[192,1024]{1,0:T(8,128)(2,1)S(1)}, u32[]{:S(2)}, u32[]{:S(2)}) collective-permute-start(bf16[192,1024]{1,0:T(8,128)(2,1)S(1)} %shard_map.65.x_ref.refs_0_), channel_id=1, source_target_pairs={{0,16},{8,24},{16,0},{24,8},{1,17},{9,25},{17,1},{25,9},{2,18},{10... | collective-permute-start | bytes 1179656 | tf_op jit(solution)/shard_map/ppermute | solution.py:142
  27.4 6.4 %collective-permute-start.17 = (bf16[64,1024]{1,0:T(8,128)(2,1)S(1)}, bf16[64,1024]{1,0:T(8,128)(2,1)S(1)}, u32[]{:S(2)}, u32[]{:S(2)}) collective-permute-start(bf16[64,1024]{1,0:T(8,128)(2,1)S(1)} %get-tuple-element.26.refs_0_), channel_id=1, source_target_pairs={{0,1},{1,0},{2,3},{3,2},{4,5},{5,4},{6,7},{7,6},{8,9},{9,8},{10,11... | collective-permute-start | bytes 393224 | tf_op jit(solution)/shard_map/ppermute | solution.py:141
  29.0 7.3 %collective-permute-start.21 = (bf16[64,1024]{1,0:T(8,128)(2,1)S(1)}, bf16[64,1024]{1,0:T(8,128)(2,1)S(1)}, u32[]{:S(2)}, u32[]{:S(2)}) collective-permute-start(bf16[64,1024]{1,0:T(8,128)(2,1)S(1)} %collective-permute-done.20.refs_4_), channel_id=1, source_target_pairs={{0,1},{1,0},{2,3},{3,2},{4,5},{5,4},{6,7},{7,6},{8,9},{9,8},{10,11... | collective-permute-start | bytes 393224 | tf_op jit(solution)/shard_map/ppermute | solution.py:141
  29.4 8.4 %collective-permute-start.19 = (bf16[64,1024]{1,0:T(8,128)(2,1)S(1)}, bf16[64,1024]{1,0:T(8,128)(2,1)S(1)}, u32[]{:S(2)}, u32[]{:S(2)}) collective-permute-start(bf16[64,1024]{1,0:T(8,128)(2,1)S(1)} %collective-permute-done.18.refs_2_), channel_id=1, source_target_pairs={{0,1},{1,0},{2,3},{3,2},{4,5},{5,4},{6,7},{7,6},{8,9},{9,8},{10,11... | collective-permute-start | bytes 393224 | tf_op jit(solution)/shard_map/ppermute | solution.py:141
  31.1 8.1 %collective-permute-start.23 = (bf16[64,1024]{1,0:T(8,128)(2,1)S(1)}, bf16[64,1024]{1,0:T(8,128)(2,1)S(1)}, u32[]{:S(2)}, u32[]{:S(2)}) collective-permute-start(bf16[64,1024]{1,0:T(8,128)(2,1)S(1)} %collective-permute-done.22.refs_6_), channel_id=1, source_target_pairs={{0,1},{1,0},{2,3},{3,2},{4,5},{5,4},{6,7},{7,6},{8,9},{9,8},{10,11... | collective-permute-start | bytes 393224 | tf_op jit(solution)/shard_map/ppermute | solution.py:141
  41.0 8.2 %collective-permute-start.26 = (bf16[192,1024]{1,0:T(8,128)(2,1)S(1)}, bf16[192,1024]{1,0:T(8,128)(2,1)S(1)}, u32[]{:S(2)}, u32[]{:S(2)}) collective-permute-start(bf16[192,1024]{1,0:T(8,128)(2,1)S(1)} %shard_map.73.x_ref.refs_0_), channel_id=1, source_target_pairs={{0,16},{8,24},{16,0},{24,8},{1,17},{9,25},{17,1},{25,9},{2,18},{10... | collective-permute-start | bytes 1179656 | tf_op jit(solution)/shard_map/ppermute | solution.py:142
  41.6 8.3 %collective-permute-start.10 = (bf16[192,1024]{1,0:T(8,128)(2,1)S(1)}, bf16[192,1024]{1,0:T(8,128)(2,1)S(1)}, u32[]{:S(2)}, u32[]{:S(2)}) collective-permute-start(bf16[192,1024]{1,0:T(8,128)(2,1)S(1)} %collective-permute-done.9.refs_0_), channel_id=1, source_target_pairs={{0,8},{8,0},{16,24},{24,16},{1,9},{9,1},{17,25},{25,17},{2,10},{10... | collective-permute-start | bytes 1179656 | tf_op jit(solution)/shard_map/ppermute | solution.py:142
  41.6 12.9 %collective-permute-start.7 = (bf16[192,1024]{1,0:T(8,128)(2,1)S(1)}, bf16[192,1024]{1,0:T(8,128)(2,1)S(1)}, u32[]{:S(2)}, u32[]{:S(2)}) collective-permute-start(bf16[192,1024]{1,0:T(8,128)(2,1)S(1)} %shard_map.65.x_ref.refs_0_), channel_id=1, source_target_pairs={{0,8},{8,0},{16,24},{24,16},{1,9},{9,1},{17,25},{25,17},{2,10},{10... | collective-permute-start | bytes 1179656 | tf_op jit(solution)/shard_map/ppermute | solution.py:142
  49.2 3.6 %collective-permute-start.27 = (bf16[192,1024]{1,0:T(8,128)(2,1)S(1)}, bf16[192,1024]{1,0:T(8,128)(2,1)S(1)}, u32[]{:S(2)}, u32[]{:S(2)}) collective-permute-start(bf16[192,1024]{1,0:T(8,128)(2,1)S(1)} %collective-permute-done.26.refs_0_), channel_id=1, source_target_pairs={{0,8},{8,0},{16,24},{24,16},{1,9},{9,1},{17,25},{25,17},{2,10},{10... | collective-permute-start | bytes 1179656 | tf_op jit(solution)/shard_map/ppermute | solution.py:142
  49.4 9.5 %collective-permute-start.24 = (bf16[192,1024]{1,0:T(8,128)(2,1)S(1)}, bf16[192,1024]{1,0:T(8,128)(2,1)S(1)}, u32[]{:S(2)}, u32[]{:S(2)}) collective-permute-start(bf16[192,1024]{1,0:T(8,128)(2,1)S(1)} %shard_map.73.x_ref.refs_0_), channel_id=1, source_target_pairs={{0,8},{8,0},{16,24},{24,16},{1,9},{9,1},{17,25},{25,17},{2,10},{10... | collective-permute-start | bytes 1179656 | tf_op jit(solution)/shard_map/ppermute | solution.py:142
  49.9 1.6 %copy-start.1 = (bf16[1,1024,1024]{2,1,0:T(8,128)(2,1)S(1)}, bf16[1,1024,1024]{2,1,0:T(8,128)(2,1)}, u32[]{:S(2)}) copy-start(bf16[1,1024,1024]{2,1,0:T(8,128)(2,1)} %param.11) | copy-start | bytes 6291460
  52.7 5.4 %collective-permute-start.11 = (bf16[192,1024]{1,0:T(8,128)(2,1)S(1)}, bf16[192,1024]{1,0:T(8,128)(2,1)S(1)}, u32[]{:S(2)}, u32[]{:S(2)}) collective-permute-start(bf16[192,1024]{1,0:T(8,128)(2,1)S(1)} %shard_map.69), channel_id=1, source_target_pairs={{0,8},{8,0},{16,24},{24,16},{1,9},{9,1},{17,25},{25,17},{2,10},{10... | collective-permute-start | bytes 1179656 | tf_op jit(solution)/shard_map/ppermute | solution.py:142
  52.8 1.7 %copy-start.2 = (bf16[1,1024,1024]{2,1,0:T(8,128)(2,1)S(1)}, bf16[1,1024,1024]{2,1,0:T(8,128)(2,1)}, u32[]{:S(2)}) copy-start(bf16[1,1024,1024]{2,1,0:T(8,128)(2,1)} %param.11) | copy-start | bytes 6291460
  54.0 8.1 %collective-permute-start.28 = (bf16[192,1024]{1,0:T(8,128)(2,1)S(1)}, bf16[192,1024]{1,0:T(8,128)(2,1)S(1)}, u32[]{:S(2)}, u32[]{:S(2)}) collective-permute-start(bf16[192,1024]{1,0:T(8,128)(2,1)S(1)} %shard_map.77), channel_id=1, source_target_pairs={{0,8},{8,0},{16,24},{24,16},{1,9},{9,1},{17,25},{25,17},{2,10},{10... | collective-permute-start | bytes 1179656 | tf_op jit(solution)/shard_map/ppermute | solution.py:142
  56.5 7.6 %collective-permute-start.8 = (bf16[192,1024]{1,0:T(8,128)(2,1)S(1)}, bf16[192,1024]{1,0:T(8,128)(2,1)S(1)}, u32[]{:S(2)}, u32[]{:S(2)}) collective-permute-start(bf16[192,1024]{1,0:T(8,128)(2,1)S(1)} %get-tuple-element.21), channel_id=1, source_target_pairs={{0,8},{8,0},{16,24},{24,16},{1,9},{9,1},{17,25},{25,17},{2,10},{10... | collective-permute-start | bytes 1179656 | tf_op jit(solution)/shard_map/ppermute | solution.py:142
  58.2 12.1 %collective-permute-start.12 = (bf16[192,1024]{1,0:T(8,128)(2,1)S(1)}, bf16[192,1024]{1,0:T(8,128)(2,1)S(1)}, u32[]{:S(2)}, u32[]{:S(2)}) collective-permute-start(bf16[192,1024]{1,0:T(8,128)(2,1)S(1)} %shard_map.70), channel_id=1, source_target_pairs={{0,16},{8,24},{16,0},{24,8},{1,17},{9,25},{17,1},{25,9},{2,18},{10... | collective-permute-start | bytes 1179656 | tf_op jit(solution)/shard_map/ppermute | solution.py:142
  60.8 3.0 %copy-start.3 = (bf16[1024,48]{0,1:T(8,128)(2,1)S(1)}, bf16[1024,48]{0,1:T(8,128)(2,1)}, u32[]{:S(2)}) copy-start(bf16[1024,48]{0,1:T(8,128)(2,1)} %param.9) | copy-start | bytes 294916
  60.8 10.6 %collective-permute-start.25 = (bf16[192,1024]{1,0:T(8,128)(2,1)S(1)}, bf16[192,1024]{1,0:T(8,128)(2,1)S(1)}, u32[]{:S(2)}, u32[]{:S(2)}) collective-permute-start(bf16[192,1024]{1,0:T(8,128)(2,1)S(1)} %get-tuple-element.28), channel_id=1, source_target_pairs={{0,8},{8,0},{16,24},{24,16},{1,9},{9,1},{17,25},{25,17},{2,10},{10... | collective-permute-start | bytes 1179656 | tf_op jit(solution)/shard_map/ppermute | solution.py:142
  62.2 15.7 %collective-permute-start.29 = (bf16[192,1024]{1,0:T(8,128)(2,1)S(1)}, bf16[192,1024]{1,0:T(8,128)(2,1)S(1)}, u32[]{:S(2)}, u32[]{:S(2)}) collective-permute-start(bf16[192,1024]{1,0:T(8,128)(2,1)S(1)} %shard_map.78), channel_id=1, source_target_pairs={{0,16},{8,24},{16,0},{24,8},{1,17},{9,25},{17,1},{25,9},{2,18},{10... | collective-permute-start | bytes 1179656 | tf_op jit(solution)/shard_map/ppermute | solution.py:142
  70.4 9.6 %collective-permute-start.13 = (bf16[192,1024]{1,0:T(8,128)(2,1)S(1)}, bf16[192,1024]{1,0:T(8,128)(2,1)S(1)}, u32[]{:S(2)}, u32[]{:S(2)}) collective-permute-start(bf16[192,1024]{1,0:T(8,128)(2,1)S(1)} %shard_map.71.refs_0_), channel_id=1, source_target_pairs={{0,1},{1,0},{2,3},{3,2},{4,5},{5,4},{6,7},{7,6},{8,9},{9,8},{10,11... | collective-permute-start | bytes 1179656 | tf_op jit(solution)/shard_map/ppermute | solution.py:141
  78.1 10.7 %collective-permute-start.30 = (bf16[192,1024]{1,0:T(8,128)(2,1)S(1)}, bf16[192,1024]{1,0:T(8,128)(2,1)S(1)}, u32[]{:S(2)}, u32[]{:S(2)}) collective-permute-start(bf16[192,1024]{1,0:T(8,128)(2,1)S(1)} %shard_map.79.refs_0_), channel_id=1, source_target_pairs={{0,1},{1,0},{2,3},{3,2},{4,5},{5,4},{6,7},{7,6},{8,9},{9,8},{10,11... | collective-permute-start | bytes 1179656 | tf_op jit(solution)/shard_map/ppermute | solution.py:141
  80.9 15.5 %collective-permute-start.14 = (bf16[64,1024]{1,0:T(8,128)(2,1)S(1)}, bf16[64,1024]{1,0:T(8,128)(2,1)S(1)}, u32[]{:S(2)}, u32[]{:S(2)}) collective-permute-start(bf16[64,1024]{1,0:T(8,128)(2,1)S(1)} %get-tuple-element.23), channel_id=1, source_target_pairs={{0,6},{1,7},{2,4},{3,5},{4,2},{5,3},{6,0},{7,1},{8,14},{9,15},{10,... | collective-permute-start | bytes 393224 | tf_op jit(solution)/shard_map/ppermute | solution.py:141
  88.1 16.8 %collective-permute-start.15 = (bf16[64,1024]{1,0:T(8,128)(2,1)S(1)}, bf16[64,1024]{1,0:T(8,128)(2,1)S(1)}, u32[]{:S(2)}, u32[]{:S(2)}) collective-permute-start(bf16[64,1024]{1,0:T(8,128)(2,1)S(1)} %get-tuple-element.24), channel_id=1, source_target_pairs={{0,4},{1,5},{2,6},{3,7},{4,0},{5,1},{6,2},{7,3},{8,12},{9,13},{10,... | collective-permute-start | bytes 393224 | tf_op jit(solution)/shard_map/ppermute | solution.py:141
  88.1 16.8 %collective-permute-start.16 = (bf16[64,1024]{1,0:T(8,128)(2,1)S(1)}, bf16[64,1024]{1,0:T(8,128)(2,1)S(1)}, u32[]{:S(2)}, u32[]{:S(2)}) collective-permute-start(bf16[64,1024]{1,0:T(8,128)(2,1)S(1)} %get-tuple-element.25), channel_id=1, source_target_pairs={{0,2},{1,3},{2,0},{3,1},{4,6},{5,7},{6,4},{7,5},{8,10},{9,11},{10,... | collective-permute-start | bytes 393224 | tf_op jit(solution)/shard_map/ppermute | solution.py:141
  89.5 15.5 %collective-permute-start.31 = (bf16[64,1024]{1,0:T(8,128)(2,1)S(1)}, bf16[64,1024]{1,0:T(8,128)(2,1)S(1)}, u32[]{:S(2)}, u32[]{:S(2)}) collective-permute-start(bf16[64,1024]{1,0:T(8,128)(2,1)S(1)} %get-tuple-element.30), channel_id=1, source_target_pairs={{0,6},{1,7},{2,4},{3,5},{4,2},{5,3},{6,0},{7,1},{8,14},{9,15},{10,... | collective-permute-start | bytes 393224 | tf_op jit(solution)/shard_map/ppermute | solution.py:141
  96.4 13.4 %collective-permute-start.32 = (bf16[64,1024]{1,0:T(8,128)(2,1)S(1)}, bf16[64,1024]{1,0:T(8,128)(2,1)S(1)}, u32[]{:S(2)}, u32[]{:S(2)}) collective-permute-start(bf16[64,1024]{1,0:T(8,128)(2,1)S(1)} %get-tuple-element.31), channel_id=1, source_target_pairs={{0,4},{1,5},{2,6},{3,7},{4,0},{5,1},{6,2},{7,3},{8,12},{9,13},{10,... | collective-permute-start | bytes 393224 | tf_op jit(solution)/shard_map/ppermute | solution.py:141
  96.4 13.4 %collective-permute-start.33 = (bf16[64,1024]{1,0:T(8,128)(2,1)S(1)}, bf16[64,1024]{1,0:T(8,128)(2,1)S(1)}, u32[]{:S(2)}, u32[]{:S(2)}) collective-permute-start(bf16[64,1024]{1,0:T(8,128)(2,1)S(1)} %get-tuple-element.32), channel_id=1, source_target_pairs={{0,2},{1,3},{2,0},{3,1},{4,6},{5,7},{6,4},{7,5},{8,10},{9,11},{10,... | collective-permute-start | bytes 393224 | tf_op jit(solution)/shard_map/ppermute | solution.py:141

commit v2 on v1

--- a/solution.py
+++ b/solution.py
@@ -14,8 +14,8 @@
 MAJOR = 4
 CORES = 2
 SPLIT_SPARE = 4
-SELECT_SPARE = 8
 LANES = 128
+DIRECT = (0,)
 
 
 VMEM = pl.BlockSpec(memory_space=pltpu.VMEM)
@@ -71,20 +71,23 @@
         copy.wait()
 
 
-def select_body(capacity, n, mask_ref, *refs):
-    blocks, out_ref, held, sems = refs[:n], refs[n], refs[n + 1], refs[n + 2]
-    copies = [pltpu.make_async_copy(blocks[k], held.at[k], sems.at[k]) for k in range(1, n)]
-    for copy in copies:
-        copy.start()
-    rows = held.shape[1]
-    for k in range(n):
-        if k:
-            copies[k - 1].wait()
-        for s in range(capacity):
-            flag = mask_ref[pl.ds(s * n + k, 1), :][:, :1]
-            term = (held[k] if k else blocks[0][...]) * flag
-            part = pl.ds(s * rows, rows)
-            out_ref[part, :] = out_ref[part, :] + term if k else term
+def select_body(capacity, n, source_ref, *refs):
+    blocks, out_ref, sems = refs[:n], refs[n], refs[n + 1]
+    rows = blocks[0].shape[0]
+    for s in range(capacity):
+        source = jnp.max(source_ref[pl.ds(s, 1), :])
+        for k in range(n):
+
+            @pl.when(source == k)
+            def _():
+                pltpu.make_async_copy(
+                    blocks[k], out_ref.at[pl.ds(s * rows, rows), :], sems.at[s]
+                ).start()
+
+    for s in range(capacity):
+        pltpu.make_async_copy(
+            blocks[0], out_ref.at[pl.ds(s * rows, rows), :], sems.at[s]
+        ).wait()
 
 
 def ffn_body(n, *refs):
@@ -123,7 +126,7 @@
                 for s in range(capacity):
                     flag = mask_ref[pl.ds((ka * n + k) * capacity + s, 1), :][:, :1]
                     piece = arrived[k][pl.ds(s * rows + start, step), :]
-                    term = piece.astype(jnp.float32) * flag
+                    term = piece * flag
                     value = term if value is None else value + term
             outs[ka][pl.ds(start, step), :] = value.astype(outs[ka].dtype)
 
@@ -152,17 +155,17 @@
     table = chosen[:, None, :] & (rank[:, None, :] == slots[None, :, None])
     hit = table[0].astype(jnp.int32)
     other = jnp.where(routing[:, 0] == me, routing[:, 1], routing[:, 0])
+    home = jnp.sum(hit * blocks[None, :], axis=1)
     slot_task = jnp.sum(hit * task_ids[None, :], axis=1)
     slot_other = jnp.sum(hit * other[None, :], axis=1)
     spread = lambda x: jnp.broadcast_to(x.reshape(-1, 1), (x.size, LANES))
 
-    relative = (blocks[None, None, :] ^ me) == blocks[None, :, None]
-    select_mask = spread(jnp.any(table[0][:, None, :] & relative, axis=2).astype(jnp.bfloat16))
+    source = spread((home ^ me).astype(jnp.float32))
     targets = me ^ (blocks[:major] * minor)
     place_mask = spread(
         jnp.any(
             table[None] & (blocks[None, None, None, :] == targets[:, None, None, None]), axis=3
-        ).astype(jnp.float32)
+        ).astype(jnp.bfloat16)
     )
     columns = jnp.arange(gate_weight.shape[1], dtype=jnp.int32)
     pick_self = columns[None, :] == (slot_task * n_experts + me)[:, None]
@@ -188,12 +191,12 @@
         scratch=[pltpu.SemaphoreType.DMA((len(split),))],
     )
     outs = []
-    for own, rows in zip(owns, split):
+    for stream, (own, rows) in enumerate(zip(owns, split)):
         full = shape(capacity * rows)
 
         gathered = {0: own}
         for mask in range(1, major):
-            low = mask & -mask
+            low = mask if stream in DIRECT else mask & -mask
             gathered[mask * minor] = move(gathered[(mask ^ low) * minor], low * minor)
         for ka in range(major):
             for kb in range(1, minor):
@@ -201,13 +204,10 @@
         picked = call(
             functools.partial(select_body, capacity, n_experts),
             full,
-            select_mask, *[gathered[k] for k in range(n_experts)],
-            flops=2e8, spare=SELECT_SPARE * 2**20,
-            in_specs=[VMEM] * 2 + [ANY] * (n_experts - 1),
-            scratch=[
-                pltpu.VMEM((n_experts, rows, width), jnp.bfloat16),
-                pltpu.SemaphoreType.DMA((n_experts,)),
-            ],
+            source, *[gathered[k] for k in range(n_experts)],
+            flops=2e8,
+            in_specs=[VMEM] + [ANY] * n_experts,
+            scratch=[pltpu.SemaphoreType.DMA((capacity,))],
         )
 
         foreign = {chip: move_dp(picked, chip * CORES) for chip in range(1, chips)}

time: 111 us -> 108 us (0.973)
  waiting for transfers between devices: 46.6 us -> 43.5 us
  Pallas kernels: 15.2 us -> 12.9 us
  starting transfers between devices: 42.3 us -> 44 us
    ppermute x22, waiting for transfers between devices: 26.9 us -> 24.4 us  [shards(): move = lambda x, mask: lax.ppermute(x, 'expert', xor_pairs(n_experts, mask))]
    pallas_call x17, Pallas kernels: 15.2 us -> 12.9 us  [call(): pl.pallas_call(body, out_shape=out_shapes, in_specs=in_specs or [VMEM] *...]
    ppermute x22, starting transfers between devices: 35.7 us -> 37.2 us  [shards(): move = lambda x, mask: lax.ppermute(x, 'expert', xor_pairs(n_experts, mask))]
    unnamed x12 -> x10, local copies, waits for them, and re-layouts: 2.71 us -> 2.7 us
  transfers between devices with their start and end apart: 34 -> 34, of which waited for: 13 -> 15; matrix products, arithmetic and copies ran while one was open for 3% -> 3% of each run, Pallas kernels for 13% -> 12%
where the time goes in v2:
time: 108 us; the launch traced here: 107 us
  starting transfers between devices  44 us (41%)
  waiting for transfers between devices  43.5 us (40%)
  Pallas kernels  12.9 us (12%)
  other arithmetic  3.72 us (3%)
  local copies, waits for them, and re-layouts  3.05 us (3%)
    ppermute x22, starting transfers between devices, shards(): move = lambda x, mask: lax.ppermute(x, 'expert', xor_pairs(n_experts, mask))  37.2 us
    ppermute x22, waiting for transfers between devices, shards(): move = lambda x, mask: lax.ppermute(x, 'expert', xor_pairs(n_experts, mask))  24.4 us
    ppermute x12, waiting for transfers between devices, shards(): move_dp = lambda x, mask: lax.ppermute(x, 'dp', xor_pairs(n_dp, mask))  19.1 us
    pallas_call x17, Pallas kernels, call(): pl.pallas_call(body, out_shape=out_shapes, in_specs=in_specs or [VMEM] *...  12.9 us
    ppermute x12, starting transfers between devices, shards(): move_dp = lambda x, mask: lax.ppermute(x, 'dp', xor_pairs(n_dp, mask))  6.89 us
    unnamed x10, local copies, waits for them, and re-layouts  2.7 us
  transfers between devices with their start and end apart: 34, of which 15 were waited for; matrix products, arithmetic and copies ran while one was open for 3% of the time, Pallas kernels for 12%

profile of v2, /device:TPU:0, one launch (start us, length us, event | category | flops | bytes accessed | tf_op | source)
XLA Modules:
  0.0 107.4 jit_solution(4919983601801179073)
XLA Ops:
  0.0 1.1 %copy-done.4 = bf16[128,1024]{1,0:T(8,128)(2,1)S(1)} copy-done((bf16[128,1024]{1,0:T(8,128)(2,1)S(1)}, bf16[128,1024]{1,0:T(8,128)(2,1)}, u32[]{:S(2)}) %copy-start.4) | copy-done | bytes 262168
  1.1 0.3 shard_map.64
  1.4 3.1 %collective-permute-start.1 = (bf16[64,1024]{1,0:T(8,128)(2,1)S(1)}, bf16[64,1024]{1,0:T(8,128)(2,1)S(1)}, u32[]{:S(2)}, u32[]{:S(2)}) collective-permute-start(bf16[64,1024]{1,0:T(8,128)(2,1)S(1)} %get-tuple-element.19.refs_0_), channel_id=1, source_target_pairs={{0,2},{1,3},{2,0},{3,1},{4,6},{5,7},{6,4},{7,5},{8,10},{9,11},{10,... | collective-permute-start | bytes 393224 | tf_op jit(solution)/shard_map/ppermute | solution.py:144
  4.6 2.6 %collective-permute-start.3 = (bf16[64,1024]{1,0:T(8,128)(2,1)S(1)}, bf16[64,1024]{1,0:T(8,128)(2,1)S(1)}, u32[]{:S(2)}, u32[]{:S(2)}) collective-permute-start(bf16[64,1024]{1,0:T(8,128)(2,1)S(1)} %get-tuple-element.19.refs_0_), channel_id=1, source_target_pairs={{0,4},{1,5},{2,6},{3,7},{4,0},{5,1},{6,2},{7,3},{8,12},{9,13},{10,... | collective-permute-start | bytes 393224 | tf_op jit(solution)/shard_map/ppermute | solution.py:144
  7.1 1.7 %collective-permute-start = (bf16[64,1024]{1,0:T(8,128)(2,1)S(1)}, bf16[64,1024]{1,0:T(8,128)(2,1)S(1)}, u32[]{:S(2)}, u32[]{:S(2)}) collective-permute-start(bf16[64,1024]{1,0:T(8,128)(2,1)S(1)} %get-tuple-element.19.refs_0_), channel_id=1, source_target_pairs={{0,1},{1,0},{2,3},{3,2},{4,5},{5,4},{6,7},{7,6},{8,9},{9,8},{10,11... | collective-permute-start | bytes 393224 | tf_op jit(solution)/shard_map/ppermute | solution.py:144
  8.9 1.7 %collective-permute-start.20 = (bf16[64,1024]{1,0:T(8,128)(2,1)S(1)}, bf16[64,1024]{1,0:T(8,128)(2,1)S(1)}, u32[]{:S(2)}, u32[]{:S(2)}) collective-permute-start(bf16[64,1024]{1,0:T(8,128)(2,1)S(1)} %get-tuple-element.26.refs_0_), channel_id=1, source_target_pairs={{0,4},{1,5},{2,6},{3,7},{4,0},{5,1},{6,2},{7,3},{8,12},{9,13},{10,... | collective-permute-start | bytes 393224 | tf_op jit(solution)/shard_map/ppermute | solution.py:144
  10.6 0.8 compare_reduce_fusion
  11.5 0.8 compare_select_fusion
  12.3 0.8 select_reduce_fusion
  13.1 2.5 %collective-permute-start.18 = (bf16[64,1024]{1,0:T(8,128)(2,1)S(1)}, bf16[64,1024]{1,0:T(8,128)(2,1)S(1)}, u32[]{:S(2)}, u32[]{:S(2)}) collective-permute-start(bf16[64,1024]{1,0:T(8,128)(2,1)S(1)} %get-tuple-element.26.refs_0_), channel_id=1, source_target_pairs={{0,2},{1,3},{2,0},{3,1},{4,6},{5,7},{6,4},{7,5},{8,10},{9,11},{10,... | collective-permute-start | bytes 393224 | tf_op jit(solution)/shard_map/ppermute | solution.py:144
  15.6 4.6 %collective-permute-done.3.refs_4_ = bf16[64,1024]{1,0:T(8,128)(2,1)S(1)} collective-permute-done((bf16[64,1024]{1,0:T(8,128)(2,1)S(1)}, bf16[64,1024]{1,0:T(8,128)(2,1)S(1)}, u32[]{:S(2)}, u32[]{:S(2)}) %collective-permute-start.3) | collective-permute-done | bytes 131104 | tf_op jit(solution)/shard_map/ppermute | solution.py:144
  20.2 1.5 %collective-permute-start.2 = (bf16[64,1024]{1,0:T(8,128)(2,1)S(1)}, bf16[64,1024]{1,0:T(8,128)(2,1)S(1)}, u32[]{:S(2)}, u32[]{:S(2)}) collective-permute-start(bf16[64,1024]{1,0:T(8,128)(2,1)S(1)} %collective-permute-done.1.refs_2_), channel_id=1, source_target_pairs={{0,1},{1,0},{2,3},{3,2},{4,5},{5,4},{6,7},{7,6},{8,9},{9,8},{10,11... | collective-permute-start | bytes 393224 | tf_op jit(solution)/shard_map/ppermute | solution.py:144
  21.8 0.5 collective-permute-start.4
  22.3 1.5 %collective-permute-start.6 = (bf16[64,1024]{1,0:T(8,128)(2,1)S(1)}, bf16[64,1024]{1,0:T(8,128)(2,1)S(1)}, u32[]{:S(2)}, u32[]{:S(2)}) collective-permute-start(bf16[64,1024]{1,0:T(8,128)(2,1)S(1)} %collective-permute-done.5.refs_6_), channel_id=1, source_target_pairs={{0,1},{1,0},{2,3},{3,2},{4,5},{5,4},{6,7},{7,6},{8,9},{9,8},{10,11... | collective-permute-start | bytes 393224 | tf_op jit(solution)/shard_map/ppermute | solution.py:144
  23.8 0.7 collective-permute-done.20.refs_4_
  24.5 1.2 %collective-permute-start.22 = (bf16[64,1024]{1,0:T(8,128)(2,1)S(1)}, bf16[64,1024]{1,0:T(8,128)(2,1)S(1)}, u32[]{:S(2)}, u32[]{:S(2)}) collective-permute-start(bf16[64,1024]{1,0:T(8,128)(2,1)S(1)} %collective-permute-done.20.refs_4_), channel_id=1, source_target_pairs={{0,2},{1,3},{2,0},{3,1},{4,6},{5,7},{6,4},{7,5},{8,10},{9,11},{10,... | collective-permute-start | bytes 393224 | tf_op jit(solution)/shard_map/ppermute | solution.py:144
  25.7 1.1 %collective-permute-done.4.refs_5_ = bf16[64,1024]{1,0:T(8,128)(2,1)S(1)} collective-permute-done((bf16[64,1024]{1,0:T(8,128)(2,1)S(1)}, bf16[64,1024]{1,0:T(8,128)(2,1)S(1)}, u32[]{:S(2)}, u32[]{:S(2)}) %collective-permute-start.4) | collective-permute-done | bytes 131104 | tf_op jit(solution)/shard_map/ppermute | solution.py:144
  26.7 1.4 %collective-permute-done.6.refs_7_ = bf16[64,1024]{1,0:T(8,128)(2,1)S(1)} collective-permute-done((bf16[64,1024]{1,0:T(8,128)(2,1)S(1)}, bf16[64,1024]{1,0:T(8,128)(2,1)S(1)}, u32[]{:S(2)}, u32[]{:S(2)}) %collective-permute-start.6) | collective-permute-done | bytes 131104 | tf_op jit(solution)/shard_map/ppermute | solution.py:144
  28.2 1.0 shard_map.65.x_ref.refs_0_
  29.2 2.4 %collective-permute-start.9 = (bf16[192,1024]{1,0:T(8,128)(2,1)S(1)}, bf16[192,1024]{1,0:T(8,128)(2,1)S(1)}, u32[]{:S(2)}, u32[]{:S(2)}) collective-permute-start(bf16[192,1024]{1,0:T(8,128)(2,1)S(1)} %shard_map.65.x_ref.refs_0_), channel_id=1, source_target_pairs={{0,16},{8,24},{16,0},{24,8},{1,17},{9,25},{17,1},{25,9},{2,18},{10... | collective-permute-start | bytes 1179656 | tf_op jit(solution)/shard_map/ppermute | solution.py:145
  31.7 1.3 %collective-permute-start.17 = (bf16[64,1024]{1,0:T(8,128)(2,1)S(1)}, bf16[64,1024]{1,0:T(8,128)(2,1)S(1)}, u32[]{:S(2)}, u32[]{:S(2)}) collective-permute-start(bf16[64,1024]{1,0:T(8,128)(2,1)S(1)} %get-tuple-element.26.refs_0_), channel_id=1, source_target_pairs={{0,1},{1,0},{2,3},{3,2},{4,5},{5,4},{6,7},{7,6},{8,9},{9,8},{10,11... | collective-permute-start | bytes 393224 | tf_op jit(solution)/shard_map/ppermute | solution.py:144
  32.9 0.7 collective-permute-start.21
  33.7 1.3 %collective-permute-start.19 = (bf16[64,1024]{1,0:T(8,128)(2,1)S(1)}, bf16[64,1024]{1,0:T(8,128)(2,1)S(1)}, u32[]{:S(2)}, u32[]{:S(2)}) collective-permute-start(bf16[64,1024]{1,0:T(8,128)(2,1)S(1)} %collective-permute-done.18.refs_2_), channel_id=1, source_target_pairs={{0,1},{1,0},{2,3},{3,2},{4,5},{5,4},{6,7},{7,6},{8,9},{9,8},{10,11... | collective-permute-start | bytes 393224 | tf_op jit(solution)/shard_map/ppermute | solution.py:144
  35.0 0.7 collective-permute-start.23
  35.7 0.9 collective-permute-done.17.refs_1_
  36.6 1.4 %collective-permute-done.21.refs_5_ = bf16[64,1024]{1,0:T(8,128)(2,1)S(1)} collective-permute-done((bf16[64,1024]{1,0:T(8,128)(2,1)S(1)}, bf16[64,1024]{1,0:T(8,128)(2,1)S(1)}, u32[]{:S(2)}, u32[]{:S(2)}) %collective-permute-start.21) | collective-permute-done | bytes 131104 | tf_op jit(solution)/shard_map/ppermute | solution.py:144
  38.0 1.4 %collective-permute-done.19.refs_3_ = bf16[64,1024]{1,0:T(8,128)(2,1)S(1)} collective-permute-done((bf16[64,1024]{1,0:T(8,128)(2,1)S(1)}, bf16[64,1024]{1,0:T(8,128)(2,1)S(1)}, u32[]{:S(2)}, u32[]{:S(2)}) %collective-permute-start.19) | collective-permute-done | bytes 131104 | tf_op jit(solution)/shard_map/ppermute | solution.py:144
  39.4 1.4 %collective-permute-done.23.refs_7_ = bf16[64,1024]{1,0:T(8,128)(2,1)S(1)} collective-permute-done((bf16[64,1024]{1,0:T(8,128)(2,1)S(1)}, bf16[64,1024]{1,0:T(8,128)(2,1)S(1)}, u32[]{:S(2)}, u32[]{:S(2)}) %collective-permute-start.23) | collective-permute-done | bytes 131104 | tf_op jit(solution)/shard_map/ppermute | solution.py:144
  40.8 1.0 shard_map.73.x_ref.refs_0_
  42.0 0.5 collective-permute-start.7
  42.5 7.2 %collective-permute-done.26.refs_0_ = bf16[192,1024]{1,0:T(8,128)(2,1)S(1)} collective-permute-done((bf16[192,1024]{1,0:T(8,128)(2,1)S(1)}, bf16[192,1024]{1,0:T(8,128)(2,1)S(1)}, u32[]{:S(2)}, u32[]{:S(2)}) %collective-permute-start.26) | collective-permute-done | bytes 393248 | tf_op jit(solution)/shard_map/ppermute | solution.py:145
  49.7 0.5 collective-permute-start.24
  50.2 1.6 %copy-done.1 = bf16[1,1024,1024]{2,1,0:T(8,128)(2,1)S(1)} copy-done((bf16[1,1024,1024]{2,1,0:T(8,128)(2,1)S(1)}, bf16[1,1024,1024]{2,1,0:T(8,128)(2,1)}, u32[]{:S(2)}) %copy-start.1) | copy-done | bytes 2097176
  51.8 1.2 %shard_map.69 = bf16[192,1024]{1,0:T(8,128)(2,1)S(1)} custom-call(bf16[192,1024]{1,0:T(8,128)(2,1)S(1)} %collective-permute-done.10.refs_0_, bf16[1024,1024]{1,0:T(8,128)(2,1)S(1)} %bitcast.15, bf16[1024,1024]{1,0:T(8,128)(2,1)S(1)} %bitcast.21), custom_call_target="tpu_custom_call" | custom-call | flops 805306368 | bytes 4980736 | tf_op jit(solution)/shard_map/pallas_call | solution.py:35
  53.1 1.2 %shard_map.77 = bf16[192,1024]{1,0:T(8,128)(2,1)S(1)} custom-call(bf16[192,1024]{1,0:T(8,128)(2,1)S(1)} %collective-permute-done.27.refs_0_, bf16[1024,1024]{1,0:T(8,128)(2,1)S(1)} %bitcast.16, bf16[1024,1024]{1,0:T(8,128)(2,1)S(1)} %bitcast.22), custom_call_target="tpu_custom_call" | custom-call | flops 805306368 | bytes 4980736 | tf_op jit(solution)/shard_map/pallas_call | solution.py:35
  54.3 0.6 collective-permute-start.28
  54.9 2.0 %shard_map.67 = (bf16[192,1024]{1,0:T(8,128)(2,1)S(1)}, bf16[192,1024]{1,0:T(8,128)(2,1)S(1)}) custom-call(bf16[192,1024]{1,0:T(8,128)(2,1)S(1)} %shard_map.65.x_ref.refs_0_, bf16[192,1024]{1,0:T(8,128)(2,1)S(1)} %collective-permute-done.7.refs_1_, bf16[1024,1024]{1,0:T(8,128)(2,1)S(1)} %bitcast.17, bf16[1024,1024]{1,0:T(8,128)(2,1)S(1)} %bitcast.23), custom_call_target="tpu_custom_call" | custom-call | flops 1610612736 | bytes 5767168 | tf_op jit(solution)/shard_map/pallas_call | solution.py:35
  56.9 0.4 collective-permute-start.8
  57.3 1.2 %shard_map.68.a_ref = bf16[192,1024]{1,0:T(8,128)(2,1)S(1)} custom-call(bf16[192,1024]{1,0:T(8,128)(2,1)S(1)} %collective-permute-done.9.refs_0_, bf16[1024,1024]{1,0:T(8,128)(2,1)S(1)} %bitcast.18, bf16[1024,1024]{1,0:T(8,128)(2,1)S(1)} %bitcast.24), custom_call_target="tpu_custom_call" | custom-call | flops 805306368 | bytes 4980736 | tf_op jit(solution)/shard_map/pallas_call | solution.py:35
  58.7 2.0 %shard_map.75 = (bf16[192,1024]{1,0:T(8,128)(2,1)S(1)}, bf16[192,1024]{1,0:T(8,128)(2,1)S(1)}) custom-call(bf16[192,1024]{1,0:T(8,128)(2,1)S(1)} %shard_map.73.x_ref.refs_0_, bf16[192,1024]{1,0:T(8,128)(2,1)S(1)} %collective-permute-done.24.refs_1_, bf16[1024,1024]{1,0:T(8,128)(2,1)S(1)} %bitcast.19, bf16[1024,1024]{1,0:T(8,128)(2,1)S(1)} %bitcast.25), custom_call_target="tpu_custom_call" | custom-call | flops 1610612736 | bytes 5767168 | tf_op jit(solution)/shard_map/pallas_call | solution.py:35
  60.7 0.2 collective-permute-start.25
  60.9 1.2 %shard_map.76.a_ref = bf16[192,1024]{1,0:T(8,128)(2,1)S(1)} custom-call(bf16[192,1024]{1,0:T(8,128)(2,1)S(1)} %collective-permute-done.26.refs_0_, bf16[1024,1024]{1,0:T(8,128)(2,1)S(1)} %bitcast.20, bf16[1024,1024]{1,0:T(8,128)(2,1)S(1)} %bitcast.26), custom_call_target="tpu_custom_call" | custom-call | flops 805306368 | bytes 4980736 | tf_op jit(solution)/shard_map/pallas_call | solution.py:35
  62.2 1.9 %collective-permute-start.29 = (bf16[192,1024]{1,0:T(8,128)(2,1)S(1)}, bf16[192,1024]{1,0:T(8,128)(2,1)S(1)}, u32[]{:S(2)}, u32[]{:S(2)}) collective-permute-start(bf16[192,1024]{1,0:T(8,128)(2,1)S(1)} %shard_map.78), channel_id=1, source_target_pairs={{0,16},{8,24},{16,0},{24,8},{1,17},{9,25},{17,1},{25,9},{2,18},{10... | collective-permute-start | bytes 1179656 | tf_op jit(solution)/shard_map/ppermute | solution.py:145
  64.1 0.3 shard_map.66.refs_0_
  64.5 6.2 %collective-permute-done.12.refs_3_ = bf16[192,1024]{1,0:T(8,128)(2,1)S(1)} collective-permute-done((bf16[192,1024]{1,0:T(8,128)(2,1)S(1)}, bf16[192,1024]{1,0:T(8,128)(2,1)S(1)}, u32[]{:S(2)}, u32[]{:S(2)}) %collective-permute-start.12) | collective-permute-done | bytes 393248 | tf_op jit(solution)/shard_map/ppermute | solution.py:145
  70.6 0.2 shard_map.71.refs_0_
  70.8 1.3 %collective-permute-start.13 = (bf16[192,1024]{1,0:T(8,128)(2,1)S(1)}, bf16[192,1024]{1,0:T(8,128)(2,1)S(1)}, u32[]{:S(2)}, u32[]{:S(2)}) collective-permute-start(bf16[192,1024]{1,0:T(8,128)(2,1)S(1)} %shard_map.71.refs_0_), channel_id=1, source_target_pairs={{0,1},{1,0},{2,3},{3,2},{4,5},{5,4},{6,7},{7,6},{8,9},{9,8},{10,11... | collective-permute-start | bytes 1179656 | tf_op jit(solution)/shard_map/ppermute | solution.py:144
  72.2 0.3 shard_map.74.refs_0_
  72.5 5.7 %collective-permute-done.29.refs_3_ = bf16[192,1024]{1,0:T(8,128)(2,1)S(1)} collective-permute-done((bf16[192,1024]{1,0:T(8,128)(2,1)S(1)}, bf16[192,1024]{1,0:T(8,128)(2,1)S(1)}, u32[]{:S(2)}, u32[]{:S(2)}) %collective-permute-start.29) | collective-permute-done | bytes 393248 | tf_op jit(solution)/shard_map/ppermute | solution.py:145
  78.2 0.2 shard_map.79.refs_0_
  78.4 1.3 %collective-permute-start.30 = (bf16[192,1024]{1,0:T(8,128)(2,1)S(1)}, bf16[192,1024]{1,0:T(8,128)(2,1)S(1)}, u32[]{:S(2)}, u32[]{:S(2)}) collective-permute-start(bf16[192,1024]{1,0:T(8,128)(2,1)S(1)} %shard_map.79.refs_0_), channel_id=1, source_target_pairs={{0,1},{1,0},{2,3},{3,2},{4,5},{5,4},{6,7},{7,6},{8,9},{9,8},{10,11... | collective-permute-start | bytes 1179656 | tf_op jit(solution)/shard_map/ppermute | solution.py:144
  79.8 0.2 and_reduce_fusion
  80.2 0.2 collective-permute-done.13.refs_1_
  80.5 0.4 shard_map.72
  80.8 2.2 %collective-permute-start.14 = (bf16[64,1024]{1,0:T(8,128)(2,1)S(1)}, bf16[64,1024]{1,0:T(8,128)(2,1)S(1)}, u32[]{:S(2)}, u32[]{:S(2)}) collective-permute-start(bf16[64,1024]{1,0:T(8,128)(2,1)S(1)} %get-tuple-element.23), channel_id=1, source_target_pairs={{0,6},{1,7},{2,4},{3,5},{4,2},{5,3},{6,0},{7,1},{8,14},{9,15},{10,... | collective-permute-start | bytes 393224 | tf_op jit(solution)/shard_map/ppermute | solution.py:144
  83.0 2.7 %collective-permute-start.15 = (bf16[64,1024]{1,0:T(8,128)(2,1)S(1)}, bf16[64,1024]{1,0:T(8,128)(2,1)S(1)}, u32[]{:S(2)}, u32[]{:S(2)}) collective-permute-start(bf16[64,1024]{1,0:T(8,128)(2,1)S(1)} %get-tuple-element.24), channel_id=1, source_target_pairs={{0,4},{1,5},{2,6},{3,7},{4,0},{5,1},{6,2},{7,3},{8,12},{9,13},{10,... | collective-permute-start | bytes 393224 | tf_op jit(solution)/shard_map/ppermute | solution.py:144
  85.7 3.1 %collective-permute-done.30.refs_1_ = bf16[192,1024]{1,0:T(8,128)(2,1)S(1)} collective-permute-done((bf16[192,1024]{1,0:T(8,128)(2,1)S(1)}, bf16[192,1024]{1,0:T(8,128)(2,1)S(1)}, u32[]{:S(2)}, u32[]{:S(2)}) %collective-permute-start.30) | collective-permute-done | bytes 393248 | tf_op jit(solution)/shard_map/ppermute | solution.py:144
  88.8 0.4 shard_map.80
  89.2 2.1 %collective-permute-start.31 = (bf16[64,1024]{1,0:T(8,128)(2,1)S(1)}, bf16[64,1024]{1,0:T(8,128)(2,1)S(1)}, u32[]{:S(2)}, u32[]{:S(2)}) collective-permute-start(bf16[64,1024]{1,0:T(8,128)(2,1)S(1)} %get-tuple-element.30), channel_id=1, source_target_pairs={{0,6},{1,7},{2,4},{3,5},{4,2},{5,3},{6,0},{7,1},{8,14},{9,15},{10,... | collective-permute-start | bytes 393224 | tf_op jit(solution)/shard_map/ppermute | solution.py:144
  91.3 2.7 %collective-permute-start.32 = (bf16[64,1024]{1,0:T(8,128)(2,1)S(1)}, bf16[64,1024]{1,0:T(8,128)(2,1)S(1)}, u32[]{:S(2)}, u32[]{:S(2)}) collective-permute-start(bf16[64,1024]{1,0:T(8,128)(2,1)S(1)} %get-tuple-element.31), channel_id=1, source_target_pairs={{0,4},{1,5},{2,6},{3,7},{4,0},{5,1},{6,2},{7,3},{8,12},{9,13},{10,... | collective-permute-start | bytes 393224 | tf_op jit(solution)/shard_map/ppermute | solution.py:144
  94.0 4.4 %collective-permute-start.33 = (bf16[64,1024]{1,0:T(8,128)(2,1)S(1)}, bf16[64,1024]{1,0:T(8,128)(2,1)S(1)}, u32[]{:S(2)}, u32[]{:S(2)}) collective-permute-start(bf16[64,1024]{1,0:T(8,128)(2,1)S(1)} %get-tuple-element.32), channel_id=1, source_target_pairs={{0,2},{1,3},{2,0},{3,1},{4,6},{5,7},{6,4},{7,5},{8,10},{9,11},{10,... | collective-permute-start | bytes 393224 | tf_op jit(solution)/shard_map/ppermute | solution.py:144
  98.3 3.5 %collective-permute-done.15 = bf16[64,1024]{1,0:T(8,128)(2,1)S(1)} collective-permute-done((bf16[64,1024]{1,0:T(8,128)(2,1)S(1)}, bf16[64,1024]{1,0:T(8,128)(2,1)S(1)}, u32[]{:S(2)}, u32[]{:S(2)}) %collective-permute-start.15) | collective-permute-done | bytes 131104 | tf_op jit(solution)/shard_map/ppermute | solution.py:144
  101.9 4.7 %collective-permute-done.32 = bf16[64,1024]{1,0:T(8,128)(2,1)S(1)} collective-permute-done((bf16[64,1024]{1,0:T(8,128)(2,1)S(1)}, bf16[64,1024]{1,0:T(8,128)(2,1)S(1)}, u32[]{:S(2)}, u32[]{:S(2)}) %collective-permute-start.32) | collective-permute-done | bytes 131104 | tf_op jit(solution)/shard_map/ppermute | solution.py:144
  106.7 0.7 pad_maximum_fusion
  (54 shorter events, 1.5 us)
Async XLA Ops:
  0.0 50.2 %copy-start = (bf16[1,1024,1024]{2,1,0:T(8,128)(2,1)S(1)}, bf16[1,1024,1024]{2,1,0:T(8,128)(2,1)}, u32[]{:S(2)}) copy-start(bf16[1,1024,1024]{2,1,0:T(8,128)(2,1)} %param.10) | copy-start | bytes 6291460
  0.0 1.1 %copy-start.4 = (bf16[128,1024]{1,0:T(8,128)(2,1)S(1)}, bf16[128,1024]{1,0:T(8,128)(2,1)}, u32[]{:S(2)}) copy-start(bf16[128,1024]{1,0:T(8,128)(2,1)} %refs_0_.1) | copy-start | bytes 786436
  1.4 11.6 %collective-permute-start.1 = (bf16[64,1024]{1,0:T(8,128)(2,1)S(1)}, bf16[64,1024]{1,0:T(8,128)(2,1)S(1)}, u32[]{:S(2)}, u32[]{:S(2)}) collective-permute-start(bf16[64,1024]{1,0:T(8,128)(2,1)S(1)} %get-tuple-element.19.refs_0_), channel_id=1, source_target_pairs={{0,2},{1,3},{2,0},{3,1},{4,6},{5,7},{6,4},{7,5},{8,10},{9,11},{10,... | collective-permute-start | bytes 393224 | tf_op jit(solution)/shard_map/ppermute | solution.py:144
  4.6 15.7 %collective-permute-start.3 = (bf16[64,1024]{1,0:T(8,128)(2,1)S(1)}, bf16[64,1024]{1,0:T(8,128)(2,1)S(1)}, u32[]{:S(2)}, u32[]{:S(2)}) collective-permute-start(bf16[64,1024]{1,0:T(8,128)(2,1)S(1)} %get-tuple-element.19.refs_0_), channel_id=1, source_target_pairs={{0,4},{1,5},{2,6},{3,7},{4,0},{5,1},{6,2},{7,3},{8,12},{9,13},{10,... | collective-permute-start | bytes 393224 | tf_op jit(solution)/shard_map/ppermute | solution.py:144
  7.1 14.6 %collective-permute-start.5 = (bf16[64,1024]{1,0:T(8,128)(2,1)S(1)}, bf16[64,1024]{1,0:T(8,128)(2,1)S(1)}, u32[]{:S(2)}, u32[]{:S(2)}) collective-permute-start(bf16[64,1024]{1,0:T(8,128)(2,1)S(1)} %get-tuple-element.19.refs_0_), channel_id=1, source_target_pairs={{0,6},{1,7},{2,4},{3,5},{4,2},{5,3},{6,0},{7,1},{8,14},{9,15},{10,... | collective-permute-start | bytes 393224 | tf_op jit(solution)/shard_map/ppermute | solution.py:144
  7.1 15.1 %collective-permute-start = (bf16[64,1024]{1,0:T(8,128)(2,1)S(1)}, bf16[64,1024]{1,0:T(8,128)(2,1)S(1)}, u32[]{:S(2)}, u32[]{:S(2)}) collective-permute-start(bf16[64,1024]{1,0:T(8,128)(2,1)S(1)} %get-tuple-element.19.refs_0_), channel_id=1, source_target_pairs={{0,1},{1,0},{2,3},{3,2},{4,5},{5,4},{6,7},{7,6},{8,9},{9,8},{10,11... | collective-permute-start | bytes 393224 | tf_op jit(solution)/shard_map/ppermute | solution.py:144
  8.9 15.6 %collective-permute-start.20 = (bf16[64,1024]{1,0:T(8,128)(2,1)S(1)}, bf16[64,1024]{1,0:T(8,128)(2,1)S(1)}, u32[]{:S(2)}, u32[]{:S(2)}) collective-permute-start(bf16[64,1024]{1,0:T(8,128)(2,1)S(1)} %get-tuple-element.26.refs_0_), channel_id=1, source_target_pairs={{0,4},{1,5},{2,6},{3,7},{4,0},{5,1},{6,2},{7,3},{8,12},{9,13},{10,... | collective-permute-start | bytes 393224 | tf_op jit(solution)/shard_map/ppermute | solution.py:144
  13.1 20.6 %collective-permute-start.18 = (bf16[64,1024]{1,0:T(8,128)(2,1)S(1)}, bf16[64,1024]{1,0:T(8,128)(2,1)S(1)}, u32[]{:S(2)}, u32[]{:S(2)}) collective-permute-start(bf16[64,1024]{1,0:T(8,128)(2,1)S(1)} %get-tuple-element.26.refs_0_), channel_id=1, source_target_pairs={{0,2},{1,3},{2,0},{3,1},{4,6},{5,7},{6,4},{7,5},{8,10},{9,11},{10,... | collective-permute-start | bytes 393224 | tf_op jit(solution)/shard_map/ppermute | solution.py:144
  20.2 5.4 %collective-permute-start.2 = (bf16[64,1024]{1,0:T(8,128)(2,1)S(1)}, bf16[64,1024]{1,0:T(8,128)(2,1)S(1)}, u32[]{:S(2)}, u32[]{:S(2)}) collective-permute-start(bf16[64,1024]{1,0:T(8,128)(2,1)S(1)} %collective-permute-done.1.refs_2_), channel_id=1, source_target_pairs={{0,1},{1,0},{2,3},{3,2},{4,5},{5,4},{6,7},{7,6},{8,9},{9,8},{10,11... | collective-permute-start | bytes 393224 | tf_op jit(solution)/shard_map/ppermute | solution.py:144
  21.8 5.0 %collective-permute-start.4 = (bf16[64,1024]{1,0:T(8,128)(2,1)S(1)}, bf16[64,1024]{1,0:T(8,128)(2,1)S(1)}, u32[]{:S(2)}, u32[]{:S(2)}) collective-permute-start(bf16[64,1024]{1,0:T(8,128)(2,1)S(1)} %collective-permute-done.3.refs_4_), channel_id=1, source_target_pairs={{0,1},{1,0},{2,3},{3,2},{4,5},{5,4},{6,7},{7,6},{8,9},{9,8},{10,11... | collective-permute-start | bytes 393224 | tf_op jit(solution)/shard_map/ppermute | solution.py:144
  22.3 5.9 %collective-permute-start.6 = (bf16[64,1024]{1,0:T(8,128)(2,1)S(1)}, bf16[64,1024]{1,0:T(8,128)(2,1)S(1)}, u32[]{:S(2)}, u32[]{:S(2)}) collective-permute-start(bf16[64,1024]{1,0:T(8,128)(2,1)S(1)} %collective-permute-done.5.refs_6_), channel_id=1, source_target_pairs={{0,1},{1,0},{2,3},{3,2},{4,5},{5,4},{6,7},{7,6},{8,9},{9,8},{10,11... | collective-permute-start | bytes 393224 | tf_op jit(solution)/shard_map/ppermute | solution.py:144
  24.5 10.5 %collective-permute-start.22 = (bf16[64,1024]{1,0:T(8,128)(2,1)S(1)}, bf16[64,1024]{1,0:T(8,128)(2,1)S(1)}, u32[]{:S(2)}, u32[]{:S(2)}) collective-permute-start(bf16[64,1024]{1,0:T(8,128)(2,1)S(1)} %collective-permute-done.20.refs_4_), channel_id=1, source_target_pairs={{0,2},{1,3},{2,0},{3,1},{4,6},{5,7},{6,4},{7,5},{8,10},{9,11},{10,... | collective-permute-start | bytes 393224 | tf_op jit(solution)/shard_map/ppermute | solution.py:144
  29.2 12.8 %collective-permute-start.9 = (bf16[192,1024]{1,0:T(8,128)(2,1)S(1)}, bf16[192,1024]{1,0:T(8,128)(2,1)S(1)}, u32[]{:S(2)}, u32[]{:S(2)}) collective-permute-start(bf16[192,1024]{1,0:T(8,128)(2,1)S(1)} %shard_map.65.x_ref.refs_0_), channel_id=1, source_target_pairs={{0,16},{8,24},{16,0},{24,8},{1,17},{9,25},{17,1},{25,9},{2,18},{10... | collective-permute-start | bytes 1179656 | tf_op jit(solution)/shard_map/ppermute | solution.py:145
  31.7 5.0 %collective-permute-start.17 = (bf16[64,1024]{1,0:T(8,128)(2,1)S(1)}, bf16[64,1024]{1,0:T(8,128)(2,1)S(1)}, u32[]{:S(2)}, u32[]{:S(2)}) collective-permute-start(bf16[64,1024]{1,0:T(8,128)(2,1)S(1)} %get-tuple-element.26.refs_0_), channel_id=1, source_target_pairs={{0,1},{1,0},{2,3},{3,2},{4,5},{5,4},{6,7},{7,6},{8,9},{9,8},{10,11... | collective-permute-start | bytes 393224 | tf_op jit(solution)/shard_map/ppermute | solution.py:144
  32.9 5.1 %collective-permute-start.21 = (bf16[64,1024]{1,0:T(8,128)(2,1)S(1)}, bf16[64,1024]{1,0:T(8,128)(2,1)S(1)}, u32[]{:S(2)}, u32[]{:S(2)}) collective-permute-start(bf16[64,1024]{1,0:T(8,128)(2,1)S(1)} %collective-permute-done.20.refs_4_), channel_id=1, source_target_pairs={{0,1},{1,0},{2,3},{3,2},{4,5},{5,4},{6,7},{7,6},{8,9},{9,8},{10,11... | collective-permute-start | bytes 393224 | tf_op jit(solution)/shard_map/ppermute | solution.py:144
  33.7 5.7 %collective-permute-start.19 = (bf16[64,1024]{1,0:T(8,128)(2,1)S(1)}, bf16[64,1024]{1,0:T(8,128)(2,1)S(1)}, u32[]{:S(2)}, u32[]{:S(2)}) collective-permute-start(bf16[64,1024]{1,0:T(8,128)(2,1)S(1)} %collective-permute-done.18.refs_2_), channel_id=1, source_target_pairs={{0,1},{1,0},{2,3},{3,2},{4,5},{5,4},{6,7},{7,6},{8,9},{9,8},{10,11... | collective-permute-start | bytes 393224 | tf_op jit(solution)/shard_map/ppermute | solution.py:144
  35.0 5.9 %collective-permute-start.23 = (bf16[64,1024]{1,0:T(8,128)(2,1)S(1)}, bf16[64,1024]{1,0:T(8,128)(2,1)S(1)}, u32[]{:S(2)}, u32[]{:S(2)}) collective-permute-start(bf16[64,1024]{1,0:T(8,128)(2,1)S(1)} %collective-permute-done.22.refs_6_), channel_id=1, source_target_pairs={{0,1},{1,0},{2,3},{3,2},{4,5},{5,4},{6,7},{7,6},{8,9},{9,8},{10,11... | collective-permute-start | bytes 393224 | tf_op jit(solution)/shard_map/ppermute | solution.py:144
  41.8 7.8 %collective-permute-start.26 = (bf16[192,1024]{1,0:T(8,128)(2,1)S(1)}, bf16[192,1024]{1,0:T(8,128)(2,1)S(1)}, u32[]{:S(2)}, u32[]{:S(2)}) collective-permute-start(bf16[192,1024]{1,0:T(8,128)(2,1)S(1)} %shard_map.73.x_ref.refs_0_), channel_id=1, source_target_pairs={{0,16},{8,24},{16,0},{24,8},{1,17},{9,25},{17,1},{25,9},{2,18},{10... | collective-permute-start | bytes 1179656 | tf_op jit(solution)/shard_map/ppermute | solution.py:145
  42.0 8.2 %collective-permute-start.10 = (bf16[192,1024]{1,0:T(8,128)(2,1)S(1)}, bf16[192,1024]{1,0:T(8,128)(2,1)S(1)}, u32[]{:S(2)}, u32[]{:S(2)}) collective-permute-start(bf16[192,1024]{1,0:T(8,128)(2,1)S(1)} %collective-permute-done.9.refs_0_), channel_id=1, source_target_pairs={{0,8},{8,0},{16,24},{24,16},{1,9},{9,1},{17,25},{25,17},{2,10},{10... | collective-permute-start | bytes 1179656 | tf_op jit(solution)/shard_map/ppermute | solution.py:145
  42.0 12.9 %collective-permute-start.7 = (bf16[192,1024]{1,0:T(8,128)(2,1)S(1)}, bf16[192,1024]{1,0:T(8,128)(2,1)S(1)}, u32[]{:S(2)}, u32[]{:S(2)}) collective-permute-start(bf16[192,1024]{1,0:T(8,128)(2,1)S(1)} %shard_map.65.x_ref.refs_0_), channel_id=1, source_target_pairs={{0,8},{8,0},{16,24},{24,16},{1,9},{9,1},{17,25},{25,17},{2,10},{10... | collective-permute-start | bytes 1179656 | tf_op jit(solution)/shard_map/ppermute | solution.py:145
  49.7 3.4 %collective-permute-start.27 = (bf16[192,1024]{1,0:T(8,128)(2,1)S(1)}, bf16[192,1024]{1,0:T(8,128)(2,1)S(1)}, u32[]{:S(2)}, u32[]{:S(2)}) collective-permute-start(bf16[192,1024]{1,0:T(8,128)(2,1)S(1)} %collective-permute-done.26.refs_0_), channel_id=1, source_target_pairs={{0,8},{8,0},{16,24},{24,16},{1,9},{9,1},{17,25},{25,17},{2,10},{10... | collective-permute-start | bytes 1179656 | tf_op jit(solution)/shard_map/ppermute | solution.py:145
  49.7 9.0 %collective-permute-start.24 = (bf16[192,1024]{1,0:T(8,128)(2,1)S(1)}, bf16[192,1024]{1,0:T(8,128)(2,1)S(1)}, u32[]{:S(2)}, u32[]{:S(2)}) collective-permute-start(bf16[192,1024]{1,0:T(8,128)(2,1)S(1)} %shard_map.73.x_ref.refs_0_), channel_id=1, source_target_pairs={{0,8},{8,0},{16,24},{24,16},{1,9},{9,1},{17,25},{25,17},{2,10},{10... | collective-permute-start | bytes 1179656 | tf_op jit(solution)/shard_map/ppermute | solution.py:145
  50.2 1.6 %copy-start.1 = (bf16[1,1024,1024]{2,1,0:T(8,128)(2,1)S(1)}, bf16[1,1024,1024]{2,1,0:T(8,128)(2,1)}, u32[]{:S(2)}) copy-start(bf16[1,1024,1024]{2,1,0:T(8,128)(2,1)} %param.11) | copy-start | bytes 6291460
  53.0 5.5 %collective-permute-start.11 = (bf16[192,1024]{1,0:T(8,128)(2,1)S(1)}, bf16[192,1024]{1,0:T(8,128)(2,1)S(1)}, u32[]{:S(2)}, u32[]{:S(2)}) collective-permute-start(bf16[192,1024]{1,0:T(8,128)(2,1)S(1)} %shard_map.69), channel_id=1, source_target_pairs={{0,8},{8,0},{16,24},{24,16},{1,9},{9,1},{17,25},{25,17},{2,10},{10... | collective-permute-start | bytes 1179656 | tf_op jit(solution)/shard_map/ppermute | solution.py:145
  53.1 1.7 %copy-start.2 = (bf16[1,1024,1024]{2,1,0:T(8,128)(2,1)S(1)}, bf16[1,1024,1024]{2,1,0:T(8,128)(2,1)}, u32[]{:S(2)}) copy-start(bf16[1,1024,1024]{2,1,0:T(8,128)(2,1)} %param.11) | copy-start | bytes 6291460
  54.3 7.8 %collective-permute-start.28 = (bf16[192,1024]{1,0:T(8,128)(2,1)S(1)}, bf16[192,1024]{1,0:T(8,128)(2,1)S(1)}, u32[]{:S(2)}, u32[]{:S(2)}) collective-permute-start(bf16[192,1024]{1,0:T(8,128)(2,1)S(1)} %shard_map.77), channel_id=1, source_target_pairs={{0,8},{8,0},{16,24},{24,16},{1,9},{9,1},{17,25},{25,17},{2,10},{10... | collective-permute-start | bytes 1179656 | tf_op jit(solution)/shard_map/ppermute | solution.py:145
  56.9 7.6 %collective-permute-start.8 = (bf16[192,1024]{1,0:T(8,128)(2,1)S(1)}, bf16[192,1024]{1,0:T(8,128)(2,1)S(1)}, u32[]{:S(2)}, u32[]{:S(2)}) collective-permute-start(bf16[192,1024]{1,0:T(8,128)(2,1)S(1)} %get-tuple-element.21), channel_id=1, source_target_pairs={{0,8},{8,0},{16,24},{24,16},{1,9},{9,1},{17,25},{25,17},{2,10},{10... | collective-permute-start | bytes 1179656 | tf_op jit(solution)/shard_map/ppermute | solution.py:145
  58.6 12.1 %collective-permute-start.12 = (bf16[192,1024]{1,0:T(8,128)(2,1)S(1)}, bf16[192,1024]{1,0:T(8,128)(2,1)S(1)}, u32[]{:S(2)}, u32[]{:S(2)}) collective-permute-start(bf16[192,1024]{1,0:T(8,128)(2,1)S(1)} %shard_map.70), channel_id=1, source_target_pairs={{0,16},{8,24},{16,0},{24,8},{1,17},{9,25},{17,1},{25,9},{2,18},{10... | collective-permute-start | bytes 1179656 | tf_op jit(solution)/shard_map/ppermute | solution.py:145
  60.7 3.4 %copy-start.3 = (bf16[1024,48]{0,1:T(8,128)(2,1)S(1)}, bf16[1024,48]{0,1:T(8,128)(2,1)}, u32[]{:S(2)}) copy-start(bf16[1024,48]{0,1:T(8,128)(2,1)} %param.9) | copy-start | bytes 294916
  60.7 11.8 %collective-permute-start.25 = (bf16[192,1024]{1,0:T(8,128)(2,1)S(1)}, bf16[192,1024]{1,0:T(8,128)(2,1)S(1)}, u32[]{:S(2)}, u32[]{:S(2)}) collective-permute-start(bf16[192,1024]{1,0:T(8,128)(2,1)S(1)} %get-tuple-element.28), channel_id=1, source_target_pairs={{0,8},{8,0},{16,24},{24,16},{1,9},{9,1},{17,25},{25,17},{2,10},{10... | collective-permute-start | bytes 1179656 | tf_op jit(solution)/shard_map/ppermute | solution.py:145
  62.2 16.1 %collective-permute-start.29 = (bf16[192,1024]{1,0:T(8,128)(2,1)S(1)}, bf16[192,1024]{1,0:T(8,128)(2,1)S(1)}, u32[]{:S(2)}, u32[]{:S(2)}) collective-permute-start(bf16[192,1024]{1,0:T(8,128)(2,1)S(1)} %shard_map.78), channel_id=1, source_target_pairs={{0,16},{8,24},{16,0},{24,8},{1,17},{9,25},{17,1},{25,9},{2,18},{10... | collective-permute-start | bytes 1179656 | tf_op jit(solution)/shard_map/ppermute | solution.py:145
  70.8 9.6 %collective-permute-start.13 = (bf16[192,1024]{1,0:T(8,128)(2,1)S(1)}, bf16[192,1024]{1,0:T(8,128)(2,1)S(1)}, u32[]{:S(2)}, u32[]{:S(2)}) collective-permute-start(bf16[192,1024]{1,0:T(8,128)(2,1)S(1)} %shard_map.71.refs_0_), channel_id=1, source_target_pairs={{0,1},{1,0},{2,3},{3,2},{4,5},{5,4},{6,7},{7,6},{8,9},{9,8},{10,11... | collective-permute-start | bytes 1179656 | tf_op jit(solution)/shard_map/ppermute | solution.py:144
  78.4 10.4 %collective-permute-start.30 = (bf16[192,1024]{1,0:T(8,128)(2,1)S(1)}, bf16[192,1024]{1,0:T(8,128)(2,1)S(1)}, u32[]{:S(2)}, u32[]{:S(2)}) collective-permute-start(bf16[192,1024]{1,0:T(8,128)(2,1)S(1)} %shard_map.79.refs_0_), channel_id=1, source_target_pairs={{0,1},{1,0},{2,3},{3,2},{4,5},{5,4},{6,7},{7,6},{8,9},{9,8},{10,11... | collective-permute-start | bytes 1179656 | tf_op jit(solution)/shard_map/ppermute | solution.py:144
  80.8 13.1 %collective-permute-start.14 = (bf16[64,1024]{1,0:T(8,128)(2,1)S(1)}, bf16[64,1024]{1,0:T(8,128)(2,1)S(1)}, u32[]{:S(2)}, u32[]{:S(2)}) collective-permute-start(bf16[64,1024]{1,0:T(8,128)(2,1)S(1)} %get-tuple-element.23), channel_id=1, source_target_pairs={{0,6},{1,7},{2,4},{3,5},{4,2},{5,3},{6,0},{7,1},{8,14},{9,15},{10,... | collective-permute-start | bytes 393224 | tf_op jit(solution)/shard_map/ppermute | solution.py:144
  83.0 18.8 %collective-permute-start.15 = (bf16[64,1024]{1,0:T(8,128)(2,1)S(1)}, bf16[64,1024]{1,0:T(8,128)(2,1)S(1)}, u32[]{:S(2)}, u32[]{:S(2)}) collective-permute-start(bf16[64,1024]{1,0:T(8,128)(2,1)S(1)} %get-tuple-element.24), channel_id=1, source_target_pairs={{0,4},{1,5},{2,6},{3,7},{4,0},{5,1},{6,2},{7,3},{8,12},{9,13},{10,... | collective-permute-start | bytes 393224 | tf_op jit(solution)/shard_map/ppermute | solution.py:144
  85.7 16.1 %collective-permute-start.16 = (bf16[64,1024]{1,0:T(8,128)(2,1)S(1)}, bf16[64,1024]{1,0:T(8,128)(2,1)S(1)}, u32[]{:S(2)}, u32[]{:S(2)}) collective-permute-start(bf16[64,1024]{1,0:T(8,128)(2,1)S(1)} %get-tuple-element.25), channel_id=1, source_target_pairs={{0,2},{1,3},{2,0},{3,1},{4,6},{5,7},{6,4},{7,5},{8,10},{9,11},{10,... | collective-permute-start | bytes 393224 | tf_op jit(solution)/shard_map/ppermute | solution.py:144
  89.2 12.7 %collective-permute-start.31 = (bf16[64,1024]{1,0:T(8,128)(2,1)S(1)}, bf16[64,1024]{1,0:T(8,128)(2,1)S(1)}, u32[]{:S(2)}, u32[]{:S(2)}) collective-permute-start(bf16[64,1024]{1,0:T(8,128)(2,1)S(1)} %get-tuple-element.30), channel_id=1, source_target_pairs={{0,6},{1,7},{2,4},{3,5},{4,2},{5,3},{6,0},{7,1},{8,14},{9,15},{10,... | collective-permute-start | bytes 393224 | tf_op jit(solution)/shard_map/ppermute | solution.py:144
  91.3 15.3 %collective-permute-start.32 = (bf16[64,1024]{1,0:T(8,128)(2,1)S(1)}, bf16[64,1024]{1,0:T(8,128)(2,1)S(1)}, u32[]{:S(2)}, u32[]{:S(2)}) collective-permute-start(bf16[64,1024]{1,0:T(8,128)(2,1)S(1)} %get-tuple-element.31), channel_id=1, source_target_pairs={{0,4},{1,5},{2,6},{3,7},{4,0},{5,1},{6,2},{7,3},{8,12},{9,13},{10,... | collective-permute-start | bytes 393224 | tf_op jit(solution)/shard_map/ppermute | solution.py:144
  94.0 12.6 %collective-permute-start.33 = (bf16[64,1024]{1,0:T(8,128)(2,1)S(1)}, bf16[64,1024]{1,0:T(8,128)(2,1)S(1)}, u32[]{:S(2)}, u32[]{:S(2)}) collective-permute-start(bf16[64,1024]{1,0:T(8,128)(2,1)S(1)} %get-tuple-element.32), channel_id=1, source_target_pairs={{0,2},{1,3},{2,0},{3,1},{4,6},{5,7},{6,4},{7,5},{8,10},{9,11},{10,... | collective-permute-start | bytes 393224 | tf_op jit(solution)/shard_map/ppermute | solution.py:144

commit v3 on v2

--- a/solution.py
+++ b/solution.py
@@ -13,7 +13,6 @@
 SPLIT = (4, 4)
 MAJOR = 4
 CORES = 2
-SPLIT_SPARE = 4
 LANES = 128
 DIRECT = (0,)
 
@@ -59,18 +58,6 @@
     out_ref[...] = (value * gate_ref[...][:, :1]).astype(out_ref.dtype)
 
 
-def split_body(n, *refs):
-    start, copies = 0, []
-    for i in range(n):
-        source = refs[0].at[pl.ds(start, refs[1 + i].shape[0]), :]
-        copies.append(pltpu.make_async_copy(source, refs[1 + i], refs[-1].at[i]))
-        start += refs[1 + i].shape[0]
-    for copy in copies:
-        copy.start()
-    for copy in copies:
-        copy.wait()
-
-
 def select_body(capacity, n, source_ref, *refs):
     blocks, out_ref, sems = refs[:n], refs[n], refs[n + 1]
     rows = blocks[0].shape[0]
@@ -183,13 +170,8 @@
             flops=4 * sum(x.size for x in xs) * weight_in.shape[1],
         )
 
-    owns = call(
-        functools.partial(split_body, len(split)),
-        [shape(rows) for rows in split],
-        tokens,
-        flops=1e8, in_specs=[ANY], spare=SPLIT_SPARE * 2**20,
-        scratch=[pltpu.SemaphoreType.DMA((len(split),))],
-    )
+    edges = [sum(split[:i]) for i in range(len(split) + 1)]
+    owns = [tokens[a:b] for a, b in zip(edges, edges[1:])]
     outs = []
     for stream, (own, rows) in enumerate(zip(owns, split)):
         full = shape(capacity * rows)

time: 108 us -> 107 us (level)
    slice x0 -> x1, local copies, waits for them, and re-layouts: none -> 1.13 us  [shards(): owns = [tokens[a:b] for a, b in zip(edges, edges[1:])]]
    unnamed x10 -> x8, local copies, waits for them, and re-layouts: 2.7 us -> 1.61 us
    pallas_call x17 -> x16, Pallas kernels: 12.9 us -> 12.6 us  [call(): pl.pallas_call(body, out_shape=out_shapes, in_specs=in_specs or [VMEM] *...]
where the time goes in v3:
time: 107 us
  starting transfers between devices  44 us (41%)
  waiting for transfers between devices  43.5 us (41%)
  Pallas kernels  12.6 us (12%)
  other arithmetic  3.72 us (3%)
  local copies, waits for them, and re-layouts  3.09 us (3%)
    ppermute x22, starting transfers between devices, shards(): move = lambda x, mask: lax.ppermute(x, 'expert', xor_pairs(n_experts, mask))  37.1 us
    ppermute x22, waiting for transfers between devices, shards(): move = lambda x, mask: lax.ppermute(x, 'expert', xor_pairs(n_experts, mask))  24.4 us
    ppermute x12, waiting for transfers between devices, shards(): move_dp = lambda x, mask: lax.ppermute(x, 'dp', xor_pairs(n_dp, mask))  19.1 us
    pallas_call x16, Pallas kernels, call(): pl.pallas_call(body, out_shape=out_shapes, in_specs=in_specs or [VMEM] *...  12.6 us
    ppermute x12, starting transfers between devices, shards(): move_dp = lambda x, mask: lax.ppermute(x, 'dp', xor_pairs(n_dp, mask))  6.87 us
  transfers between devices with their start and end apart: 34, of which 15 were waited for; matrix products, arithmetic and copies ran while one was open for 3% of the time, Pallas kernels for 12%

profile of v3, /device:TPU:0, one launch (start us, length us, event | category | flops | bytes accessed | tf_op | source)
XLA Modules:
  0.0 107.1 jit_solution(12838379096446771843)
XLA Ops:
  0.0 1.1 %fusion.1 = (bf16[64,1024]{1,0:T(8,128)(2,1)S(1)}, bf16[64,1024]{1,0:T(8,128)(2,1)S(1)}) fusion(bf16[128,1024]{1,0:T(8,128)(2,1)} %param.6), kind=kLoop, calls=%fused_computation.24 | loop fusion | bytes 524288 | tf_op jit(solution)/shard_map/slice | solution.py:174
  1.1 3.1 %collective-permute-start.1 = (bf16[64,1024]{1,0:T(8,128)(2,1)S(1)}, bf16[64,1024]{1,0:T(8,128)(2,1)S(1)}, u32[]{:S(2)}, u32[]{:S(2)}) collective-permute-start(bf16[64,1024]{1,0:T(8,128)(2,1)S(1)} %get-tuple-element.32.refs_0_), channel_id=1, source_target_pairs={{0,2},{1,3},{2,0},{3,1},{4,6},{5,7},{6,4},{7,5},{8,10},{9,11},{10,... | collective-permute-start | bytes 393224 | tf_op jit(solution)/shard_map/ppermute | solution.py:131
  4.3 2.6 %collective-permute-start.3 = (bf16[64,1024]{1,0:T(8,128)(2,1)S(1)}, bf16[64,1024]{1,0:T(8,128)(2,1)S(1)}, u32[]{:S(2)}, u32[]{:S(2)}) collective-permute-start(bf16[64,1024]{1,0:T(8,128)(2,1)S(1)} %get-tuple-element.32.refs_0_), channel_id=1, source_target_pairs={{0,4},{1,5},{2,6},{3,7},{4,0},{5,1},{6,2},{7,3},{8,12},{9,13},{10,... | collective-permute-start | bytes 393224 | tf_op jit(solution)/shard_map/ppermute | solution.py:131
  6.9 1.7 %collective-permute-start = (bf16[64,1024]{1,0:T(8,128)(2,1)S(1)}, bf16[64,1024]{1,0:T(8,128)(2,1)S(1)}, u32[]{:S(2)}, u32[]{:S(2)}) collective-permute-start(bf16[64,1024]{1,0:T(8,128)(2,1)S(1)} %get-tuple-element.32.refs_0_), channel_id=1, source_target_pairs={{0,1},{1,0},{2,3},{3,2},{4,5},{5,4},{6,7},{7,6},{8,9},{9,8},{10,11... | collective-permute-start | bytes 393224 | tf_op jit(solution)/shard_map/ppermute | solution.py:131
  8.6 1.7 %collective-permute-start.20 = (bf16[64,1024]{1,0:T(8,128)(2,1)S(1)}, bf16[64,1024]{1,0:T(8,128)(2,1)S(1)}, u32[]{:S(2)}, u32[]{:S(2)}) collective-permute-start(bf16[64,1024]{1,0:T(8,128)(2,1)S(1)} %get-tuple-element.33.refs_0_), channel_id=1, source_target_pairs={{0,4},{1,5},{2,6},{3,7},{4,0},{5,1},{6,2},{7,3},{8,12},{9,13},{10,... | collective-permute-start | bytes 393224 | tf_op jit(solution)/shard_map/ppermute | solution.py:131
  10.3 0.8 compare_reduce_fusion
  11.2 0.8 compare_select_fusion
  12.0 0.8 select_reduce_fusion
  12.8 2.5 %collective-permute-start.18 = (bf16[64,1024]{1,0:T(8,128)(2,1)S(1)}, bf16[64,1024]{1,0:T(8,128)(2,1)S(1)}, u32[]{:S(2)}, u32[]{:S(2)}) collective-permute-start(bf16[64,1024]{1,0:T(8,128)(2,1)S(1)} %get-tuple-element.33.refs_0_), channel_id=1, source_target_pairs={{0,2},{1,3},{2,0},{3,1},{4,6},{5,7},{6,4},{7,5},{8,10},{9,11},{10,... | collective-permute-start | bytes 393224 | tf_op jit(solution)/shard_map/ppermute | solution.py:131
  15.3 4.6 %collective-permute-done.3.refs_4_ = bf16[64,1024]{1,0:T(8,128)(2,1)S(1)} collective-permute-done((bf16[64,1024]{1,0:T(8,128)(2,1)S(1)}, bf16[64,1024]{1,0:T(8,128)(2,1)S(1)}, u32[]{:S(2)}, u32[]{:S(2)}) %collective-permute-start.3) | collective-permute-done | bytes 131104 | tf_op jit(solution)/shard_map/ppermute | solution.py:131
  20.0 1.5 %collective-permute-start.2 = (bf16[64,1024]{1,0:T(8,128)(2,1)S(1)}, bf16[64,1024]{1,0:T(8,128)(2,1)S(1)}, u32[]{:S(2)}, u32[]{:S(2)}) collective-permute-start(bf16[64,1024]{1,0:T(8,128)(2,1)S(1)} %collective-permute-done.1.refs_2_), channel_id=1, source_target_pairs={{0,1},{1,0},{2,3},{3,2},{4,5},{5,4},{6,7},{7,6},{8,9},{9,8},{10,11... | collective-permute-start | bytes 393224 | tf_op jit(solution)/shard_map/ppermute | solution.py:131
  21.5 0.5 collective-permute-start.4
  22.0 1.5 %collective-permute-start.6 = (bf16[64,1024]{1,0:T(8,128)(2,1)S(1)}, bf16[64,1024]{1,0:T(8,128)(2,1)S(1)}, u32[]{:S(2)}, u32[]{:S(2)}) collective-permute-start(bf16[64,1024]{1,0:T(8,128)(2,1)S(1)} %collective-permute-done.5.refs_6_), channel_id=1, source_target_pairs={{0,1},{1,0},{2,3},{3,2},{4,5},{5,4},{6,7},{7,6},{8,9},{9,8},{10,11... | collective-permute-start | bytes 393224 | tf_op jit(solution)/shard_map/ppermute | solution.py:131
  23.5 0.7 collective-permute-done.20.refs_4_
  24.2 1.2 %collective-permute-start.22 = (bf16[64,1024]{1,0:T(8,128)(2,1)S(1)}, bf16[64,1024]{1,0:T(8,128)(2,1)S(1)}, u32[]{:S(2)}, u32[]{:S(2)}) collective-permute-start(bf16[64,1024]{1,0:T(8,128)(2,1)S(1)} %collective-permute-done.20.refs_4_), channel_id=1, source_target_pairs={{0,2},{1,3},{2,0},{3,1},{4,6},{5,7},{6,4},{7,5},{8,10},{9,11},{10,... | collective-permute-start | bytes 393224 | tf_op jit(solution)/shard_map/ppermute | solution.py:131
  25.4 1.1 %collective-permute-done.4.refs_5_ = bf16[64,1024]{1,0:T(8,128)(2,1)S(1)} collective-permute-done((bf16[64,1024]{1,0:T(8,128)(2,1)S(1)}, bf16[64,1024]{1,0:T(8,128)(2,1)S(1)}, u32[]{:S(2)}, u32[]{:S(2)}) %collective-permute-start.4) | collective-permute-done | bytes 131104 | tf_op jit(solution)/shard_map/ppermute | solution.py:131
  26.4 1.4 %collective-permute-done.6.refs_7_ = bf16[64,1024]{1,0:T(8,128)(2,1)S(1)} collective-permute-done((bf16[64,1024]{1,0:T(8,128)(2,1)S(1)}, bf16[64,1024]{1,0:T(8,128)(2,1)S(1)}, u32[]{:S(2)}, u32[]{:S(2)}) %collective-permute-start.6) | collective-permute-done | bytes 131104 | tf_op jit(solution)/shard_map/ppermute | solution.py:131
  27.9 1.0 shard_map.64.x_ref.refs_0_
  28.9 2.4 %collective-permute-start.9 = (bf16[192,1024]{1,0:T(8,128)(2,1)S(1)}, bf16[192,1024]{1,0:T(8,128)(2,1)S(1)}, u32[]{:S(2)}, u32[]{:S(2)}) collective-permute-start(bf16[192,1024]{1,0:T(8,128)(2,1)S(1)} %shard_map.64.x_ref.refs_0_), channel_id=1, source_target_pairs={{0,16},{8,24},{16,0},{24,8},{1,17},{9,25},{17,1},{25,9},{2,18},{10... | collective-permute-start | bytes 1179656 | tf_op jit(solution)/shard_map/ppermute | solution.py:132
  31.4 1.3 %collective-permute-start.17 = (bf16[64,1024]{1,0:T(8,128)(2,1)S(1)}, bf16[64,1024]{1,0:T(8,128)(2,1)S(1)}, u32[]{:S(2)}, u32[]{:S(2)}) collective-permute-start(bf16[64,1024]{1,0:T(8,128)(2,1)S(1)} %get-tuple-element.33.refs_0_), channel_id=1, source_target_pairs={{0,1},{1,0},{2,3},{3,2},{4,5},{5,4},{6,7},{7,6},{8,9},{9,8},{10,11... | collective-permute-start | bytes 393224 | tf_op jit(solution)/shard_map/ppermute | solution.py:131
  32.6 0.7 collective-permute-start.21
  33.4 1.3 %collective-permute-start.19 = (bf16[64,1024]{1,0:T(8,128)(2,1)S(1)}, bf16[64,1024]{1,0:T(8,128)(2,1)S(1)}, u32[]{:S(2)}, u32[]{:S(2)}) collective-permute-start(bf16[64,1024]{1,0:T(8,128)(2,1)S(1)} %collective-permute-done.18.refs_2_), channel_id=1, source_target_pairs={{0,1},{1,0},{2,3},{3,2},{4,5},{5,4},{6,7},{7,6},{8,9},{9,8},{10,11... | collective-permute-start | bytes 393224 | tf_op jit(solution)/shard_map/ppermute | solution.py:131
  34.7 0.7 collective-permute-start.23
  35.4 0.9 collective-permute-done.17.refs_1_
  36.3 1.4 %collective-permute-done.21.refs_5_ = bf16[64,1024]{1,0:T(8,128)(2,1)S(1)} collective-permute-done((bf16[64,1024]{1,0:T(8,128)(2,1)S(1)}, bf16[64,1024]{1,0:T(8,128)(2,1)S(1)}, u32[]{:S(2)}, u32[]{:S(2)}) %collective-permute-start.21) | collective-permute-done | bytes 131104 | tf_op jit(solution)/shard_map/ppermute | solution.py:131
  37.7 1.4 %collective-permute-done.19.refs_3_ = bf16[64,1024]{1,0:T(8,128)(2,1)S(1)} collective-permute-done((bf16[64,1024]{1,0:T(8,128)(2,1)S(1)}, bf16[64,1024]{1,0:T(8,128)(2,1)S(1)}, u32[]{:S(2)}, u32[]{:S(2)}) %collective-permute-start.19) | collective-permute-done | bytes 131104 | tf_op jit(solution)/shard_map/ppermute | solution.py:131
  39.1 1.4 %collective-permute-done.23.refs_7_ = bf16[64,1024]{1,0:T(8,128)(2,1)S(1)} collective-permute-done((bf16[64,1024]{1,0:T(8,128)(2,1)S(1)}, bf16[64,1024]{1,0:T(8,128)(2,1)S(1)}, u32[]{:S(2)}, u32[]{:S(2)}) %collective-permute-start.23) | collective-permute-done | bytes 131104 | tf_op jit(solution)/shard_map/ppermute | solution.py:131
  40.5 1.0 shard_map.72.x_ref.refs_0_
  41.7 0.5 collective-permute-start.7
  42.2 7.2 %collective-permute-done.26.refs_0_ = bf16[192,1024]{1,0:T(8,128)(2,1)S(1)} collective-permute-done((bf16[192,1024]{1,0:T(8,128)(2,1)S(1)}, bf16[192,1024]{1,0:T(8,128)(2,1)S(1)}, u32[]{:S(2)}, u32[]{:S(2)}) %collective-permute-start.26) | collective-permute-done | bytes 393248 | tf_op jit(solution)/shard_map/ppermute | solution.py:132
  49.4 0.5 collective-permute-start.24
  49.9 1.6 %copy-done.1 = bf16[1,1024,1024]{2,1,0:T(8,128)(2,1)S(1)} copy-done((bf16[1,1024,1024]{2,1,0:T(8,128)(2,1)S(1)}, bf16[1,1024,1024]{2,1,0:T(8,128)(2,1)}, u32[]{:S(2)}) %copy-start.1) | copy-done | bytes 2097176
  51.5 1.2 %shard_map.68 = bf16[192,1024]{1,0:T(8,128)(2,1)S(1)} custom-call(bf16[192,1024]{1,0:T(8,128)(2,1)S(1)} %collective-permute-done.10.refs_0_, bf16[1024,1024]{1,0:T(8,128)(2,1)S(1)} %bitcast.15, bf16[1024,1024]{1,0:T(8,128)(2,1)S(1)} %bitcast.21), custom_call_target="tpu_custom_call" | custom-call | flops 805306368 | bytes 4980736 | tf_op jit(solution)/shard_map/pallas_call | solution.py:34
  52.8 1.2 %shard_map.76 = bf16[192,1024]{1,0:T(8,128)(2,1)S(1)} custom-call(bf16[192,1024]{1,0:T(8,128)(2,1)S(1)} %collective-permute-done.27.refs_0_, bf16[1024,1024]{1,0:T(8,128)(2,1)S(1)} %bitcast.16, bf16[1024,1024]{1,0:T(8,128)(2,1)S(1)} %bitcast.22), custom_call_target="tpu_custom_call" | custom-call | flops 805306368 | bytes 4980736 | tf_op jit(solution)/shard_map/pallas_call | solution.py:34
  54.0 0.6 collective-permute-start.28
  54.6 2.0 %shard_map.66 = (bf16[192,1024]{1,0:T(8,128)(2,1)S(1)}, bf16[192,1024]{1,0:T(8,128)(2,1)S(1)}) custom-call(bf16[192,1024]{1,0:T(8,128)(2,1)S(1)} %shard_map.64.x_ref.refs_0_, bf16[192,1024]{1,0:T(8,128)(2,1)S(1)} %collective-permute-done.7.refs_1_, bf16[1024,1024]{1,0:T(8,128)(2,1)S(1)} %bitcast.17, bf16[1024,1024]{1,0:T(8,128)(2,1)S(1)} %bitcast.23), custom_call_target="tpu_custom_call" | custom-call | flops 1610612736 | bytes 5767168 | tf_op jit(solution)/shard_map/pallas_call | solution.py:34
  56.6 0.4 collective-permute-start.8
  57.0 1.2 %shard_map.67.a_ref = bf16[192,1024]{1,0:T(8,128)(2,1)S(1)} custom-call(bf16[192,1024]{1,0:T(8,128)(2,1)S(1)} %collective-permute-done.9.refs_0_, bf16[1024,1024]{1,0:T(8,128)(2,1)S(1)} %bitcast.18, bf16[1024,1024]{1,0:T(8,128)(2,1)S(1)} %bitcast.24), custom_call_target="tpu_custom_call" | custom-call | flops 805306368 | bytes 4980736 | tf_op jit(solution)/shard_map/pallas_call | solution.py:34
  58.3 0.1 collective-permute-start.12
  58.4 2.0 %shard_map.74 = (bf16[192,1024]{1,0:T(8,128)(2,1)S(1)}, bf16[192,1024]{1,0:T(8,128)(2,1)S(1)}) custom-call(bf16[192,1024]{1,0:T(8,128)(2,1)S(1)} %shard_map.72.x_ref.refs_0_, bf16[192,1024]{1,0:T(8,128)(2,1)S(1)} %collective-permute-done.24.refs_1_, bf16[1024,1024]{1,0:T(8,128)(2,1)S(1)} %bitcast.19, bf16[1024,1024]{1,0:T(8,128)(2,1)S(1)} %bitcast.25), custom_call_target="tpu_custom_call" | custom-call | flops 1610612736 | bytes 5767168 | tf_op jit(solution)/shard_map/pallas_call | solution.py:34
  60.4 0.2 collective-permute-start.25
  60.6 1.2 %shard_map.75.a_ref = bf16[192,1024]{1,0:T(8,128)(2,1)S(1)} custom-call(bf16[192,1024]{1,0:T(8,128)(2,1)S(1)} %collective-permute-done.26.refs_0_, bf16[1024,1024]{1,0:T(8,128)(2,1)S(1)} %bitcast.20, bf16[1024,1024]{1,0:T(8,128)(2,1)S(1)} %bitcast.26), custom_call_target="tpu_custom_call" | custom-call | flops 805306368 | bytes 4980736 | tf_op jit(solution)/shard_map/pallas_call | solution.py:34
  61.9 1.9 %collective-permute-start.29 = (bf16[192,1024]{1,0:T(8,128)(2,1)S(1)}, bf16[192,1024]{1,0:T(8,128)(2,1)S(1)}, u32[]{:S(2)}, u32[]{:S(2)}) collective-permute-start(bf16[192,1024]{1,0:T(8,128)(2,1)S(1)} %shard_map.77), channel_id=1, source_target_pairs={{0,16},{8,24},{16,0},{24,8},{1,17},{9,25},{17,1},{25,9},{2,18},{10... | collective-permute-start | bytes 1179656 | tf_op jit(solution)/shard_map/ppermute | solution.py:132
  63.8 0.3 shard_map.65.refs_0_
  64.1 6.2 %collective-permute-done.12.refs_3_ = bf16[192,1024]{1,0:T(8,128)(2,1)S(1)} collective-permute-done((bf16[192,1024]{1,0:T(8,128)(2,1)S(1)}, bf16[192,1024]{1,0:T(8,128)(2,1)S(1)}, u32[]{:S(2)}, u32[]{:S(2)}) %collective-permute-start.12) | collective-permute-done | bytes 393248 | tf_op jit(solution)/shard_map/ppermute | solution.py:132
  70.3 0.2 shard_map.70.refs_0_
  70.5 1.3 %collective-permute-start.13 = (bf16[192,1024]{1,0:T(8,128)(2,1)S(1)}, bf16[192,1024]{1,0:T(8,128)(2,1)S(1)}, u32[]{:S(2)}, u32[]{:S(2)}) collective-permute-start(bf16[192,1024]{1,0:T(8,128)(2,1)S(1)} %shard_map.70.refs_0_), channel_id=1, source_target_pairs={{0,1},{1,0},{2,3},{3,2},{4,5},{5,4},{6,7},{7,6},{8,9},{9,8},{10,11... | collective-permute-start | bytes 1179656 | tf_op jit(solution)/shard_map/ppermute | solution.py:131
  71.9 0.3 shard_map.73.refs_0_
  72.3 5.7 %collective-permute-done.29.refs_3_ = bf16[192,1024]{1,0:T(8,128)(2,1)S(1)} collective-permute-done((bf16[192,1024]{1,0:T(8,128)(2,1)S(1)}, bf16[192,1024]{1,0:T(8,128)(2,1)S(1)}, u32[]{:S(2)}, u32[]{:S(2)}) %collective-permute-start.29) | collective-permute-done | bytes 393248 | tf_op jit(solution)/shard_map/ppermute | solution.py:132
  78.0 0.2 shard_map.78.refs_0_
  78.1 1.3 %collective-permute-start.30 = (bf16[192,1024]{1,0:T(8,128)(2,1)S(1)}, bf16[192,1024]{1,0:T(8,128)(2,1)S(1)}, u32[]{:S(2)}, u32[]{:S(2)}) collective-permute-start(bf16[192,1024]{1,0:T(8,128)(2,1)S(1)} %shard_map.78.refs_0_), channel_id=1, source_target_pairs={{0,1},{1,0},{2,3},{3,2},{4,5},{5,4},{6,7},{7,6},{8,9},{9,8},{10,11... | collective-permute-start | bytes 1179656 | tf_op jit(solution)/shard_map/ppermute | solution.py:131
  79.5 0.2 and_reduce_fusion
  79.9 0.2 collective-permute-done.13.refs_1_
  80.2 0.4 shard_map.71
  80.6 2.2 %collective-permute-start.14 = (bf16[64,1024]{1,0:T(8,128)(2,1)S(1)}, bf16[64,1024]{1,0:T(8,128)(2,1)S(1)}, u32[]{:S(2)}, u32[]{:S(2)}) collective-permute-start(bf16[64,1024]{1,0:T(8,128)(2,1)S(1)} %get-tuple-element.20), channel_id=1, source_target_pairs={{0,6},{1,7},{2,4},{3,5},{4,2},{5,3},{6,0},{7,1},{8,14},{9,15},{10,... | collective-permute-start | bytes 393224 | tf_op jit(solution)/shard_map/ppermute | solution.py:131
  82.7 2.7 %collective-permute-start.15 = (bf16[64,1024]{1,0:T(8,128)(2,1)S(1)}, bf16[64,1024]{1,0:T(8,128)(2,1)S(1)}, u32[]{:S(2)}, u32[]{:S(2)}) collective-permute-start(bf16[64,1024]{1,0:T(8,128)(2,1)S(1)} %get-tuple-element.21), channel_id=1, source_target_pairs={{0,4},{1,5},{2,6},{3,7},{4,0},{5,1},{6,2},{7,3},{8,12},{9,13},{10,... | collective-permute-start | bytes 393224 | tf_op jit(solution)/shard_map/ppermute | solution.py:131
  85.4 3.1 %collective-permute-done.30.refs_1_ = bf16[192,1024]{1,0:T(8,128)(2,1)S(1)} collective-permute-done((bf16[192,1024]{1,0:T(8,128)(2,1)S(1)}, bf16[192,1024]{1,0:T(8,128)(2,1)S(1)}, u32[]{:S(2)}, u32[]{:S(2)}) %collective-permute-start.30) | collective-permute-done | bytes 393248 | tf_op jit(solution)/shard_map/ppermute | solution.py:131
  88.5 0.4 shard_map.79
  88.9 2.1 %collective-permute-start.31 = (bf16[64,1024]{1,0:T(8,128)(2,1)S(1)}, bf16[64,1024]{1,0:T(8,128)(2,1)S(1)}, u32[]{:S(2)}, u32[]{:S(2)}) collective-permute-start(bf16[64,1024]{1,0:T(8,128)(2,1)S(1)} %get-tuple-element.26), channel_id=1, source_target_pairs={{0,6},{1,7},{2,4},{3,5},{4,2},{5,3},{6,0},{7,1},{8,14},{9,15},{10,... | collective-permute-start | bytes 393224 | tf_op jit(solution)/shard_map/ppermute | solution.py:131
  91.0 2.7 %collective-permute-start.32 = (bf16[64,1024]{1,0:T(8,128)(2,1)S(1)}, bf16[64,1024]{1,0:T(8,128)(2,1)S(1)}, u32[]{:S(2)}, u32[]{:S(2)}) collective-permute-start(bf16[64,1024]{1,0:T(8,128)(2,1)S(1)} %get-tuple-element.27), channel_id=1, source_target_pairs={{0,4},{1,5},{2,6},{3,7},{4,0},{5,1},{6,2},{7,3},{8,12},{9,13},{10,... | collective-permute-start | bytes 393224 | tf_op jit(solution)/shard_map/ppermute | solution.py:131
  93.7 4.4 %collective-permute-start.33 = (bf16[64,1024]{1,0:T(8,128)(2,1)S(1)}, bf16[64,1024]{1,0:T(8,128)(2,1)S(1)}, u32[]{:S(2)}, u32[]{:S(2)}) collective-permute-start(bf16[64,1024]{1,0:T(8,128)(2,1)S(1)} %get-tuple-element.28), channel_id=1, source_target_pairs={{0,2},{1,3},{2,0},{3,1},{4,6},{5,7},{6,4},{7,5},{8,10},{9,11},{10,... | collective-permute-start | bytes 393224 | tf_op jit(solution)/shard_map/ppermute | solution.py:131
  98.1 3.5 %collective-permute-done.15 = bf16[64,1024]{1,0:T(8,128)(2,1)S(1)} collective-permute-done((bf16[64,1024]{1,0:T(8,128)(2,1)S(1)}, bf16[64,1024]{1,0:T(8,128)(2,1)S(1)}, u32[]{:S(2)}, u32[]{:S(2)}) %collective-permute-start.15) | collective-permute-done | bytes 131104 | tf_op jit(solution)/shard_map/ppermute | solution.py:131
  101.6 4.7 %collective-permute-done.32 = bf16[64,1024]{1,0:T(8,128)(2,1)S(1)} collective-permute-done((bf16[64,1024]{1,0:T(8,128)(2,1)S(1)}, bf16[64,1024]{1,0:T(8,128)(2,1)S(1)}, u32[]{:S(2)}, u32[]{:S(2)}) %collective-permute-start.32) | collective-permute-done | bytes 131104 | tf_op jit(solution)/shard_map/ppermute | solution.py:131
  106.4 0.7 pad_maximum_fusion
  (52 shorter events, 1.3 us)
Async XLA Ops:
  0.0 49.9 %copy-start = (bf16[1,1024,1024]{2,1,0:T(8,128)(2,1)S(1)}, bf16[1,1024,1024]{2,1,0:T(8,128)(2,1)}, u32[]{:S(2)}) copy-start(bf16[1,1024,1024]{2,1,0:T(8,128)(2,1)} %param.10) | copy-start | bytes 6291460
  1.1 11.6 %collective-permute-start.1 = (bf16[64,1024]{1,0:T(8,128)(2,1)S(1)}, bf16[64,1024]{1,0:T(8,128)(2,1)S(1)}, u32[]{:S(2)}, u32[]{:S(2)}) collective-permute-start(bf16[64,1024]{1,0:T(8,128)(2,1)S(1)} %get-tuple-element.32.refs_0_), channel_id=1, source_target_pairs={{0,2},{1,3},{2,0},{3,1},{4,6},{5,7},{6,4},{7,5},{8,10},{9,11},{10,... | collective-permute-start | bytes 393224 | tf_op jit(solution)/shard_map/ppermute | solution.py:131
  4.3 15.7 %collective-permute-start.3 = (bf16[64,1024]{1,0:T(8,128)(2,1)S(1)}, bf16[64,1024]{1,0:T(8,128)(2,1)S(1)}, u32[]{:S(2)}, u32[]{:S(2)}) collective-permute-start(bf16[64,1024]{1,0:T(8,128)(2,1)S(1)} %get-tuple-element.32.refs_0_), channel_id=1, source_target_pairs={{0,4},{1,5},{2,6},{3,7},{4,0},{5,1},{6,2},{7,3},{8,12},{9,13},{10,... | collective-permute-start | bytes 393224 | tf_op jit(solution)/shard_map/ppermute | solution.py:131
  6.8 14.6 %collective-permute-start.5 = (bf16[64,1024]{1,0:T(8,128)(2,1)S(1)}, bf16[64,1024]{1,0:T(8,128)(2,1)S(1)}, u32[]{:S(2)}, u32[]{:S(2)}) collective-permute-start(bf16[64,1024]{1,0:T(8,128)(2,1)S(1)} %get-tuple-element.32.refs_0_), channel_id=1, source_target_pairs={{0,6},{1,7},{2,4},{3,5},{4,2},{5,3},{6,0},{7,1},{8,14},{9,15},{10,... | collective-permute-start | bytes 393224 | tf_op jit(solution)/shard_map/ppermute | solution.py:131
  6.9 15.1 %collective-permute-start = (bf16[64,1024]{1,0:T(8,128)(2,1)S(1)}, bf16[64,1024]{1,0:T(8,128)(2,1)S(1)}, u32[]{:S(2)}, u32[]{:S(2)}) collective-permute-start(bf16[64,1024]{1,0:T(8,128)(2,1)S(1)} %get-tuple-element.32.refs_0_), channel_id=1, source_target_pairs={{0,1},{1,0},{2,3},{3,2},{4,5},{5,4},{6,7},{7,6},{8,9},{9,8},{10,11... | collective-permute-start | bytes 393224 | tf_op jit(solution)/shard_map/ppermute | solution.py:131
  8.6 15.6 %collective-permute-start.20 = (bf16[64,1024]{1,0:T(8,128)(2,1)S(1)}, bf16[64,1024]{1,0:T(8,128)(2,1)S(1)}, u32[]{:S(2)}, u32[]{:S(2)}) collective-permute-start(bf16[64,1024]{1,0:T(8,128)(2,1)S(1)} %get-tuple-element.33.refs_0_), channel_id=1, source_target_pairs={{0,4},{1,5},{2,6},{3,7},{4,0},{5,1},{6,2},{7,3},{8,12},{9,13},{10,... | collective-permute-start | bytes 393224 | tf_op jit(solution)/shard_map/ppermute | solution.py:131
  12.8 20.6 %collective-permute-start.18 = (bf16[64,1024]{1,0:T(8,128)(2,1)S(1)}, bf16[64,1024]{1,0:T(8,128)(2,1)S(1)}, u32[]{:S(2)}, u32[]{:S(2)}) collective-permute-start(bf16[64,1024]{1,0:T(8,128)(2,1)S(1)} %get-tuple-element.33.refs_0_), channel_id=1, source_target_pairs={{0,2},{1,3},{2,0},{3,1},{4,6},{5,7},{6,4},{7,5},{8,10},{9,11},{10,... | collective-permute-start | bytes 393224 | tf_op jit(solution)/shard_map/ppermute | solution.py:131
  20.0 5.4 %collective-permute-start.2 = (bf16[64,1024]{1,0:T(8,128)(2,1)S(1)}, bf16[64,1024]{1,0:T(8,128)(2,1)S(1)}, u32[]{:S(2)}, u32[]{:S(2)}) collective-permute-start(bf16[64,1024]{1,0:T(8,128)(2,1)S(1)} %collective-permute-done.1.refs_2_), channel_id=1, source_target_pairs={{0,1},{1,0},{2,3},{3,2},{4,5},{5,4},{6,7},{7,6},{8,9},{9,8},{10,11... | collective-permute-start | bytes 393224 | tf_op jit(solution)/shard_map/ppermute | solution.py:131
  21.5 5.0 %collective-permute-start.4 = (bf16[64,1024]{1,0:T(8,128)(2,1)S(1)}, bf16[64,1024]{1,0:T(8,128)(2,1)S(1)}, u32[]{:S(2)}, u32[]{:S(2)}) collective-permute-start(bf16[64,1024]{1,0:T(8,128)(2,1)S(1)} %collective-permute-done.3.refs_4_), channel_id=1, source_target_pairs={{0,1},{1,0},{2,3},{3,2},{4,5},{5,4},{6,7},{7,6},{8,9},{9,8},{10,11... | collective-permute-start | bytes 393224 | tf_op jit(solution)/shard_map/ppermute | solution.py:131
  22.0 5.9 %collective-permute-start.6 = (bf16[64,1024]{1,0:T(8,128)(2,1)S(1)}, bf16[64,1024]{1,0:T(8,128)(2,1)S(1)}, u32[]{:S(2)}, u32[]{:S(2)}) collective-permute-start(bf16[64,1024]{1,0:T(8,128)(2,1)S(1)} %collective-permute-done.5.refs_6_), channel_id=1, source_target_pairs={{0,1},{1,0},{2,3},{3,2},{4,5},{5,4},{6,7},{7,6},{8,9},{9,8},{10,11... | collective-permute-start | bytes 393224 | tf_op jit(solution)/shard_map/ppermute | solution.py:131
  24.2 10.5 %collective-permute-start.22 = (bf16[64,1024]{1,0:T(8,128)(2,1)S(1)}, bf16[64,1024]{1,0:T(8,128)(2,1)S(1)}, u32[]{:S(2)}, u32[]{:S(2)}) collective-permute-start(bf16[64,1024]{1,0:T(8,128)(2,1)S(1)} %collective-permute-done.20.refs_4_), channel_id=1, source_target_pairs={{0,2},{1,3},{2,0},{3,1},{4,6},{5,7},{6,4},{7,5},{8,10},{9,11},{10,... | collective-permute-start | bytes 393224 | tf_op jit(solution)/shard_map/ppermute | solution.py:131
  28.9 12.8 %collective-permute-start.9 = (bf16[192,1024]{1,0:T(8,128)(2,1)S(1)}, bf16[192,1024]{1,0:T(8,128)(2,1)S(1)}, u32[]{:S(2)}, u32[]{:S(2)}) collective-permute-start(bf16[192,1024]{1,0:T(8,128)(2,1)S(1)} %shard_map.64.x_ref.refs_0_), channel_id=1, source_target_pairs={{0,16},{8,24},{16,0},{24,8},{1,17},{9,25},{17,1},{25,9},{2,18},{10... | collective-permute-start | bytes 1179656 | tf_op jit(solution)/shard_map/ppermute | solution.py:132
  31.4 5.0 %collective-permute-start.17 = (bf16[64,1024]{1,0:T(8,128)(2,1)S(1)}, bf16[64,1024]{1,0:T(8,128)(2,1)S(1)}, u32[]{:S(2)}, u32[]{:S(2)}) collective-permute-start(bf16[64,1024]{1,0:T(8,128)(2,1)S(1)} %get-tuple-element.33.refs_0_), channel_id=1, source_target_pairs={{0,1},{1,0},{2,3},{3,2},{4,5},{5,4},{6,7},{7,6},{8,9},{9,8},{10,11... | collective-permute-start | bytes 393224 | tf_op jit(solution)/shard_map/ppermute | solution.py:131
  32.6 5.1 %collective-permute-start.21 = (bf16[64,1024]{1,0:T(8,128)(2,1)S(1)}, bf16[64,1024]{1,0:T(8,128)(2,1)S(1)}, u32[]{:S(2)}, u32[]{:S(2)}) collective-permute-start(bf16[64,1024]{1,0:T(8,128)(2,1)S(1)} %collective-permute-done.20.refs_4_), channel_id=1, source_target_pairs={{0,1},{1,0},{2,3},{3,2},{4,5},{5,4},{6,7},{7,6},{8,9},{9,8},{10,11... | collective-permute-start | bytes 393224 | tf_op jit(solution)/shard_map/ppermute | solution.py:131
  33.4 5.7 %collective-permute-start.19 = (bf16[64,1024]{1,0:T(8,128)(2,1)S(1)}, bf16[64,1024]{1,0:T(8,128)(2,1)S(1)}, u32[]{:S(2)}, u32[]{:S(2)}) collective-permute-start(bf16[64,1024]{1,0:T(8,128)(2,1)S(1)} %collective-permute-done.18.refs_2_), channel_id=1, source_target_pairs={{0,1},{1,0},{2,3},{3,2},{4,5},{5,4},{6,7},{7,6},{8,9},{9,8},{10,11... | collective-permute-start | bytes 393224 | tf_op jit(solution)/shard_map/ppermute | solution.py:131
  34.7 5.9 %collective-permute-start.23 = (bf16[64,1024]{1,0:T(8,128)(2,1)S(1)}, bf16[64,1024]{1,0:T(8,128)(2,1)S(1)}, u32[]{:S(2)}, u32[]{:S(2)}) collective-permute-start(bf16[64,1024]{1,0:T(8,128)(2,1)S(1)} %collective-permute-done.22.refs_6_), channel_id=1, source_target_pairs={{0,1},{1,0},{2,3},{3,2},{4,5},{5,4},{6,7},{7,6},{8,9},{9,8},{10,11... | collective-permute-start | bytes 393224 | tf_op jit(solution)/shard_map/ppermute | solution.py:131
  41.5 7.8 %collective-permute-start.26 = (bf16[192,1024]{1,0:T(8,128)(2,1)S(1)}, bf16[192,1024]{1,0:T(8,128)(2,1)S(1)}, u32[]{:S(2)}, u32[]{:S(2)}) collective-permute-start(bf16[192,1024]{1,0:T(8,128)(2,1)S(1)} %shard_map.72.x_ref.refs_0_), channel_id=1, source_target_pairs={{0,16},{8,24},{16,0},{24,8},{1,17},{9,25},{17,1},{25,9},{2,18},{10... | collective-permute-start | bytes 1179656 | tf_op jit(solution)/shard_map/ppermute | solution.py:132
  41.7 8.2 %collective-permute-start.10 = (bf16[192,1024]{1,0:T(8,128)(2,1)S(1)}, bf16[192,1024]{1,0:T(8,128)(2,1)S(1)}, u32[]{:S(2)}, u32[]{:S(2)}) collective-permute-start(bf16[192,1024]{1,0:T(8,128)(2,1)S(1)} %collective-permute-done.9.refs_0_), channel_id=1, source_target_pairs={{0,8},{8,0},{16,24},{24,16},{1,9},{9,1},{17,25},{25,17},{2,10},{10... | collective-permute-start | bytes 1179656 | tf_op jit(solution)/shard_map/ppermute | solution.py:132
  41.7 12.9 %collective-permute-start.7 = (bf16[192,1024]{1,0:T(8,128)(2,1)S(1)}, bf16[192,1024]{1,0:T(8,128)(2,1)S(1)}, u32[]{:S(2)}, u32[]{:S(2)}) collective-permute-start(bf16[192,1024]{1,0:T(8,128)(2,1)S(1)} %shard_map.64.x_ref.refs_0_), channel_id=1, source_target_pairs={{0,8},{8,0},{16,24},{24,16},{1,9},{9,1},{17,25},{25,17},{2,10},{10... | collective-permute-start | bytes 1179656 | tf_op jit(solution)/shard_map/ppermute | solution.py:132
  49.4 3.4 %collective-permute-start.27 = (bf16[192,1024]{1,0:T(8,128)(2,1)S(1)}, bf16[192,1024]{1,0:T(8,128)(2,1)S(1)}, u32[]{:S(2)}, u32[]{:S(2)}) collective-permute-start(bf16[192,1024]{1,0:T(8,128)(2,1)S(1)} %collective-permute-done.26.refs_0_), channel_id=1, source_target_pairs={{0,8},{8,0},{16,24},{24,16},{1,9},{9,1},{17,25},{25,17},{2,10},{10... | collective-permute-start | bytes 1179656 | tf_op jit(solution)/shard_map/ppermute | solution.py:132
  49.4 9.0 %collective-permute-start.24 = (bf16[192,1024]{1,0:T(8,128)(2,1)S(1)}, bf16[192,1024]{1,0:T(8,128)(2,1)S(1)}, u32[]{:S(2)}, u32[]{:S(2)}) collective-permute-start(bf16[192,1024]{1,0:T(8,128)(2,1)S(1)} %shard_map.72.x_ref.refs_0_), channel_id=1, source_target_pairs={{0,8},{8,0},{16,24},{24,16},{1,9},{9,1},{17,25},{25,17},{2,10},{10... | collective-permute-start | bytes 1179656 | tf_op jit(solution)/shard_map/ppermute | solution.py:132
  49.9 1.6 %copy-start.1 = (bf16[1,1024,1024]{2,1,0:T(8,128)(2,1)S(1)}, bf16[1,1024,1024]{2,1,0:T(8,128)(2,1)}, u32[]{:S(2)}) copy-start(bf16[1,1024,1024]{2,1,0:T(8,128)(2,1)} %param.11) | copy-start | bytes 6291460
  52.7 5.5 %collective-permute-start.11 = (bf16[192,1024]{1,0:T(8,128)(2,1)S(1)}, bf16[192,1024]{1,0:T(8,128)(2,1)S(1)}, u32[]{:S(2)}, u32[]{:S(2)}) collective-permute-start(bf16[192,1024]{1,0:T(8,128)(2,1)S(1)} %shard_map.68), channel_id=1, source_target_pairs={{0,8},{8,0},{16,24},{24,16},{1,9},{9,1},{17,25},{25,17},{2,10},{10... | collective-permute-start | bytes 1179656 | tf_op jit(solution)/shard_map/ppermute | solution.py:132
  52.8 1.7 %copy-start.2 = (bf16[1,1024,1024]{2,1,0:T(8,128)(2,1)S(1)}, bf16[1,1024,1024]{2,1,0:T(8,128)(2,1)}, u32[]{:S(2)}) copy-start(bf16[1,1024,1024]{2,1,0:T(8,128)(2,1)} %param.11) | copy-start | bytes 6291460
  54.0 7.8 %collective-permute-start.28 = (bf16[192,1024]{1,0:T(8,128)(2,1)S(1)}, bf16[192,1024]{1,0:T(8,128)(2,1)S(1)}, u32[]{:S(2)}, u32[]{:S(2)}) collective-permute-start(bf16[192,1024]{1,0:T(8,128)(2,1)S(1)} %shard_map.76), channel_id=1, source_target_pairs={{0,8},{8,0},{16,24},{24,16},{1,9},{9,1},{17,25},{25,17},{2,10},{10... | collective-permute-start | bytes 1179656 | tf_op jit(solution)/shard_map/ppermute | solution.py:132
  56.6 7.6 %collective-permute-start.8 = (bf16[192,1024]{1,0:T(8,128)(2,1)S(1)}, bf16[192,1024]{1,0:T(8,128)(2,1)S(1)}, u32[]{:S(2)}, u32[]{:S(2)}) collective-permute-start(bf16[192,1024]{1,0:T(8,128)(2,1)S(1)} %get-tuple-element.18), channel_id=1, source_target_pairs={{0,8},{8,0},{16,24},{24,16},{1,9},{9,1},{17,25},{25,17},{2,10},{10... | collective-permute-start | bytes 1179656 | tf_op jit(solution)/shard_map/ppermute | solution.py:132
  58.3 12.1 %collective-permute-start.12 = (bf16[192,1024]{1,0:T(8,128)(2,1)S(1)}, bf16[192,1024]{1,0:T(8,128)(2,1)S(1)}, u32[]{:S(2)}, u32[]{:S(2)}) collective-permute-start(bf16[192,1024]{1,0:T(8,128)(2,1)S(1)} %shard_map.69), channel_id=1, source_target_pairs={{0,16},{8,24},{16,0},{24,8},{1,17},{9,25},{17,1},{25,9},{2,18},{10... | collective-permute-start | bytes 1179656 | tf_op jit(solution)/shard_map/ppermute | solution.py:132
  60.4 3.4 %copy-start.3 = (bf16[1024,48]{0,1:T(8,128)(2,1)S(1)}, bf16[1024,48]{0,1:T(8,128)(2,1)}, u32[]{:S(2)}) copy-start(bf16[1024,48]{0,1:T(8,128)(2,1)} %param.9) | copy-start | bytes 294916
  60.4 11.8 %collective-permute-start.25 = (bf16[192,1024]{1,0:T(8,128)(2,1)S(1)}, bf16[192,1024]{1,0:T(8,128)(2,1)S(1)}, u32[]{:S(2)}, u32[]{:S(2)}) collective-permute-start(bf16[192,1024]{1,0:T(8,128)(2,1)S(1)} %get-tuple-element.24), channel_id=1, source_target_pairs={{0,8},{8,0},{16,24},{24,16},{1,9},{9,1},{17,25},{25,17},{2,10},{10... | collective-permute-start | bytes 1179656 | tf_op jit(solution)/shard_map/ppermute | solution.py:132
  61.9 16.1 %collective-permute-start.29 = (bf16[192,1024]{1,0:T(8,128)(2,1)S(1)}, bf16[192,1024]{1,0:T(8,128)(2,1)S(1)}, u32[]{:S(2)}, u32[]{:S(2)}) collective-permute-start(bf16[192,1024]{1,0:T(8,128)(2,1)S(1)} %shard_map.77), channel_id=1, source_target_pairs={{0,16},{8,24},{16,0},{24,8},{1,17},{9,25},{17,1},{25,9},{2,18},{10... | collective-permute-start | bytes 1179656 | tf_op jit(solution)/shard_map/ppermute | solution.py:132
  70.5 9.6 %collective-permute-start.13 = (bf16[192,1024]{1,0:T(8,128)(2,1)S(1)}, bf16[192,1024]{1,0:T(8,128)(2,1)S(1)}, u32[]{:S(2)}, u32[]{:S(2)}) collective-permute-start(bf16[192,1024]{1,0:T(8,128)(2,1)S(1)} %shard_map.70.refs_0_), channel_id=1, source_target_pairs={{0,1},{1,0},{2,3},{3,2},{4,5},{5,4},{6,7},{7,6},{8,9},{9,8},{10,11... | collective-permute-start | bytes 1179656 | tf_op jit(solution)/shard_map/ppermute | solution.py:131
  78.1 10.4 %collective-permute-start.30 = (bf16[192,1024]{1,0:T(8,128)(2,1)S(1)}, bf16[192,1024]{1,0:T(8,128)(2,1)S(1)}, u32[]{:S(2)}, u32[]{:S(2)}) collective-permute-start(bf16[192,1024]{1,0:T(8,128)(2,1)S(1)} %shard_map.78.refs_0_), channel_id=1, source_target_pairs={{0,1},{1,0},{2,3},{3,2},{4,5},{5,4},{6,7},{7,6},{8,9},{9,8},{10,11... | collective-permute-start | bytes 1179656 | tf_op jit(solution)/shard_map/ppermute | solution.py:131
  80.6 13.1 %collective-permute-start.14 = (bf16[64,1024]{1,0:T(8,128)(2,1)S(1)}, bf16[64,1024]{1,0:T(8,128)(2,1)S(1)}, u32[]{:S(2)}, u32[]{:S(2)}) collective-permute-start(bf16[64,1024]{1,0:T(8,128)(2,1)S(1)} %get-tuple-element.20), channel_id=1, source_target_pairs={{0,6},{1,7},{2,4},{3,5},{4,2},{5,3},{6,0},{7,1},{8,14},{9,15},{10,... | collective-permute-start | bytes 393224 | tf_op jit(solution)/shard_map/ppermute | solution.py:131
  82.7 18.8 %collective-permute-start.15 = (bf16[64,1024]{1,0:T(8,128)(2,1)S(1)}, bf16[64,1024]{1,0:T(8,128)(2,1)S(1)}, u32[]{:S(2)}, u32[]{:S(2)}) collective-permute-start(bf16[64,1024]{1,0:T(8,128)(2,1)S(1)} %get-tuple-element.21), channel_id=1, source_target_pairs={{0,4},{1,5},{2,6},{3,7},{4,0},{5,1},{6,2},{7,3},{8,12},{9,13},{10,... | collective-permute-start | bytes 393224 | tf_op jit(solution)/shard_map/ppermute | solution.py:131
  85.4 16.1 %collective-permute-start.16 = (bf16[64,1024]{1,0:T(8,128)(2,1)S(1)}, bf16[64,1024]{1,0:T(8,128)(2,1)S(1)}, u32[]{:S(2)}, u32[]{:S(2)}) collective-permute-start(bf16[64,1024]{1,0:T(8,128)(2,1)S(1)} %get-tuple-element.22), channel_id=1, source_target_pairs={{0,2},{1,3},{2,0},{3,1},{4,6},{5,7},{6,4},{7,5},{8,10},{9,11},{10,... | collective-permute-start | bytes 393224 | tf_op jit(solution)/shard_map/ppermute | solution.py:131
  88.9 12.7 %collective-permute-start.31 = (bf16[64,1024]{1,0:T(8,128)(2,1)S(1)}, bf16[64,1024]{1,0:T(8,128)(2,1)S(1)}, u32[]{:S(2)}, u32[]{:S(2)}) collective-permute-start(bf16[64,1024]{1,0:T(8,128)(2,1)S(1)} %get-tuple-element.26), channel_id=1, source_target_pairs={{0,6},{1,7},{2,4},{3,5},{4,2},{5,3},{6,0},{7,1},{8,14},{9,15},{10,... | collective-permute-start | bytes 393224 | tf_op jit(solution)/shard_map/ppermute | solution.py:131
  91.0 15.3 %collective-permute-start.32 = (bf16[64,1024]{1,0:T(8,128)(2,1)S(1)}, bf16[64,1024]{1,0:T(8,128)(2,1)S(1)}, u32[]{:S(2)}, u32[]{:S(2)}) collective-permute-start(bf16[64,1024]{1,0:T(8,128)(2,1)S(1)} %get-tuple-element.27), channel_id=1, source_target_pairs={{0,4},{1,5},{2,6},{3,7},{4,0},{5,1},{6,2},{7,3},{8,12},{9,13},{10,... | collective-permute-start | bytes 393224 | tf_op jit(solution)/shard_map/ppermute | solution.py:131
  93.7 12.6 %collective-permute-start.33 = (bf16[64,1024]{1,0:T(8,128)(2,1)S(1)}, bf16[64,1024]{1,0:T(8,128)(2,1)S(1)}, u32[]{:S(2)}, u32[]{:S(2)}) collective-permute-start(bf16[64,1024]{1,0:T(8,128)(2,1)S(1)} %get-tuple-element.28), channel_id=1, source_target_pairs={{0,2},{1,3},{2,0},{3,1},{4,6},{5,7},{6,4},{7,5},{8,10},{9,11},{10,... | collective-permute-start | bytes 393224 | tf_op jit(solution)/shard_map/ppermute | solution.py:131
